TPU v7x, 256 devices: a whole 4x4x8 slice. The times are simulated.
256 devices in a mesh: grp: 8 (over x, z_lo), facet: 32 (over z_hi, y, core).
Axes of the slice: x: 4, y: 4, z: 8 (z_hi: 4, z_lo: 2; z = z_hi * 2 + z_lo), core: 2. Of those that a mesh axis runs over, the one named last changes fastest.
Arguments:
- image: float32 [16, 512, 1024], P(None, 'facet', 'grp'), may hold values from 0 to 2
- wavelet_dual: bfloat16 [8, 16, 512, 1024], P(None, None, 'facet', 'grp'), may hold values from -6 to 6
- thresholds: float32 [8, 512, 1024], P(None, 'facet', 'grp'), may hold values from 1 to 10
- filter_taps: float32 [8, 2, 7], replicated, may hold values from -2 to 2
- visibilities: float32 [32, 8, 8, 16, 256], P('facet', 'grp'), may hold values from -6 to 6
- data_dual: float32 [32, 8, 8, 16, 256], P('facet', 'grp'), may hold values from -6 to 6
- ball_radii: float32 [32, 8, 8], P('facet', 'grp'), may hold values from 19.2 to 256
- blocks: bfloat16 [32, 8, 16, 256, 256], P('facet', 'grp'), may hold values from -0.375 to 0.375
- row_index: int32 [32, 8, 16], P('facet', 'grp'), may hold values from 0 to 7
- col_index: int32 [32, 8, 16], P('facet', 'grp'), may hold values from 0 to 23
Outputs:
- image_out: float32 [16, 512, 1024], P(None, 'facet', 'grp')
- data_dual_out: float32 [32, 8, 8, 16, 256], P('facet', 'grp')
- wavelet_dual_out: bfloat16 [8, 16, 512, 1024], P(None, None, 'facet', 'grp')
Inputs may be any that keep to these rules, and one draw needn't show every extreme that they name: `row_index`: the visibility block of the same device that an operator block feeds. `col_index`: a tile of the band of three facets (the facet above, the device's own, the facet below) over the device's 128 columns, numbered row of tiles by row of tiles, 8 tiles a row.
All inputs are finite; a program needn't handle non-finite values.
Results may differ from a plain program's by a relative error of at most 0.0071.
Values may be sent and summed in bfloat16 or wider, within the bound.
No kernel may reach another device: no remote copies, remote signals or barrier semaphores. Data moves between devices by JAX's collectives and lax.ppermute only.
A program may use at most 64 MiB of HBM per device.

v0:
```python
import jax
import jax.numpy as jnp
from jax import lax
from jax.experimental import pallas as pl
from jax.experimental.pallas import tpu as pltpu
from jax.sharding import PartitionSpec as P

ITERS = 2
NB = 8
C = 16
R = 16
L = 128
W = 3
TAPS = 7
RB = 8
KDEV = 16
NT3 = 24
VB = 256
RE = R + 2 * W
BAND = 3 * R
F32 = jnp.float32
BF16 = jnp.bfloat16

VMEM = pl.BlockSpec(memory_space=pltpu.VMEM)
SMEM = pl.BlockSpec(memory_space=pltpu.SMEM)


def lanes():
    return lax.broadcasted_iota(jnp.int32, (C, L), 1)


def roll(x, shift):
    shift = shift % L
    return x if shift == 0 else pltpu.roll(x, shift, 1)


def is_odd(axis):
    return lax.rem(lax.axis_index(axis), 2) == 1


def pack(rows):
    total = rows[0]
    for i in range(1, len(rows)):
        total = total + roll(rows[i], 8 * i)
    return total


def unpack(packed, i, lane):
    return jnp.where(lane < 6, roll(packed, -8 * i), 0.0)


def swap_blocks(xs):
    xs = list(xs)
    lane = lanes()
    for bit in range(3):
        m = 1 << bit
        low = (lane // (16 * m)) % 2 == 0
        for i in range(8):
            if i & m == 0:
                a, b = xs[i], xs[i | m]
                xs[i] = jnp.where(low, a, roll(b, 16 * m))
                xs[i | m] = jnp.where(low, roll(a, -16 * m), b)
    return xs


def build_columns(taps, high, low):
    n = lax.broadcasted_iota(jnp.int32, (L, 2 * L), 1)
    j = lax.broadcasted_iota(jnp.int32, (L, 2 * L), 0)
    place = jnp.where(n < L, n, jnp.where(n < L + W, n - L - W, n - W))
    tap = jnp.where(n < L + 2 * W, place - j + W, -1)
    for b in range(NB):
        value = jnp.zeros((L, 2 * L), F32)
        for e in range(TAPS):
            value = jnp.where(tap == e, taps[b, 1, e], value)
        rounded = value.astype(BF16)
        high[b * L : (b + 1) * L, :] = rounded
        low[b * L : (b + 1) * L, :] = (value - rounded.astype(F32)).astype(BF16)


def back_project(vb, blocks, row_ids, col_ids, contrib, sums):
    for k in range(KDEV):
        contrib[k] = lax.dot_general(
            vb[row_ids[k]], blocks[k], (((1,), (1,)), ((), ())), preferred_element_type=F32
        )
    sums[...] = jnp.zeros(sums.shape, F32)
    for k in range(KDEV):
        q = col_ids[k]
        sums[q] = sums[q] + contrib[k]


def synth_rows(taps, b, rows, wide_h, wide_l):
    for i in range(RE):
        total = None
        for a in range(TAPS):
            r = i - a
            if 0 <= r < R:
                term = taps[b, 0, a] * rows[r]
                total = term if total is None else total + term
        high = total.astype(BF16)
        wide_h[i * C : (i + 1) * C, b * L : (b + 1) * L] = high
        wide_l[i * C : (i + 1) * C, b * L : (b + 1) * L] = (total - high.astype(F32)).astype(BF16)


def finish_backward(sums, wide_h, wide_l, col_h, col_l, smooth, main, ext, msg):
    wh = wide_h[...]
    smooth[...] = (
        jnp.dot(wh, col_h[...], preferred_element_type=F32)
        + jnp.dot(wide_l[...], col_h[...], preferred_element_type=F32)
        + jnp.dot(wh, col_l[...], preferred_element_type=F32)
    )
    for tr in range(3):
        for h in range(2):
            xs = swap_blocks([sums[tr * 8 + t, :, h * L : (h + 1) * L] for t in range(8)])
            for i in range(8):
                r = tr * R + h * 8 + i
                t = r - (R - W)
                value = xs[i]
                if 0 <= t < RE:
                    value = value + smooth[t * C : (t + 1) * C, :L]
                main[r] = value
    for t in range(RE):
        ext[t] = smooth[t * C : (t + 1) * C, L:]
    odd = is_odd("facet")
    base = jnp.where(odd, 0, 2 * R)
    base_ext = jnp.where(odd, 0, R + W)
    for r in range(R):
        msg[r] = main[base + r].astype(BF16)
    msg[R] = pack([ext[base_ext + i] for i in range(W)]).astype(BF16)


def first_kernel(
    taps, row_ids, col_ids, u, v, blocks,
    main, ext, msg, u_rows, col_h, col_l,
    vb, contrib, sums, turned, wide_h, wide_l, smooth,
):
    build_columns(taps, col_h, col_l)
    vb[...] = v[...].astype(BF16)
    back_project(vb, blocks, row_ids, col_ids, contrib, sums)
    for b in range(NB):
        turned[b] = u[b].astype(F32)
        rows = [turned[b, pl.ds(r, C, stride=R), :] for r in range(R)]
        for r in range(R):
            u_rows[b, r * C : (r + 1) * C, :] = rows[r].astype(BF16)
        synth_rows(taps, b, rows, wide_h, wide_l)
    finish_backward(sums, wide_h, wide_l, col_h, col_l, smooth, main, ext, msg)


def pair_kernel(with_image, *refs):
    if with_image:
        main, ext, got, image, total, total_ext, msg = refs
    else:
        main, ext, got, total, total_ext, msg = refs
    odd = is_odd("facet")
    lane = lanes()
    for r in range(R):
        row = main[R + r] + got[r].astype(F32)
        total[r] = row
        msg[R + r] = row.astype(BF16)
        total_ext[r] = ext[W + r]
    spot = jnp.where(odd, 0, R - W)
    packed = got[R].astype(F32)
    for i in range(W):
        total_ext[spot + i] = total_ext[spot + i] + unpack(packed, i, lane)
    far = jnp.where(odd, 2 * R, 0)
    far_ext = jnp.where(odd, R + W, 0)
    for r in range(R):
        msg[r] = main[far + r].astype(BF16)
    msg[2 * R] = pack([total_ext[r] for r in range(R)]).astype(BF16)
    msg[2 * R + 1] = pack([ext[far_ext + i] for i in range(W)]).astype(BF16)
    if with_image:
        for r in range(R):
            msg[2 * R + 2 + r] = image[pl.ds(r, C, stride=R), :].astype(BF16)


def rim_kernel(with_image, *refs):
    if with_image:
        total, total_ext, main, ext, got, image, part, part_ext, msg_a, msg_b, x = refs
    else:
        total, total_ext, main, ext, got, part, part_ext, msg_a, msg_b = refs
    odd = is_odd("facet")
    lane = lanes()
    far = jnp.where(odd, 2 * R, 0)
    far_ext = jnp.where(odd, R + W, 0)
    packed = got[2 * R].astype(F32)
    for r in range(R):
        part[r] = total[r] + got[r].astype(F32)
        part_ext[r] = total_ext[r]
        part[R + r] = got[R + r].astype(F32) + main[far + r]
        part_ext[R + r] = unpack(packed, r, lane)
    near = jnp.where(odd, R - W, 0)
    away = jnp.where(odd, 0, R - W)
    packed = got[2 * R + 1].astype(F32)
    for i in range(W):
        part_ext[near + i] = part_ext[near + i] + unpack(packed, i, lane)
        part_ext[R + away + i] = part_ext[R + away + i] + ext[far_ext + i]
    if with_image:
        for r in range(R):
            x[r] = image[pl.ds(r, C, stride=R), :]
            x[R + r] = got[2 * R + 2 + r].astype(F32)
    godd = is_odd("grp")
    slot = lane // 8
    sub = lane % 8
    first = sub < W
    second = (sub >= W) & (sub < 2 * W)
    for p in range(2):
        left = jnp.zeros((C, L), F32)
        right = jnp.zeros((C, L), F32)
        for r in range(R):
            row, row_ext = part[p * R + r], part_ext[p * R + r]
            one = (slot == r) & first
            two = (slot == r) & second
            left = jnp.where(one, roll(row_ext, 8 * r), left)
            left = jnp.where(two, roll(row, 8 * r + W), left)
            right = jnp.where(one, roll(row_ext, 8 * r - W), right)
            right = jnp.where(two, roll(row, 8 * r + 2 * W), right)
        msg_a[p] = jnp.where(godd, left, right).astype(BF16)
        msg_b[p] = jnp.where(godd, right, left).astype(BF16)
        if with_image:
            left = jnp.zeros((C, L), F32)
            right = jnp.zeros((C, L), F32)
            for r in range(R):
                row = x[p * R + r]
                one = (slot == r) & first
                left = jnp.where(one, roll(row, 8 * r), left)
                right = jnp.where(one, roll(row, 8 * r + W), right)
            msg_a[2 + p] = jnp.where(godd, left, right).astype(BF16)
            msg_b[2 + p] = jnp.where(godd, right, left).astype(BF16)


def primal_kernel(first, last, *refs):
    refs = list(refs)
    part, part_ext, got_a, got_b, x = refs[:5]
    refs = refs[5:]
    if not first:
        x_ext = refs.pop(0)
    if last:
        image_out, e, e_ext, msg, turned = refs
    else:
        new_x, new_x_ext, e, e_ext, msg = refs
    lane = lanes()
    facet, grp = lax.axis_index("facet"), lax.axis_index("grp")
    odd = is_odd("facet")
    godd = is_odd("grp")
    on_left = (grp > 0) & (lane < W)
    on_right = (grp < lax.axis_size("grp") - 1) & (lane >= W) & (lane < 2 * W)
    inside = on_left | on_right
    there = jnp.where(odd, facet < lax.axis_size("facet") - 1, facet > 0)
    got_a_wide = got_a[...].astype(F32)
    got_b_wide = got_b[...].astype(F32)
    from_left = jnp.where(godd, got_a_wide, got_b_wide)
    from_right = jnp.where(godd, got_b_wide, got_a_wide)
    rims = []
    for p in range(2):
        for r in range(R):
            i = p * R + r
            grad = part[i] + jnp.where(lane < W, roll(from_left[p], -8 * r), 0.0)
            grad = grad + jnp.where(lane >= L - W, roll(from_right[p], -8 * r - W), 0.0)
            rim = jnp.where(
                lane < W, roll(from_left[p], -8 * r - W), roll(from_right[p], -8 * r)
            )
            grad_ext = part_ext[i] + rim
            old = x[i]
            if first:
                old_ext = jnp.where(
                    lane < W, roll(from_left[2 + p], -8 * r), roll(from_right[2 + p], -8 * r + W)
                )
            else:
                old_ext = x_ext[i]
            new = jnp.maximum(old - 0.5 * grad, 0.0)
            new_ext = jnp.maximum(old_ext - 0.5 * grad_ext, 0.0)
            ahead = 2.0 * new - old
            ahead_ext = jnp.where(inside, 2.0 * new_ext - old_ext, 0.0)
            if p == 1:
                ahead = jnp.where(there, ahead, 0.0)
                ahead_ext = jnp.where(there, ahead_ext, 0.0)
            e[i] = ahead.astype(BF16)
            e_ext[i] = ahead_ext.astype(BF16)
            if p == 0:
                msg[r] = ahead.astype(BF16)
                rims.append(ahead_ext)
                if last:
                    turned[r * C : (r + 1) * C, :] = new
            if not last:
                new_x[i] = new
                new_x_ext[i] = new_ext
    msg[R] = pack(rims).astype(BF16)
    if last:
        for c in range(C):
            image_out[c * R : (c + 1) * R, :] = turned[pl.ds(c, R, stride=C), :]


def dual_kernel(last, *refs):
    taps, row_ids, col_ids, radii, e, e_ext, got, v, vis, blocks, u_rows, thr, col_h, col_l = refs[:14]
    refs = refs[14:]
    if last:
        v_out, u_out, band, band_ext, near, wide, flat, contrib, sums, turned = refs
    else:
        main, ext, msg, v_out, u_out = refs[:5]
        band, band_ext, near, wide, flat, contrib, sums, turned, vb, tiles, wide_h, wide_l, smooth = refs[5:]
    odd = is_odd("facet")
    lane = lanes()
    base_a = jnp.where(odd, 0, 2 * R)
    base_b = jnp.where(odd, 2 * R, 0)
    packed = got[R].astype(F32)
    for r in range(R):
        band[R + r] = e[r].astype(F32)
        band[base_b + r] = e[R + r].astype(F32)
        band[base_a + r] = got[r].astype(F32)
        band_ext[R + r] = e_ext[r].astype(F32)
        band_ext[base_b + r] = e_ext[R + r].astype(F32)
        band_ext[base_a + r] = unpack(packed, r, lane)
    for t in range(RE):
        near[t * C : (t + 1) * C, :L] = band[R - W + t].astype(BF16)
        near[t * C : (t + 1) * C, L:] = band_ext[R - W + t].astype(BF16)
    for tr in range(3):
        for h in range(2):
            xs = swap_blocks([band[tr * R + h * 8 + i] for i in range(8)])
            for t in range(8):
                flat[tr * 8 + t, :, h * L : (h + 1) * L] = xs[t].astype(BF16)
    for k in range(KDEV):
        contrib[k] = jnp.dot(flat[col_ids[k]], blocks[k], preferred_element_type=F32)
    sums[...] = jnp.zeros(sums.shape, F32)
    for k in range(KDEV):
        r = row_ids[k]
        sums[r] = sums[r] + contrib[k]
    for r in range(RB):
        seen = vis[r]
        moved = v[r] + 0.5 * sums[r]
        offset = 2.0 * moved - seen
        length = jnp.sqrt(jnp.sum(jnp.sum(offset * offset, axis=1, keepdims=True), axis=0, keepdims=True))
        scale = radii[r] / jnp.maximum(length, radii[r])
        new = moved - 0.5 * (seen + offset * scale)
        v_out[r] = new
        if not last:
            vb[r] = new.astype(BF16)
    both = (((1,), (1,)), ((), ()))
    wide[...] = lax.dot_general(
        near[...], col_h[...], both, preferred_element_type=F32
    ) + lax.dot_general(near[...], col_l[...], both, preferred_element_type=F32)
    if not last:
        back_project(vb, blocks, row_ids, col_ids, tiles[0], tiles[1])
    for b in range(NB):
        rows = []
        for r in range(R):
            total = None
            for a in range(TAPS):
                term = taps[b, 0, a] * wide[(r + a) * C : (r + a + 1) * C, b * L : (b + 1) * L]
                total = term if total is None else total + term
            full = u_rows[b, r * C : (r + 1) * C, :].astype(F32) + 0.5 * total
            size = jnp.sqrt(jnp.sum(full * full, axis=0, keepdims=True))
            limit = thr[b, r : r + 1, :]
            new = full * (limit / jnp.maximum(size, limit))
            if last:
                turned[b, r * C : (r + 1) * C, :] = new
            else:
                new = new.astype(BF16)
                u_out[b, r * C : (r + 1) * C, :] = new
                rows.append(new.astype(F32))
        if last:
            for c in range(C):
                u_out[b, c * R : (c + 1) * R, :] = turned[b, pl.ds(c, R, stride=C), :].astype(BF16)
        else:
            synth_rows(taps, b, rows, wide_h, wide_l)
    if not last:
        finish_backward(tiles[1], wide_h, wide_l, col_h, col_l, smooth, main, ext, msg)


def shape(dims, dtype=F32):
    return jax.ShapeDtypeStruct(dims, dtype)


def scratch(*dims, dtype=F32):
    return pltpu.VMEM(dims, dtype)


BACK = [shape((BAND, C, L)), shape((RE, C, L)), shape((R + 1, C, L), BF16)]


def call(kernel, scalars, arrays, outs, temps=(), name=None):
    return pl.pallas_call(
        kernel,
        out_shape=tuple(outs),
        in_specs=[SMEM] * len(scalars) + [VMEM] * len(arrays),
        out_specs=tuple(VMEM for _ in outs),
        scratch_shapes=list(temps),
        name=name,
    )(*scalars, *arrays)


def pairs_of(axis):
    count = lax.axis_size(axis)
    inner = [(i, i ^ 1) for i in range(count)]
    outer = [(i, ((i + 1) ^ 1) - 1) for i in range(1, count - 1)]
    return inner, outer


def per_device(
    image, wavelet_dual, thresholds, filter_taps, visibilities,
    data_dual, ball_radii, blocks, row_index, col_index,
):
    image_rows = image.reshape(C * R, L)
    u = wavelet_dual.reshape(NB, C * R, L)
    operators, seen, v = blocks[0, 0], visibilities[0, 0], data_dual[0, 0]
    radii, row_ids, col_ids = ball_radii[0, 0], row_index[0, 0], col_index[0, 0]
    facet_in, facet_out = pairs_of("facet")
    grp_in, grp_out = pairs_of("grp")
    synth_temps = [
        scratch(NB, C * R, L),
        scratch(RE * C, NB * L, dtype=BF16),
        scratch(RE * C, NB * L, dtype=BF16),
        scratch(RE * C, 2 * L),
    ]
    main, ext, msg, u, col_h, col_l = call(
        first_kernel,
        (filter_taps, row_ids, col_ids),
        (u, v, operators),
        BACK
        + [shape((NB, R * C, L), BF16), shape((NB * L, 2 * L), BF16), shape((NB * L, 2 * L), BF16)],
        [scratch(RB, C, VB, dtype=BF16), scratch(KDEV, C, VB), scratch(NT3, C, VB)] + synth_temps,
        name="first",
    )
    x = x_ext = None
    for iteration in range(ITERS):
        first, last = iteration == 0, iteration == ITERS - 1
        got = lax.ppermute(msg, "facet", facet_in)
        total, total_ext, msg = call(
            lambda *refs: pair_kernel(first, *refs),
            (),
            (main, ext, got) + ((image_rows,) if first else ()),
            [
                shape((R, C, L)),
                shape((R, C, L)),
                shape(((3 if first else 2) * R + 2, C, L), BF16),
            ],
            name="pair",
        )
        got = lax.ppermute(msg, "facet", facet_out)
        rim = shape((4 if first else 2, C, L), BF16)
        part, part_ext, msg_a, msg_b, *rest = call(
            lambda *refs: rim_kernel(first, *refs),
            (),
            (total, total_ext, main, ext, got) + ((image_rows,) if first else ()),
            [shape((2 * R, C, L)), shape((2 * R, C, L)), rim, rim]
            + ([shape((2 * R, C, L))] if first else []),
            name="rim",
        )
        if first:
            x = rest[0]
        got_a = lax.ppermute(msg_a, "grp", grp_in)
        got_b = lax.ppermute(msg_b, "grp", grp_out)
        wide = shape((2 * R, C, L))
        outs = [shape((2 * R, C, L), BF16), shape((2 * R, C, L), BF16), shape((R + 1, C, L), BF16)]
        results = call(
            lambda *refs: primal_kernel(first, last, *refs),
            (),
            (part, part_ext, got_a, got_b, x) + (() if first else (x_ext,)),
            ([shape((C * R, L))] if last else [wide, wide]) + outs,
            [scratch(R * C, L)] if last else [],
            name="primal",
        )
        e, e_ext, msg = results[-3:]
        if last:
            image_out = results[0]
        else:
            x, x_ext = results[:2]
        got = lax.ppermute(msg, "facet", facet_in)
        temps = [
            scratch(BAND, C, L),
            scratch(BAND, C, L),
            scratch(RE * C, 2 * L, dtype=BF16),
            scratch(RE * C, NB * L),
            scratch(NT3, C, VB, dtype=BF16),
            scratch(KDEV, C, VB),
            scratch(RB, C, VB),
        ]
        if last:
            temps += synth_temps[:1]
        else:
            temps += [
                synth_temps[0],
                scratch(RB, C, VB, dtype=BF16),
                (scratch(KDEV, C, VB), scratch(NT3, C, VB)),
            ] + synth_temps[1:]
        *back, v, u = call(
            lambda *refs: dual_kernel(last, *refs),
            (filter_taps, row_ids, col_ids, radii),
            (e, e_ext, got, v, seen, operators, u, thresholds, col_h, col_l),
            ([] if last else BACK) + [shape((RB, C, VB)), shape((NB, R * C, L), BF16)],
            temps,
            name="dual",
        )
        if not last:
            main, ext, msg = back
    return (image_out.reshape(C, R, L), v[None, None], u.reshape(NB, C, R, L))


def solution(mesh):
    in_specs = (
        P(None, "facet", "grp"),
        P(None, None, "facet", "grp"),
        P(None, "facet", "grp"),
        P(),
        P("facet", "grp", None, None, None),
        P("facet", "grp", None, None, None),
        P("facet", "grp", None),
        P("facet", "grp", None, None, None),
        P("facet", "grp", None),
        P("facet", "grp", None),
    )
    out_specs = (
        P(None, "facet", "grp"),
        P("facet", "grp", None, None, None),
        P(None, None, "facet", "grp"),
    )
    return jax.shard_map(
        per_device, mesh=mesh, in_specs=in_specs, out_specs=out_specs, check_vma=False
    )
```

profile of v0, /device:TPU:131, one launch (start us, length us, event | category | flops | bytes accessed | tf_op | source)
XLA Modules:
  0.0 84.8 jit_solution(15098097071057334844)
XLA Ops:
  0.6 1.4 %copy.14.taps.refs_0_ = f32[8,2,7]{2,1,0:T(2,128)} copy(f32[8,2,7]{0,1,2:T(2,128)} %param.13) | data formatting | bytes 896 | tf_op args[3]
  2.0 5.4 %first.1 = (f32[48,16,128]{2,1,0:T(8,128)}, f32[22,16,128]{2,1,0:T(8,128)}, bf16[17,16,128]{2,1,0:T(8,128)(2,1)}, bf16[8,256,128]{2,1,0:T(8,128)(2,1)}, bf16[102...) custom-call(f32[8,2,7]{2,1,0:T(2,128)} %copy.14.taps.refs_0_, s32[16]{0:T(128)} %bitcast.21, s32[16]{0:T(128)} %bitcast.24, ...), custom_call_target="tpu_custom_call" | custom-call | tf_op jit(solution)/shard_map/first/pallas_call | solution.py:380
  7.4 0.7 collective-permute-start
  8.1 1.1 %collective-permute-done.refs_2_ = bf16[17,16,128]{2,1,0:T(8,128)(2,1)S(1)} collective-permute-done((bf16[17,16,128]{2,1,0:T(8,128)(2,1)}, bf16[17,16,128]{2,1,0:T(8,128)(2,1)S(1)}, u32[]{:S(2)}, u32[]{:S(2)}) %collective-permute-start) | collective-permute-done | bytes 69664 | tf_op jit(solution)/shard_map/ppermute | solution.py:425
  9.2 0.0 copy-start.2
  9.2 0.6 copy-done.2
  9.8 2.0 %pair.2 = (f32[16,16,128]{2,1,0:T(8,128)}, f32[16,16,128]{2,1,0:T(8,128)}, bf16[50,16,128]{2,1,0:T(8,128)(2,1)}) custom-call(f32[48,16,128]{2,1,0:T(8,128)} %get-tuple-element.40.refs_0_.refs_2_, f32[22,16,128]{2,1,0:T(8,128)} %get-tuple-element.41.refs_1_.refs_3_, bf16[17,16,128]{2,1,0:T(8,128)(2,1)} %copy-done.2, f32[256,128]{1,0:T(8,128)} %bitcast.19), custom_call_target="tpu_custom_call" | custom-call | tf_op jit(solution)/shard_map/pair/pallas_call | solution.py:380
  11.8 3.4 %collective-permute-start.1 = (bf16[50,16,128]{2,1,0:T(8,128)(2,1)}, bf16[50,16,128]{2,1,0:T(8,128)(2,1)S(1)}, u32[]{:S(2)}, u32[]{:S(2)}) collective-permute-start(bf16[50,16,128]{2,1,0:T(8,128)(2,1)} %get-tuple-element.45), channel_id=1, source_target_pairs={{1,2},{2,1},{3,4},{4,3},{5,6},{6,5},{7,8},{8,7},{9,10},{10,9},{11,... | collective-permute-start | bytes 614408 | tf_op jit(solution)/shard_map/ppermute | solution.py:437
  15.3 3.8 %collective-permute-done.1.refs_4_ = bf16[50,16,128]{2,1,0:T(8,128)(2,1)S(1)} collective-permute-done((bf16[50,16,128]{2,1,0:T(8,128)(2,1)}, bf16[50,16,128]{2,1,0:T(8,128)(2,1)S(1)}, u32[]{:S(2)}, u32[]{:S(2)}) %collective-permute-start.1) | collective-permute-done | bytes 204832 | tf_op jit(solution)/shard_map/ppermute | solution.py:437
  19.1 0.0 copy-start
  19.1 0.7 copy-done
  19.8 2.5 %rim.2 = (f32[32,16,128]{2,1,0:T(8,128)}, f32[32,16,128]{2,1,0:T(8,128)}, bf16[4,16,128]{2,1,0:T(8,128)(2,1)}, bf16[4,16,128]{2,1,0:T(8,128)(2,1)}, f32[32,16,128]{2,1,0:T(8,128)}) custom-call(f32[16,16,128]{2,1,0:T(8,128)} %get-tuple-element.43.refs_0_, f32[16,16,128]{2,1,0:T(8,128)} %get-tuple-element.44.refs_1_, ...), custom_call_target="tpu_custom_call" | custom-call | tf_op jit(solution)/shard_map/rim/pallas_call | solution.py:380
  22.3 0.7 collective-permute-start.2
  23.1 2.6 %collective-permute-start.3 = (bf16[4,16,128]{2,1,0:T(8,128)(2,1)}, bf16[4,16,128]{2,1,0:T(8,128)(2,1)S(1)}, u32[]{:S(2)}, u32[]{:S(2)}) collective-permute-start(bf16[4,16,128]{2,1,0:T(8,128)(2,1)} %get-tuple-element.49), channel_id=1, source_target_pairs={{32,64},{64,32},{96,128},{128,96},{160,192},{192,160},{33,65},{65,... | collective-permute-start | bytes 49160 | tf_op jit(solution)/shard_map/ppermute | solution.py:450
  25.7 0.0 collective-permute-done.2.refs_2_
  25.7 0.0 copy-start.6
  25.7 3.0 %collective-permute-done.3.refs_3_ = bf16[4,16,128]{2,1,0:T(8,128)(2,1)S(1)} collective-permute-done((bf16[4,16,128]{2,1,0:T(8,128)(2,1)}, bf16[4,16,128]{2,1,0:T(8,128)(2,1)S(1)}, u32[]{:S(2)}, u32[]{:S(2)}) %collective-permute-start.3) | collective-permute-done | bytes 16416 | tf_op jit(solution)/shard_map/ppermute | solution.py:450
  28.6 0.0 copy-start.7
  28.6 0.0 copy-done.6
  28.6 0.6 copy-done.7
  29.2 2.3 %primal.2 = (f32[32,16,128]{2,1,0:T(8,128)}, f32[32,16,128]{2,1,0:T(8,128)}, bf16[32,16,128]{2,1,0:T(8,128)(2,1)}, bf16[32,16,128]{2,1,0:T(8,128)(2,1)}, bf16[17,16,128]{2,1,0:T(8,128)(2,1)}) custom-call(f32[32,16,128]{2,1,0:T(8,128)} %get-tuple-element.46.refs_0_, f32[32,16,128]{2,1,0:T(8,128)} %get-tuple-element.47.refs_1_, bf16[4,16,128]{2,1,0:T(8,128)(2,1)} %copy-done.6, ...), custom_call_target="tpu_custom_call" | custom-call | tf_op jit(solution)/shard_map/primal/pallas_call | solution.py:380
  31.6 7.1 %collective-permute-start.4 = (bf16[17,16,128]{2,1,0:T(8,128)(2,1)}, bf16[17,16,128]{2,1,0:T(8,128)(2,1)S(1)}, u32[]{:S(2)}, u32[]{:S(2)}) collective-permute-start(bf16[17,16,128]{2,1,0:T(8,128)(2,1)} %get-tuple-element.53), channel_id=1, source_target_pairs={{0,1},{1,0},{2,3},{3,2},{4,5},{5,4},{6,7},{7,6},{8,9},{9,8},{10,11... | collective-permute-start | bytes 208904 | tf_op jit(solution)/shard_map/ppermute | solution.py:466
  38.6 1.1 %collective-permute-done.4.refs_6_ = bf16[17,16,128]{2,1,0:T(8,128)(2,1)S(1)} collective-permute-done((bf16[17,16,128]{2,1,0:T(8,128)(2,1)}, bf16[17,16,128]{2,1,0:T(8,128)(2,1)S(1)}, u32[]{:S(2)}, u32[]{:S(2)}) %collective-permute-start.4) | collective-permute-done | bytes 69664 | tf_op jit(solution)/shard_map/ppermute | solution.py:466
  39.8 0.0 copy-start.5
  39.8 0.6 copy-done.5
  40.4 6.8 %dual.2 = (f32[48,16,128]{2,1,0:T(8,128)}, f32[22,16,128]{2,1,0:T(8,128)}, bf16[17,16,128]{2,1,0:T(8,128)(2,1)}, f32[8,16,256]{2,1,0:T(8,128)}, bf16[8,256,128]{2,1,0:T(8,128)(2,1)}) custom-call(f32[8,2,7]{2,1,0:T(2,128)} %copy.14.taps.refs_0_, s32[16]{0:T(128)} %bitcast.22, s32[16]{0:T(128)} %bitcast.25, f32[8]{0:T(128)} %bitcast.27, ...), custom_call_target="tpu_custom_call" | custom-call | tf_op jit(solution)/shard_map/dual/pallas_call | solution.py:380
  47.2 0.4 collective-permute-start.5
  47.6 1.1 %collective-permute-done.5.refs_2_ = bf16[17,16,128]{2,1,0:T(8,128)(2,1)S(1)} collective-permute-done((bf16[17,16,128]{2,1,0:T(8,128)(2,1)}, bf16[17,16,128]{2,1,0:T(8,128)(2,1)S(1)}, u32[]{:S(2)}, u32[]{:S(2)}) %collective-permute-start.5) | collective-permute-done | bytes 69664 | tf_op jit(solution)/shard_map/ppermute | solution.py:425
  48.7 0.0 copy-start.3
  48.7 0.6 copy-done.3
  49.3 1.9 %pair.3 = (f32[16,16,128]{2,1,0:T(8,128)}, f32[16,16,128]{2,1,0:T(8,128)}, bf16[34,16,128]{2,1,0:T(8,128)(2,1)}) custom-call(f32[48,16,128]{2,1,0:T(8,128)} %get-tuple-element.57.refs_0_.refs_2_, f32[22,16,128]{2,1,0:T(8,128)} %get-tuple-element.58.refs_1_.refs_3_, bf16[17,16,128]{2,1,0:T(8,128)(2,1)} %copy-done.3), custom_call_target="tpu_custom_call" | custom-call | tf_op jit(solution)/shard_map/pair/pallas_call | solution.py:380
  51.3 1.9 %collective-permute-start.6 = (bf16[34,16,128]{2,1,0:T(8,128)(2,1)}, bf16[34,16,128]{2,1,0:T(8,128)(2,1)S(1)}, u32[]{:S(2)}, u32[]{:S(2)}) collective-permute-start(bf16[34,16,128]{2,1,0:T(8,128)(2,1)} %get-tuple-element.62), channel_id=1, source_target_pairs={{1,2},{2,1},{3,4},{4,3},{5,6},{6,5},{7,8},{8,7},{9,10},{10,9},{11,... | collective-permute-start | bytes 417800 | tf_op jit(solution)/shard_map/ppermute | solution.py:437
  53.2 4.7 %collective-permute-done.6.refs_4_ = bf16[34,16,128]{2,1,0:T(8,128)(2,1)S(1)} collective-permute-done((bf16[34,16,128]{2,1,0:T(8,128)(2,1)}, bf16[34,16,128]{2,1,0:T(8,128)(2,1)S(1)}, u32[]{:S(2)}, u32[]{:S(2)}) %collective-permute-start.6) | collective-permute-done | bytes 139296 | tf_op jit(solution)/shard_map/ppermute | solution.py:437
  57.9 0.0 copy-start.1
  57.9 0.7 copy-done.1
  58.5 2.2 %rim.3 = (f32[32,16,128]{2,1,0:T(8,128)}, f32[32,16,128]{2,1,0:T(8,128)}, bf16[2,16,128]{2,1,0:T(8,128)(2,1)}, bf16[2,16,128]{2,1,0:T(8,128)(2,1)}) custom-call(f32[16,16,128]{2,1,0:T(8,128)} %get-tuple-element.60.refs_0_, f32[16,16,128]{2,1,0:T(8,128)} %get-tuple-element.61.refs_1_, f32[48,16,128]{2,1,0:T(8,128)} %get-tuple-element.57.refs_0_.refs_2_, ...), custom_call_target="tpu_custom_call" | custom-call | tf_op jit(solution)/shard_map/rim/pallas_call | solution.py:380
  60.7 1.7 %collective-permute-start.7 = (bf16[2,16,128]{2,1,0:T(8,128)(2,1)}, bf16[2,16,128]{2,1,0:T(8,128)(2,1)S(1)}, u32[]{:S(2)}, u32[]{:S(2)}) collective-permute-start(bf16[2,16,128]{2,1,0:T(8,128)(2,1)} %get-tuple-element.65), channel_id=1, source_target_pairs={{0,32},{32,0},{64,96},{96,64},{128,160},{160,128},{192,224},{224,1... | collective-permute-start | bytes 24584 | tf_op jit(solution)/shard_map/ppermute | solution.py:449
  62.5 1.9 %collective-permute-start.8 = (bf16[2,16,128]{2,1,0:T(8,128)(2,1)}, bf16[2,16,128]{2,1,0:T(8,128)(2,1)S(1)}, u32[]{:S(2)}, u32[]{:S(2)}) collective-permute-start(bf16[2,16,128]{2,1,0:T(8,128)(2,1)} %get-tuple-element.66), channel_id=1, source_target_pairs={{32,64},{64,32},{96,128},{128,96},{160,192},{192,160},{33,65},{65,... | collective-permute-start | bytes 24584 | tf_op jit(solution)/shard_map/ppermute | solution.py:450
  64.4 0.0 collective-permute-done.7.refs_2_
  64.4 0.0 copy-start.8
  64.4 3.6 %collective-permute-done.8.refs_3_ = bf16[2,16,128]{2,1,0:T(8,128)(2,1)S(1)} collective-permute-done((bf16[2,16,128]{2,1,0:T(8,128)(2,1)}, bf16[2,16,128]{2,1,0:T(8,128)(2,1)S(1)}, u32[]{:S(2)}, u32[]{:S(2)}) %collective-permute-start.8) | collective-permute-done | bytes 8224 | tf_op jit(solution)/shard_map/ppermute | solution.py:450
  68.0 0.0 copy-done.8
  68.0 0.6 copy-done.9
  68.6 2.2 %primal.3 = (f32[256,128]{1,0:T(8,128)}, bf16[32,16,128]{2,1,0:T(8,128)(2,1)}, bf16[32,16,128]{2,1,0:T(8,128)(2,1)}, bf16[17,16,128]{2,1,0:T(8,128)(2,1)}) custom-call(f32[32,16,128]{2,1,0:T(8,128)} %get-tuple-element.63.refs_0_, f32[32,16,128]{2,1,0:T(8,128)} %get-tuple-element.64.refs_1_, bf16[2,16,128]{2,1,0:T(8,128)(2,1)} %copy-done.8, ...), custom_call_target="tpu_custom_call" | custom-call | tf_op jit(solution)/shard_map/primal/pallas_call | solution.py:380
  70.8 6.9 %collective-permute-start.9 = (bf16[17,16,128]{2,1,0:T(8,128)(2,1)}, bf16[17,16,128]{2,1,0:T(8,128)(2,1)S(1)}, u32[]{:S(2)}, u32[]{:S(2)}) collective-permute-start(bf16[17,16,128]{2,1,0:T(8,128)(2,1)} %get-tuple-element.72), channel_id=1, source_target_pairs={{0,1},{1,0},{2,3},{3,2},{4,5},{5,4},{6,7},{7,6},{8,9},{9,8},{10,11... | collective-permute-start | bytes 208904 | tf_op jit(solution)/shard_map/ppermute | solution.py:466
  77.7 1.1 %collective-permute-done.9.refs_6_ = bf16[17,16,128]{2,1,0:T(8,128)(2,1)S(1)} collective-permute-done((bf16[17,16,128]{2,1,0:T(8,128)(2,1)}, bf16[17,16,128]{2,1,0:T(8,128)(2,1)S(1)}, u32[]{:S(2)}, u32[]{:S(2)}) %collective-permute-start.9) | collective-permute-done | bytes 69664 | tf_op jit(solution)/shard_map/ppermute | solution.py:466
  78.9 0.6 copy-done.4
  79.5 5.3 %dual.3 = (f32[8,16,256]{2,1,0:T(8,128)}, bf16[8,256,128]{2,1,0:T(8,128)(2,1)}) custom-call(f32[8,2,7]{2,1,0:T(2,128)} %copy.14.taps.refs_0_, s32[16]{0:T(128)} %bitcast.23, s32[16]{0:T(128)} %bitcast.26, f32[8]{0:T(128)} %bitcast.28, bf16[32,16,128]{2,1,0:T(8,128)(2,1)} %get-tuple-element.70.refs_4_, bf16[32,16,128]{2,1,0:T(8,128)(2,1)} %get-tuple-element.71.refs_5_, ...), custom_call_target="tpu_custom_call" | custom-call | tf_op jit(solution)/shard_map/dual/pallas_call | solution.py:380
  (2 shorter events, 0.0 us)
Async XLA Ops:
  7.4 1.8 %collective-permute-start = (bf16[17,16,128]{2,1,0:T(8,128)(2,1)}, bf16[17,16,128]{2,1,0:T(8,128)(2,1)S(1)}, u32[]{:S(2)}, u32[]{:S(2)}) collective-permute-start(bf16[17,16,128]{2,1,0:T(8,128)(2,1)} %get-tuple-element.42), channel_id=1, source_target_pairs={{0,1},{1,0},{2,3},{3,2},{4,5},{5,4},{6,7},{7,6},{8,9},{9,8},{10,11... | collective-permute-start | bytes 208904 | tf_op jit(solution)/shard_map/ppermute | solution.py:425
  9.2 0.6 copy-start.2
  11.8 7.3 %collective-permute-start.1 = (bf16[50,16,128]{2,1,0:T(8,128)(2,1)}, bf16[50,16,128]{2,1,0:T(8,128)(2,1)S(1)}, u32[]{:S(2)}, u32[]{:S(2)}) collective-permute-start(bf16[50,16,128]{2,1,0:T(8,128)(2,1)} %get-tuple-element.45), channel_id=1, source_target_pairs={{1,2},{2,1},{3,4},{4,3},{5,6},{6,5},{7,8},{8,7},{9,10},{10,9},{11,... | collective-permute-start | bytes 614408 | tf_op jit(solution)/shard_map/ppermute | solution.py:437
  19.1 0.7 copy-start
  22.3 3.3 %collective-permute-start.2 = (bf16[4,16,128]{2,1,0:T(8,128)(2,1)}, bf16[4,16,128]{2,1,0:T(8,128)(2,1)S(1)}, u32[]{:S(2)}, u32[]{:S(2)}) collective-permute-start(bf16[4,16,128]{2,1,0:T(8,128)(2,1)} %get-tuple-element.48), channel_id=1, source_target_pairs={{0,32},{32,0},{64,96},{96,64},{128,160},{160,128},{192,224},{224,1... | collective-permute-start | bytes 49160 | tf_op jit(solution)/shard_map/ppermute | solution.py:449
  23.1 5.6 %collective-permute-start.3 = (bf16[4,16,128]{2,1,0:T(8,128)(2,1)}, bf16[4,16,128]{2,1,0:T(8,128)(2,1)S(1)}, u32[]{:S(2)}, u32[]{:S(2)}) collective-permute-start(bf16[4,16,128]{2,1,0:T(8,128)(2,1)} %get-tuple-element.49), channel_id=1, source_target_pairs={{32,64},{64,32},{96,128},{128,96},{160,192},{192,160},{33,65},{65,... | collective-permute-start | bytes 49160 | tf_op jit(solution)/shard_map/ppermute | solution.py:450
  25.7 3.0 %copy-start.6 = (bf16[4,16,128]{2,1,0:T(8,128)(2,1)}, bf16[4,16,128]{2,1,0:T(8,128)(2,1)S(1)}, u32[]{:S(2)}) copy-start(bf16[4,16,128]{2,1,0:T(8,128)(2,1)S(1)} %collective-permute-done.2.refs_2_) | copy-start | bytes 49156
  28.6 0.6 copy-start.7
  31.6 8.2 %collective-permute-start.4 = (bf16[17,16,128]{2,1,0:T(8,128)(2,1)}, bf16[17,16,128]{2,1,0:T(8,128)(2,1)S(1)}, u32[]{:S(2)}, u32[]{:S(2)}) collective-permute-start(bf16[17,16,128]{2,1,0:T(8,128)(2,1)} %get-tuple-element.53), channel_id=1, source_target_pairs={{0,1},{1,0},{2,3},{3,2},{4,5},{5,4},{6,7},{7,6},{8,9},{9,8},{10,11... | collective-permute-start | bytes 208904 | tf_op jit(solution)/shard_map/ppermute | solution.py:466
  39.8 0.6 copy-start.5
  47.2 1.6 %collective-permute-start.5 = (bf16[17,16,128]{2,1,0:T(8,128)(2,1)}, bf16[17,16,128]{2,1,0:T(8,128)(2,1)S(1)}, u32[]{:S(2)}, u32[]{:S(2)}) collective-permute-start(bf16[17,16,128]{2,1,0:T(8,128)(2,1)} %get-tuple-element.59), channel_id=1, source_target_pairs={{0,1},{1,0},{2,3},{3,2},{4,5},{5,4},{6,7},{7,6},{8,9},{9,8},{10,11... | collective-permute-start | bytes 208904 | tf_op jit(solution)/shard_map/ppermute | solution.py:425
  48.7 0.6 copy-start.3
  51.3 6.6 %collective-permute-start.6 = (bf16[34,16,128]{2,1,0:T(8,128)(2,1)}, bf16[34,16,128]{2,1,0:T(8,128)(2,1)S(1)}, u32[]{:S(2)}, u32[]{:S(2)}) collective-permute-start(bf16[34,16,128]{2,1,0:T(8,128)(2,1)} %get-tuple-element.62), channel_id=1, source_target_pairs={{1,2},{2,1},{3,4},{4,3},{5,6},{6,5},{7,8},{8,7},{9,10},{10,9},{11,... | collective-permute-start | bytes 417800 | tf_op jit(solution)/shard_map/ppermute | solution.py:437
  57.9 0.7 copy-start.1
  60.7 3.7 %collective-permute-start.7 = (bf16[2,16,128]{2,1,0:T(8,128)(2,1)}, bf16[2,16,128]{2,1,0:T(8,128)(2,1)S(1)}, u32[]{:S(2)}, u32[]{:S(2)}) collective-permute-start(bf16[2,16,128]{2,1,0:T(8,128)(2,1)} %get-tuple-element.65), channel_id=1, source_target_pairs={{0,32},{32,0},{64,96},{96,64},{128,160},{160,128},{192,224},{224,1... | collective-permute-start | bytes 24584 | tf_op jit(solution)/shard_map/ppermute | solution.py:449
  62.5 5.5 %collective-permute-start.8 = (bf16[2,16,128]{2,1,0:T(8,128)(2,1)}, bf16[2,16,128]{2,1,0:T(8,128)(2,1)S(1)}, u32[]{:S(2)}, u32[]{:S(2)}) collective-permute-start(bf16[2,16,128]{2,1,0:T(8,128)(2,1)} %get-tuple-element.66), channel_id=1, source_target_pairs={{32,64},{64,32},{96,128},{128,96},{160,192},{192,160},{33,65},{65,... | collective-permute-start | bytes 24584 | tf_op jit(solution)/shard_map/ppermute | solution.py:450
  64.4 3.6 %copy-start.8 = (bf16[2,16,128]{2,1,0:T(8,128)(2,1)}, bf16[2,16,128]{2,1,0:T(8,128)(2,1)S(1)}, u32[]{:S(2)}) copy-start(bf16[2,16,128]{2,1,0:T(8,128)(2,1)S(1)} %collective-permute-done.7.refs_2_) | copy-start | bytes 24580
  68.0 0.6 copy-start.9
  70.8 8.1 %collective-permute-start.9 = (bf16[17,16,128]{2,1,0:T(8,128)(2,1)}, bf16[17,16,128]{2,1,0:T(8,128)(2,1)S(1)}, u32[]{:S(2)}, u32[]{:S(2)}) collective-permute-start(bf16[17,16,128]{2,1,0:T(8,128)(2,1)} %get-tuple-element.72), channel_id=1, source_target_pairs={{0,1},{1,0},{2,3},{3,2},{4,5},{5,4},{6,7},{7,6},{8,9},{9,8},{10,11... | collective-permute-start | bytes 208904 | tf_op jit(solution)/shard_map/ppermute | solution.py:466
  78.9 0.6 copy-start.4
where the time goes:
time: 85.2 us; the launch traced here: 84.8 us
  Pallas kernels  30.7 us (36%)
  starting transfers between devices  27.5 us (32%)
  waiting for transfers between devices  19.5 us (23%)
  local copies, waits for them, and re-layouts  6.41 us (8%)
    pallas_call x9, Pallas kernels, call(): pl.pallas_call(kernel, out_shape=tuple(outs), in_specs=[SMEM] * len(scala...  30.7 us
    ppermute x4, starting transfers between devices, per_device(): got = lax.ppermute(msg, 'facet', facet_in)  15.1 us
    ppermute x2, waiting for transfers between devices, per_device(): got = lax.ppermute(msg, 'facet', facet_out)  8.49 us
    ppermute x2, waiting for transfers between devices, per_device(): got_b = lax.ppermute(msg_b, 'grp', grp_out)  6.51 us
    unnamed x21, local copies, waits for them, and re-layouts  6.41 us
    ppermute x2, starting transfers between devices, per_device(): got = lax.ppermute(msg, 'facet', facet_out)  5.34 us
    ppermute x2, starting transfers between devices, per_device(): got_b = lax.ppermute(msg_b, 'grp', grp_out)  4.5 us
    ppermute x4, waiting for transfers between devices, per_device(): got = lax.ppermute(msg, 'facet', facet_in)  4.47 us
  transfers between devices with their start and end apart: 10, of which 8 were waited for; matrix products, arithmetic and copies ran while one was open for 0% of the time, Pallas kernels for 0%

commit v1 on v0

--- a/solution.py
+++ b/solution.py
@@ -22,7 +22,6 @@
 BF16 = jnp.bfloat16
 
 VMEM = pl.BlockSpec(memory_space=pltpu.VMEM)
-SMEM = pl.BlockSpec(memory_space=pltpu.SMEM)
 
 
 def lanes():
@@ -71,7 +70,7 @@
     for b in range(NB):
         value = jnp.zeros((L, 2 * L), F32)
         for e in range(TAPS):
-            value = jnp.where(tap == e, taps[b, 1, e], value)
+            value = jnp.where(tap == e, taps[e, 1, b], value)
         rounded = value.astype(BF16)
         high[b * L : (b + 1) * L, :] = rounded
         low[b * L : (b + 1) * L, :] = (value - rounded.astype(F32)).astype(BF16)
@@ -94,20 +93,45 @@
         for a in range(TAPS):
             r = i - a
             if 0 <= r < R:
-                term = taps[b, 0, a] * rows[r]
+                term = taps[a, 0, b] * rows[r]
                 total = term if total is None else total + term
         high = total.astype(BF16)
         wide_h[i * C : (i + 1) * C, b * L : (b + 1) * L] = high
         wide_l[i * C : (i + 1) * C, b * L : (b + 1) * L] = (total - high.astype(F32)).astype(BF16)
 
 
-def finish_backward(sums, wide_h, wide_l, col_h, col_l, smooth, main, ext, msg):
-    wh = wide_h[...]
-    smooth[...] = (
-        jnp.dot(wh, col_h[...], preferred_element_type=F32)
-        + jnp.dot(wide_l[...], col_h[...], preferred_element_type=F32)
-        + jnp.dot(wh, col_l[...], preferred_element_type=F32)
-    )
+def filter_columns(rows_h, rows_l, col_h, col_l):
+    return (
+        jnp.dot(rows_h, col_h[...], preferred_element_type=F32)
+        + jnp.dot(rows_l, col_h[...], preferred_element_type=F32)
+        + jnp.dot(rows_h, col_l[...], preferred_element_type=F32)
+    )
+
+
+def make_message(sums, wide_h, wide_l, col_h, col_l, smooth, msg):
+    odd = is_odd("facet")
+    tile_row = jnp.where(odd, 0, 2)
+    top = pl.multiple_of(jnp.where(odd, 0, (R + W) * C), C)
+    smooth[...] = filter_columns(
+        wide_h[pl.ds(top, W * C), :], wide_l[pl.ds(top, W * C), :], col_h, col_l
+    )
+    spot = jnp.where(odd, R - W, 0)
+    for h in range(2):
+        xs = swap_blocks([sums[tile_row * 8 + t, :, h * L : (h + 1) * L] for t in range(8)])
+        for i in range(8):
+            r = h * 8 + i
+            value = xs[i]
+            if r < W:
+                value = value + jnp.where(odd, 0.0, smooth[r * C : (r + 1) * C, :L])
+            if r >= R - W:
+                t = r - (R - W)
+                value = value + jnp.where(odd, smooth[t * C : (t + 1) * C, :L], 0.0)
+            msg[r] = value.astype(BF16)
+    msg[R] = pack([smooth[i * C : (i + 1) * C, L:] for i in range(W)]).astype(BF16)
+
+
+def sums_kernel(sums, wide_h, wide_l, col_h, col_l, main, ext, smooth):
+    smooth[...] = filter_columns(wide_h[...], wide_l[...], col_h, col_l)
     for tr in range(3):
         for h in range(2):
             xs = swap_blocks([sums[tr * 8 + t, :, h * L : (h + 1) * L] for t in range(8)])
@@ -120,29 +144,41 @@
                 main[r] = value
     for t in range(RE):
         ext[t] = smooth[t * C : (t + 1) * C, L:]
-    odd = is_odd("facet")
-    base = jnp.where(odd, 0, 2 * R)
-    base_ext = jnp.where(odd, 0, R + W)
-    for r in range(R):
-        msg[r] = main[base + r].astype(BF16)
-    msg[R] = pack([ext[base_ext + i] for i in range(W)]).astype(BF16)
+
+
+def fetch(sources, targets, sems):
+    copies = [pltpu.make_async_copy(s, t, sems.at[i]) for i, (s, t) in enumerate(zip(sources, targets))]
+    for copy in copies:
+        copy.start()
+    return copies
 
 
 def first_kernel(
-    taps, row_ids, col_ids, u, v, blocks,
-    main, ext, msg, u_rows, col_h, col_l,
-    vb, contrib, sums, turned, wide_h, wide_l, smooth,
+    taps_hbm, rows_hbm, cols_hbm, u_hbm, v_hbm, blocks_hbm,
+    sums, wide_h, wide_l, msg, u_rows, col_h, col_l, blocks,
+    taps, row_ids, col_ids, u, v, vb, contrib, turned, smooth, sems,
 ):
+    get_taps, get_u, get_v, get_blocks, get_rows, get_cols = fetch(
+        (taps_hbm, u_hbm, v_hbm, blocks_hbm, rows_hbm, cols_hbm),
+        (taps, u, v, blocks, row_ids, col_ids),
+        sems,
+    )
+    get_taps.wait()
     build_columns(taps, col_h, col_l)
-    vb[...] = v[...].astype(BF16)
-    back_project(vb, blocks, row_ids, col_ids, contrib, sums)
+    get_u.wait()
     for b in range(NB):
         turned[b] = u[b].astype(F32)
         rows = [turned[b, pl.ds(r, C, stride=R), :] for r in range(R)]
         for r in range(R):
             u_rows[b, r * C : (r + 1) * C, :] = rows[r].astype(BF16)
         synth_rows(taps, b, rows, wide_h, wide_l)
-    finish_backward(sums, wide_h, wide_l, col_h, col_l, smooth, main, ext, msg)
+    get_v.wait()
+    get_rows.wait()
+    get_cols.wait()
+    get_blocks.wait()
+    vb[...] = v[...].astype(BF16)
+    back_project(vb, blocks, row_ids, col_ids, contrib, sums)
+    make_message(sums, wide_h, wide_l, col_h, col_l, smooth, msg)
 
 
 def pair_kernel(with_image, *refs):
@@ -289,43 +325,66 @@
             image_out[c * R : (c + 1) * R, :] = turned[pl.ds(c, R, stride=C), :]
 
 
+def near_kernel(e, e_ext, col_h, col_l, flat, wide, edge):
+    odd = is_odd("facet")
+    base_b = jnp.where(odd, 2, 0)
+    for tile_row, base in ((1, 0), (base_b, R)):
+        for h in range(2):
+            xs = swap_blocks([e[base + h * 8 + i].astype(F32) for i in range(8)])
+            for t in range(8):
+                flat[tile_row * 8 + t, :, h * L : (h + 1) * L] = xs[t].astype(BF16)
+    near = jnp.concatenate([e[:R].reshape(R * C, L), e_ext[:R].reshape(R * C, L)], axis=1)
+    wide[...] = spread_columns(near, col_h, col_l)
+    start = jnp.where(odd, R, 2 * R - W)
+    for i in range(W):
+        edge[i * C : (i + 1) * C, :L] = e[start + i]
+        edge[i * C : (i + 1) * C, L:] = e_ext[start + i]
+
+
+def spread_columns(rows, col_h, col_l):
+    both = (((1,), (1,)), ((), ()))
+    return lax.dot_general(rows, col_h[...], both, preferred_element_type=F32) + lax.dot_general(
+        rows, col_l[...], both, preferred_element_type=F32
+    )
+
+
 def dual_kernel(last, *refs):
-    taps, row_ids, col_ids, radii, e, e_ext, got, v, vis, blocks, u_rows, thr, col_h, col_l = refs[:14]
-    refs = refs[14:]
+    taps_hbm, rows_hbm, cols_hbm, radii_hbm = refs[:4]
+    flat_in, inner, edge, got, v, vis, blocks, u_rows, thr, col_h, col_l = refs[4:15]
+    refs = refs[15:]
     if last:
-        v_out, u_out, band, band_ext, near, wide, flat, contrib, sums, turned = refs
+        v_hbm, u_hbm, *refs = refs
+        v_out, u_out, turned, out_sems, *refs = refs
     else:
-        main, ext, msg, v_out, u_out = refs[:5]
-        band, band_ext, near, wide, flat, contrib, sums, turned, vb, tiles, wide_h, wide_l, smooth = refs[5:]
+        sums, wide_h, wide_l, msg, v_out, u_out, *refs = refs
+        vb, tiles, smooth, *refs = refs
+    taps, row_ids, col_ids, radii, sems, flat, wide, edges, contrib, totals = refs
+    get_rows, get_cols, get_radii, get_taps = fetch(
+        (rows_hbm, cols_hbm, radii_hbm, taps_hbm), (row_ids, col_ids, radii, taps), sems
+    )
     odd = is_odd("facet")
     lane = lanes()
-    base_a = jnp.where(odd, 0, 2 * R)
-    base_b = jnp.where(odd, 2 * R, 0)
-    packed = got[R].astype(F32)
-    for r in range(R):
-        band[R + r] = e[r].astype(F32)
-        band[base_b + r] = e[R + r].astype(F32)
-        band[base_a + r] = got[r].astype(F32)
-        band_ext[R + r] = e_ext[r].astype(F32)
-        band_ext[base_b + r] = e_ext[R + r].astype(F32)
-        band_ext[base_a + r] = unpack(packed, r, lane)
-    for t in range(RE):
-        near[t * C : (t + 1) * C, :L] = band[R - W + t].astype(BF16)
-        near[t * C : (t + 1) * C, L:] = band_ext[R - W + t].astype(BF16)
-    for tr in range(3):
-        for h in range(2):
-            xs = swap_blocks([band[tr * R + h * 8 + i] for i in range(8)])
-            for t in range(8):
-                flat[tr * 8 + t, :, h * L : (h + 1) * L] = xs[t].astype(BF16)
+    tile_a = jnp.where(odd, 0, 2)
+    tile_b = jnp.where(odd, 2, 0)
+    for h in range(2):
+        xs = swap_blocks([got[h * 8 + i].astype(F32) for i in range(8)])
+        for t in range(8):
+            flat[tile_a * 8 + t, :, h * L : (h + 1) * L] = xs[t].astype(BF16)
+    for t in range(8):
+        flat[8 + t] = flat_in[8 + t]
+        flat[tile_b * 8 + t] = flat_in[tile_b * 8 + t]
+    get_rows.wait()
+    get_cols.wait()
     for k in range(KDEV):
         contrib[k] = jnp.dot(flat[col_ids[k]], blocks[k], preferred_element_type=F32)
-    sums[...] = jnp.zeros(sums.shape, F32)
+    totals[...] = jnp.zeros(totals.shape, F32)
     for k in range(KDEV):
         r = row_ids[k]
-        sums[r] = sums[r] + contrib[k]
+        totals[r] = totals[r] + contrib[k]
+    get_radii.wait()
     for r in range(RB):
         seen = vis[r]
-        moved = v[r] + 0.5 * sums[r]
+        moved = v[r] + 0.5 * totals[r]
         offset = 2.0 * moved - seen
         length = jnp.sqrt(jnp.sum(jnp.sum(offset * offset, axis=1, keepdims=True), axis=0, keepdims=True))
         scale = radii[r] / jnp.maximum(length, radii[r])
@@ -333,18 +392,42 @@
         v_out[r] = new
         if not last:
             vb[r] = new.astype(BF16)
-    both = (((1,), (1,)), ((), ()))
-    wide[...] = lax.dot_general(
-        near[...], col_h[...], both, preferred_element_type=F32
-    ) + lax.dot_general(near[...], col_l[...], both, preferred_element_type=F32)
+    if last:
+        put_v = pltpu.make_async_copy(v_out, v_hbm, out_sems.at[NB])
+        put_v.start()
+    packed = got[R].astype(F32)
+    near_a = jnp.where(odd, R - W, 0)
+    above, below = edges.at[0], edges.at[1]
+    for i in range(W):
+        rows = slice(i * C, (i + 1) * C)
+        mine = edge[rows, :]
+        theirs = jnp.concatenate(
+            [got[near_a + i].astype(F32), jnp.where(lane < 2 * W, jnp.where(odd, roll(packed, -8 * (R - W + i)), roll(packed, -8 * i)), 0.0)],
+            axis=1,
+        ).astype(BF16)
+        above[rows, :] = jnp.where(odd, theirs, mine)
+        below[rows, :] = jnp.where(odd, mine, theirs)
+    wide[: W * C, :] = spread_columns(above[...], col_h, col_l)
+    wide[W * C :, :] = spread_columns(below[...], col_h, col_l)
     if not last:
-        back_project(vb, blocks, row_ids, col_ids, tiles[0], tiles[1])
+        back_project(vb, blocks, row_ids, col_ids, tiles, sums)
+    get_taps.wait()
+
+    def filtered(t, b):
+        cols = slice(b * L, (b + 1) * L)
+        if t < W:
+            return wide[t * C : (t + 1) * C, cols]
+        if t < W + R:
+            return inner[(t - W) * C : (t - W + 1) * C, cols]
+        return wide[(t - R) * C : (t - R + 1) * C, cols]
+
+    puts = []
     for b in range(NB):
         rows = []
         for r in range(R):
             total = None
             for a in range(TAPS):
-                term = taps[b, 0, a] * wide[(r + a) * C : (r + a + 1) * C, b * L : (b + 1) * L]
+                term = taps[a, 0, b] * filtered(r + a, b)
                 total = term if total is None else total + term
             full = u_rows[b, r * C : (r + 1) * C, :].astype(F32) + 0.5 * total
             size = jnp.sqrt(jnp.sum(full * full, axis=0, keepdims=True))
@@ -359,10 +442,17 @@
         if last:
             for c in range(C):
                 u_out[b, c * R : (c + 1) * R, :] = turned[b, pl.ds(c, R, stride=C), :].astype(BF16)
+            put = pltpu.make_async_copy(u_out.at[b], u_hbm.at[b], out_sems.at[b])
+            put.start()
+            puts.append(put)
         else:
             synth_rows(taps, b, rows, wide_h, wide_l)
-    if not last:
-        finish_backward(tiles[1], wide_h, wide_l, col_h, col_l, smooth, main, ext, msg)
+    if last:
+        put_v.wait()
+        for put in puts:
+            put.wait()
+    else:
+        make_message(sums, wide_h, wide_l, col_h, col_l, smooth, msg)
 
 
 def shape(dims, dtype=F32):
@@ -373,18 +463,28 @@
     return pltpu.VMEM(dims, dtype)
 
 
-BACK = [shape((BAND, C, L)), shape((RE, C, L)), shape((R + 1, C, L), BF16)]
-
-
-def call(kernel, scalars, arrays, outs, temps=(), name=None):
+def small(dims, dtype):
+    return pltpu.SMEM(dims, dtype)
+
+
+HALF = [shape((NT3, C, VB)), shape((RE * C, NB * L), BF16), shape((RE * C, NB * L), BF16), shape((R + 1, C, L), BF16)]
+
+
+def call(kernel, far, arrays, outs, temps=(), name=None, mib=8, final=0):
+    far = [pltpu.with_memory_space_constraint(a, pltpu.HBM) for a in far]
+    arrays = [pltpu.with_memory_space_constraint(a, pltpu.VMEM) for a in arrays]
+    anywhere = pl.BlockSpec(memory_space=pl.ANY)
     return pl.pallas_call(
         kernel,
-        out_shape=tuple(outs),
-        in_specs=[SMEM] * len(scalars) + [VMEM] * len(arrays),
-        out_specs=tuple(VMEM for _ in outs),
+        out_shape=tuple(
+            (pltpu.HBM if i < final else pltpu.VMEM)(o.shape, o.dtype) for i, o in enumerate(outs)
+        ),
+        in_specs=[anywhere] * len(far) + [VMEM] * len(arrays),
+        out_specs=tuple(anywhere if i < final else VMEM for i in range(len(outs))),
         scratch_shapes=list(temps),
+        compiler_params=pltpu.CompilerParams(vmem_limit_bytes=mib << 20),
         name=name,
-    )(*scalars, *arrays)
+    )(*far, *arrays)
 
 
 def pairs_of(axis):
@@ -400,29 +500,48 @@
 ):
     image_rows = image.reshape(C * R, L)
     u = wavelet_dual.reshape(NB, C * R, L)
-    operators, seen, v = blocks[0, 0], visibilities[0, 0], data_dual[0, 0]
+    seen, v = visibilities[0, 0], data_dual[0, 0]
     radii, row_ids, col_ids = ball_radii[0, 0], row_index[0, 0], col_index[0, 0]
+    taps = filter_taps.transpose(2, 1, 0)
     facet_in, facet_out = pairs_of("facet")
     grp_in, grp_out = pairs_of("grp")
-    synth_temps = [
-        scratch(NB, C * R, L),
-        scratch(RE * C, NB * L, dtype=BF16),
-        scratch(RE * C, NB * L, dtype=BF16),
-        scratch(RE * C, 2 * L),
-    ]
-    main, ext, msg, u, col_h, col_l = call(
+    scalars = [small((TAPS, 2, NB), F32), small((KDEV,), jnp.int32), small((KDEV,), jnp.int32)]
+    sums, wide_h, wide_l, msg, u, col_h, col_l, operators = call(
         first_kernel,
-        (filter_taps, row_ids, col_ids),
-        (u, v, operators),
-        BACK
-        + [shape((NB, R * C, L), BF16), shape((NB * L, 2 * L), BF16), shape((NB * L, 2 * L), BF16)],
-        [scratch(RB, C, VB, dtype=BF16), scratch(KDEV, C, VB), scratch(NT3, C, VB)] + synth_temps,
+        (taps, row_ids, col_ids, u, v, blocks[0, 0]),
+        (),
+        HALF
+        + [
+            shape((NB, R * C, L), BF16),
+            shape((NB * L, 2 * L), BF16),
+            shape((NB * L, 2 * L), BF16),
+            shape((KDEV, VB, VB), BF16),
+        ],
+        scalars
+        + [
+            scratch(NB, C * R, L, dtype=BF16),
+            scratch(RB, C, VB),
+            scratch(RB, C, VB, dtype=BF16),
+            scratch(KDEV, C, VB),
+            scratch(NB, C * R, L),
+            scratch(W * C, 2 * L),
+            pltpu.SemaphoreType.DMA((6,)),
+        ],
         name="first",
+        mib=16,
     )
     x = x_ext = None
     for iteration in range(ITERS):
         first, last = iteration == 0, iteration == ITERS - 1
         got = lax.ppermute(msg, "facet", facet_in)
+        main, ext = call(
+            sums_kernel,
+            (),
+            (sums, wide_h, wide_l, col_h, col_l),
+            [shape((BAND, C, L)), shape((RE, C, L))],
+            [scratch(RE * C, 2 * L)],
+            name="sums",
+        )
         total, total_ext, msg = call(
             lambda *refs: pair_kernel(first, *refs),
             (),
@@ -464,33 +583,45 @@
         else:
             x, x_ext = results[:2]
         got = lax.ppermute(msg, "facet", facet_in)
-        temps = [
-            scratch(BAND, C, L),
-            scratch(BAND, C, L),
-            scratch(RE * C, 2 * L, dtype=BF16),
-            scratch(RE * C, NB * L),
-            scratch(NT3, C, VB, dtype=BF16),
-            scratch(KDEV, C, VB),
-            scratch(RB, C, VB),
-        ]
+        flat, inner, edge = call(
+            near_kernel,
+            (),
+            (e, e_ext, col_h, col_l),
+            [shape((NT3, C, VB), BF16), shape((R * C, NB * L)), shape((W * C, 2 * L), BF16)],
+            name="near",
+        )
+        outs = [shape((RB, C, VB)), shape((NB, R * C, L), BF16)]
         if last:
-            temps += synth_temps[:1]
+            temps = [
+                scratch(RB, C, VB),
+                scratch(NB, C * R, L, dtype=BF16),
+                scratch(NB, R * C, L),
+                pltpu.SemaphoreType.DMA((NB + 1,)),
+            ]
         else:
-            temps += [
-                synth_temps[0],
-                scratch(RB, C, VB, dtype=BF16),
-                (scratch(KDEV, C, VB), scratch(NT3, C, VB)),
-            ] + synth_temps[1:]
-        *back, v, u = call(
+            temps = [scratch(RB, C, VB, dtype=BF16), scratch(KDEV, C, VB), scratch(W * C, 2 * L)]
+        *half, v, u = call(
             lambda *refs: dual_kernel(last, *refs),
-            (filter_taps, row_ids, col_ids, radii),
-            (e, e_ext, got, v, seen, operators, u, thresholds, col_h, col_l),
-            ([] if last else BACK) + [shape((RB, C, VB)), shape((NB, R * C, L), BF16)],
-            temps,
+            (taps, row_ids, col_ids, radii),
+            (flat, inner, edge, got, v, seen, operators, u, thresholds, col_h, col_l),
+            ([] if last else HALF) + outs,
+            temps
+            + scalars
+            + [
+                small((RB,), F32),
+                pltpu.SemaphoreType.DMA((4,)),
+                scratch(NT3, C, VB, dtype=BF16),
+                scratch(2 * W * C, NB * L),
+                scratch(2, W * C, 2 * L, dtype=BF16),
+                scratch(KDEV, C, VB),
+                scratch(RB, C, VB),
+            ],
             name="dual",
+            mib=16,
+            final=2 if last else 0,
         )
         if not last:
-            main, ext, msg = back
+            sums, wide_h, wide_l, msg = half
     return (image_out.reshape(C, R, L), v[None, None], u.reshape(NB, C, R, L))
 
 

time: 85.2 us -> 61.4 us (0.72)
  Pallas kernels: 30.7 us -> 16.3 us
  local copies, waits for them, and re-layouts: 6.41 us -> 0.68 us
  waiting for transfers between devices: 19.5 us -> 14.9 us
    pallas_call x9 -> x13, Pallas kernels: 30.7 us -> 16.3 us  [call(): pl.pallas_call(kernel, out_shape=tuple(((pltpu.HBM if i < final else pltp...]
    unnamed x21 -> x9, local copies, waits for them, and re-layouts: 6.41 us -> 0.68 us
    ppermute x4, waiting for transfers between devices: 4.47 us -> 0.73 us  [per_device(): got = lax.ppermute(msg, 'facet', facet_in)]
  transfers between devices with their start and end apart: 10 -> 10, of which waited for: 8 -> 7; matrix products, arithmetic and copies ran while one was open for 0% -> 1% of each run, Pallas kernels for 0% -> 4%
where the time goes in v1:
time: 61.4 us; the launch traced here: 61.1 us
  starting transfers between devices  28.3 us (46%)
  Pallas kernels  16.3 us (27%)
  waiting for transfers between devices  14.9 us (24%)
  between operations  0.96 us (2%)
  local copies, waits for them, and re-layouts  0.68 us (1%)
    pallas_call x13, Pallas kernels, call(): pl.pallas_call(kernel, out_shape=tuple(((pltpu.HBM if i < final else pltp...  16.3 us
    ppermute x4, starting transfers between devices, per_device(): got = lax.ppermute(msg, 'facet', facet_in)  15.8 us
    ppermute x2, waiting for transfers between devices, per_device(): got = lax.ppermute(msg, 'facet', facet_out)  8.08 us
    ppermute x2, waiting for transfers between devices, per_device(): got_b = lax.ppermute(msg_b, 'grp', grp_out)  6.11 us
    ppermute x2, starting transfers between devices, per_device(): got = lax.ppermute(msg, 'facet', facet_out)  5.36 us
    ppermute x2, starting transfers between devices, per_device(): got_b = lax.ppermute(msg_b, 'grp', grp_out)  4.51 us
    ppermute x2, starting transfers between devices, per_device(): got_a = lax.ppermute(msg_a, 'grp', grp_in)  2.63 us
  transfers between devices with their start and end apart: 10, of which 7 were waited for; matrix products, arithmetic and copies ran while one was open for 1% of the time, Pallas kernels for 4%

profile of v1, /device:TPU:131, one launch (start us, length us, event | category | flops | bytes accessed | tf_op | source)
XLA Modules:
  0.0 61.1 jit_solution(5856999177191950525)
XLA Ops:
  0.6 3.6 %first.1 = (f32[24,16,256]{2,1,0:T(8,128)S(1)}, bf16[352,1024]{1,0:T(8,128)(2,1)S(1)}, bf16[352,1024]{1,0:T(8,128)(2,1)S(1)}, bf16[17,16,128]{2,1,0:T(8,128)(2,1...) custom-call(f32[7,2,8]{2,1,0:T(2,128)} %bitcast.21, ...), custom_call_target="tpu_custom_call" | custom-call | tf_op jit(solution)/shard_map/first/pallas_call | solution.py:477
  4.2 0.0 copy-start.1
  4.2 0.8 %collective-permute-start = (bf16[17,16,128]{2,1,0:T(8,128)(2,1)S(1)}, bf16[17,16,128]{2,1,0:T(8,128)(2,1)S(1)}, u32[]{:S(2)}, u32[]{:S(2)}) collective-permute-start(bf16[17,16,128]{2,1,0:T(8,128)(2,1)S(1)} %get-tuple-element.60), channel_id=1, source_target_pairs={{0,1},{1,0},{2,3},{3,2},{4,5},{5,4},{6,7},{7,6},{8,9},{9,8},{10,11... | collective-permute-start | bytes 208904 | tf_op jit(solution)/shard_map/ppermute | solution.py:536
  5.0 0.7 %sums.2 = (f32[48,16,128]{2,1,0:T(8,128)S(1)}, f32[22,16,128]{2,1,0:T(8,128)S(1)}) custom-call(f32[24,16,256]{2,1,0:T(8,128)S(1)} %get-tuple-element.53.sums, bf16[352,1024]{1,0:T(8,128)(2,1)S(1)} %get-tuple-element.54.wide_h, bf16[352,1024]{1,0:T(8,128)(2,1)S(1)} %get-tuple-element.55.wide_l, bf16[1024,256]{1,0:T(8,128)(2,1)S(1)} %get-tuple-element.56.col_h.refs_13_, ...), custom_call_target="tpu_custom_call" | custom-call | tf_op jit(solution)/shard_map/sums/pallas_call | solution.py:477
  5.7 0.0 copy-start
  5.7 0.0 copy-start.2
  5.7 0.0 copy-start.3
  5.8 0.1 collective-permute-done.refs_2_
  5.9 0.0 copy-done.1
  5.9 0.2 pair.2
  6.1 3.4 %collective-permute-start.1 = (bf16[50,16,128]{2,1,0:T(8,128)(2,1)S(1)}, bf16[50,16,128]{2,1,0:T(8,128)(2,1)S(1)}, u32[]{:S(2)}, u32[]{:S(2)}) collective-permute-start(bf16[50,16,128]{2,1,0:T(8,128)(2,1)S(1)} %get-tuple-element.63), channel_id=1, source_target_pairs={{1,2},{2,1},{3,4},{4,3},{5,6},{6,5},{7,8},{8,7},{9,10},{10,9},{11,... | collective-permute-start | bytes 614408 | tf_op jit(solution)/shard_map/ppermute | solution.py:556
  9.5 3.6 %collective-permute-done.1.refs_4_ = bf16[50,16,128]{2,1,0:T(8,128)(2,1)S(1)} collective-permute-done((bf16[50,16,128]{2,1,0:T(8,128)(2,1)S(1)}, bf16[50,16,128]{2,1,0:T(8,128)(2,1)S(1)}, u32[]{:S(2)}, u32[]{:S(2)}) %collective-permute-start.1) | collective-permute-done | bytes 204832 | tf_op jit(solution)/shard_map/ppermute | solution.py:556
  13.2 0.3 rim.2
  13.5 0.8 %collective-permute-start.2 = (bf16[4,16,128]{2,1,0:T(8,128)(2,1)S(1)}, bf16[4,16,128]{2,1,0:T(8,128)(2,1)S(1)}, u32[]{:S(2)}, u32[]{:S(2)}) collective-permute-start(bf16[4,16,128]{2,1,0:T(8,128)(2,1)S(1)} %get-tuple-element.66), channel_id=1, source_target_pairs={{0,32},{32,0},{64,96},{96,64},{128,160},{160,128},{192,224},{224,1... | collective-permute-start | bytes 49160 | tf_op jit(solution)/shard_map/ppermute | solution.py:568
  14.3 2.6 %collective-permute-start.3 = (bf16[4,16,128]{2,1,0:T(8,128)(2,1)S(1)}, bf16[4,16,128]{2,1,0:T(8,128)(2,1)S(1)}, u32[]{:S(2)}, u32[]{:S(2)}) collective-permute-start(bf16[4,16,128]{2,1,0:T(8,128)(2,1)S(1)} %get-tuple-element.67), channel_id=1, source_target_pairs={{32,64},{64,32},{96,128},{128,96},{160,192},{192,160},{33,65},{65,... | collective-permute-start | bytes 49160 | tf_op jit(solution)/shard_map/ppermute | solution.py:569
  16.9 0.0 collective-permute-done.2.refs_2_
  16.9 2.8 %collective-permute-done.3.refs_3_ = bf16[4,16,128]{2,1,0:T(8,128)(2,1)S(1)} collective-permute-done((bf16[4,16,128]{2,1,0:T(8,128)(2,1)S(1)}, bf16[4,16,128]{2,1,0:T(8,128)(2,1)S(1)}, u32[]{:S(2)}, u32[]{:S(2)}) %collective-permute-start.3) | collective-permute-done | bytes 16416 | tf_op jit(solution)/shard_map/ppermute | solution.py:569
  19.7 0.3 primal.2
  20.0 7.4 %collective-permute-start.4 = (bf16[17,16,128]{2,1,0:T(8,128)(2,1)S(1)}, bf16[17,16,128]{2,1,0:T(8,128)(2,1)S(1)}, u32[]{:S(2)}, u32[]{:S(2)}) collective-permute-start(bf16[17,16,128]{2,1,0:T(8,128)(2,1)S(1)} %get-tuple-element.74), channel_id=1, source_target_pairs={{0,1},{1,0},{2,3},{3,2},{4,5},{5,4},{6,7},{7,6},{8,9},{9,8},{10,11... | collective-permute-start | bytes 208904 | tf_op jit(solution)/shard_map/ppermute | solution.py:585
  27.4 0.5 near.2
  27.9 0.4 collective-permute-done.4.refs_7_
  28.3 0.0 copy-done
  28.3 0.0 copy-done.2
  28.3 0.0 copy-done.3
  28.3 4.8 %dual.2 = (f32[24,16,256]{2,1,0:T(8,128)S(1)}, bf16[352,1024]{1,0:T(8,128)(2,1)S(1)}, bf16[352,1024]{1,0:T(8,128)(2,1)S(1)}, bf16[17,16,128]{2,1,0:T(8,128)(2,1)...) custom-call(f32[7,2,8]{2,1,0:T(2,128)} %bitcast.22, s32[16]{0:T(128)} %bitcast.25, s32[16]{0:T(128)} %bitcast.28, ...), custom_call_target="tpu_custom_call" | custom-call | tf_op jit(solution)/shard_map/dual/pallas_call | solution.py:477
  33.1 0.5 collective-permute-start.5
  33.6 0.7 %sums.3 = (f32[48,16,128]{2,1,0:T(8,128)S(1)}, f32[22,16,128]{2,1,0:T(8,128)S(1)}) custom-call(f32[24,16,256]{2,1,0:T(8,128)S(1)} %get-tuple-element.77.sums, bf16[352,1024]{1,0:T(8,128)(2,1)S(1)} %get-tuple-element.78.wide_h, bf16[352,1024]{1,0:T(8,128)(2,1)S(1)} %get-tuple-element.79.wide_l, bf16[1024,256]{1,0:T(8,128)(2,1)S(1)} %get-tuple-element.56.col_h.refs_13_, ...), custom_call_target="tpu_custom_call" | custom-call | tf_op jit(solution)/shard_map/sums/pallas_call | solution.py:477
  34.3 0.2 collective-permute-done.5.refs_2_
  34.5 0.2 pair.3
  34.6 1.9 %collective-permute-start.6 = (bf16[34,16,128]{2,1,0:T(8,128)(2,1)S(1)}, bf16[34,16,128]{2,1,0:T(8,128)(2,1)S(1)}, u32[]{:S(2)}, u32[]{:S(2)}) collective-permute-start(bf16[34,16,128]{2,1,0:T(8,128)(2,1)S(1)} %get-tuple-element.85), channel_id=1, source_target_pairs={{1,2},{2,1},{3,4},{4,3},{5,6},{6,5},{7,8},{8,7},{9,10},{10,9},{11,... | collective-permute-start | bytes 417800 | tf_op jit(solution)/shard_map/ppermute | solution.py:556
  36.6 4.4 %collective-permute-done.6.refs_4_ = bf16[34,16,128]{2,1,0:T(8,128)(2,1)S(1)} collective-permute-done((bf16[34,16,128]{2,1,0:T(8,128)(2,1)S(1)}, bf16[34,16,128]{2,1,0:T(8,128)(2,1)S(1)}, u32[]{:S(2)}, u32[]{:S(2)}) %collective-permute-start.6) | collective-permute-done | bytes 139296 | tf_op jit(solution)/shard_map/ppermute | solution.py:556
  41.0 0.3 rim.3
  41.3 1.8 %collective-permute-start.7 = (bf16[2,16,128]{2,1,0:T(8,128)(2,1)S(1)}, bf16[2,16,128]{2,1,0:T(8,128)(2,1)S(1)}, u32[]{:S(2)}, u32[]{:S(2)}) collective-permute-start(bf16[2,16,128]{2,1,0:T(8,128)(2,1)S(1)} %get-tuple-element.88), channel_id=1, source_target_pairs={{0,32},{32,0},{64,96},{96,64},{128,160},{160,128},{192,224},{224,1... | collective-permute-start | bytes 24584 | tf_op jit(solution)/shard_map/ppermute | solution.py:568
  43.1 1.9 %collective-permute-start.8 = (bf16[2,16,128]{2,1,0:T(8,128)(2,1)S(1)}, bf16[2,16,128]{2,1,0:T(8,128)(2,1)S(1)}, u32[]{:S(2)}, u32[]{:S(2)}) collective-permute-start(bf16[2,16,128]{2,1,0:T(8,128)(2,1)S(1)} %get-tuple-element.89), channel_id=1, source_target_pairs={{32,64},{64,32},{96,128},{128,96},{160,192},{192,160},{33,65},{65,... | collective-permute-start | bytes 24584 | tf_op jit(solution)/shard_map/ppermute | solution.py:569
  45.0 0.0 collective-permute-done.7.refs_2_
  45.0 3.4 %collective-permute-done.8.refs_3_ = bf16[2,16,128]{2,1,0:T(8,128)(2,1)S(1)} collective-permute-done((bf16[2,16,128]{2,1,0:T(8,128)(2,1)S(1)}, bf16[2,16,128]{2,1,0:T(8,128)(2,1)S(1)}, u32[]{:S(2)}, u32[]{:S(2)}) %collective-permute-start.8) | collective-permute-done | bytes 8224 | tf_op jit(solution)/shard_map/ppermute | solution.py:569
  48.4 0.3 primal.3
  48.7 7.2 %collective-permute-start.9 = (bf16[17,16,128]{2,1,0:T(8,128)(2,1)S(1)}, bf16[17,16,128]{2,1,0:T(8,128)(2,1)S(1)}, u32[]{:S(2)}, u32[]{:S(2)}) collective-permute-start(bf16[17,16,128]{2,1,0:T(8,128)(2,1)S(1)} %get-tuple-element.98), channel_id=1, source_target_pairs={{0,1},{1,0},{2,3},{3,2},{4,5},{5,4},{6,7},{7,6},{8,9},{9,8},{10,11... | collective-permute-start | bytes 208904 | tf_op jit(solution)/shard_map/ppermute | solution.py:585
  56.0 0.7 %copy.13 = f32[16,16,128]{2,1,0:T(8,128)} copy(f32[16,16,128]{2,1,0:T(8,128)S(1)} %bitcast.12) | data formatting | bytes 262144
  56.6 0.5 near.3
  57.1 0.0 collective-permute-done.9.refs_7_
  57.1 3.8 %dual.3 = (f32[8,16,256]{2,1,0:T(8,128)}, bf16[8,256,128]{2,1,0:T(8,128)(2,1)}) custom-call(f32[7,2,8]{2,1,0:T(2,128)} %bitcast.23, s32[16]{0:T(128)} %bitcast.26, s32[16]{0:T(128)} %bitcast.29, f32[8]{0:T(128)} %bitcast.31, bf16[24,16,256]{2,1,0:T(8,128)(2,1)S(1)} %get-tuple-element.95.refs_4_, f32[256,1024]{1,0:T(8,128)S(1)} %get-tuple-element.96.refs_5_, ...), custom_call_target="tpu_custom_call" | custom-call | tf_op jit(solution)/shard_map/dual/pallas_call | solution.py:477
Async XLA Ops:
  4.2 1.7 %copy-start.1 = (f32[16,16,128]{2,1,0:T(8,128)S(1)}, f32[16,16,128]{2,1,0:T(8,128)}, u32[]{:S(2)}) copy-start(f32[16,16,128]{2,1,0:T(8,128)} %param.10) | copy-start | bytes 393220
  4.2 1.7 %collective-permute-start = (bf16[17,16,128]{2,1,0:T(8,128)(2,1)S(1)}, bf16[17,16,128]{2,1,0:T(8,128)(2,1)S(1)}, u32[]{:S(2)}, u32[]{:S(2)}) collective-permute-start(bf16[17,16,128]{2,1,0:T(8,128)(2,1)S(1)} %get-tuple-element.60), channel_id=1, source_target_pairs={{0,1},{1,0},{2,3},{3,2},{4,5},{5,4},{6,7},{7,6},{8,9},{9,8},{10,11... | collective-permute-start | bytes 208904 | tf_op jit(solution)/shard_map/ppermute | solution.py:536
  5.7 22.6 %copy-start = (f32[1,1,8,16,256]{4,3,2,1,0:T(8,128)S(1)}, f32[1,1,8,16,256]{4,3,2,1,0:T(8,128)}, u32[]{:S(2)}) copy-start(f32[1,1,8,16,256]{4,3,2,1,0:T(8,128)} %param.14) | copy-start | bytes 393220
  5.7 22.6 %copy-start.2 = (f32[1,1,8,16,256]{4,3,2,1,0:T(8,128)S(1)}, f32[1,1,8,16,256]{4,3,2,1,0:T(8,128)}, u32[]{:S(2)}) copy-start(f32[1,1,8,16,256]{4,3,2,1,0:T(8,128)} %param.15) | copy-start | bytes 393220
  5.7 22.6 %copy-start.3 = (f32[8,16,128]{2,1,0:T(8,128)S(1)}, f32[8,16,128]{2,1,0:T(8,128)}, u32[]{:S(2)}) copy-start(f32[8,16,128]{2,1,0:T(8,128)} %refs_12_.3) | copy-start | bytes 196612
  6.1 7.1 %collective-permute-start.1 = (bf16[50,16,128]{2,1,0:T(8,128)(2,1)S(1)}, bf16[50,16,128]{2,1,0:T(8,128)(2,1)S(1)}, u32[]{:S(2)}, u32[]{:S(2)}) collective-permute-start(bf16[50,16,128]{2,1,0:T(8,128)(2,1)S(1)} %get-tuple-element.63), channel_id=1, source_target_pairs={{1,2},{2,1},{3,4},{4,3},{5,6},{6,5},{7,8},{8,7},{9,10},{10,9},{11,... | collective-permute-start | bytes 614408 | tf_op jit(solution)/shard_map/ppermute | solution.py:556
  13.5 3.4 %collective-permute-start.2 = (bf16[4,16,128]{2,1,0:T(8,128)(2,1)S(1)}, bf16[4,16,128]{2,1,0:T(8,128)(2,1)S(1)}, u32[]{:S(2)}, u32[]{:S(2)}) collective-permute-start(bf16[4,16,128]{2,1,0:T(8,128)(2,1)S(1)} %get-tuple-element.66), channel_id=1, source_target_pairs={{0,32},{32,0},{64,96},{96,64},{128,160},{160,128},{192,224},{224,1... | collective-permute-start | bytes 49160 | tf_op jit(solution)/shard_map/ppermute | solution.py:568
  14.3 5.4 %collective-permute-start.3 = (bf16[4,16,128]{2,1,0:T(8,128)(2,1)S(1)}, bf16[4,16,128]{2,1,0:T(8,128)(2,1)S(1)}, u32[]{:S(2)}, u32[]{:S(2)}) collective-permute-start(bf16[4,16,128]{2,1,0:T(8,128)(2,1)S(1)} %get-tuple-element.67), channel_id=1, source_target_pairs={{32,64},{64,32},{96,128},{128,96},{160,192},{192,160},{33,65},{65,... | collective-permute-start | bytes 49160 | tf_op jit(solution)/shard_map/ppermute | solution.py:569
  20.0 8.3 %collective-permute-start.4 = (bf16[17,16,128]{2,1,0:T(8,128)(2,1)S(1)}, bf16[17,16,128]{2,1,0:T(8,128)(2,1)S(1)}, u32[]{:S(2)}, u32[]{:S(2)}) collective-permute-start(bf16[17,16,128]{2,1,0:T(8,128)(2,1)S(1)} %get-tuple-element.74), channel_id=1, source_target_pairs={{0,1},{1,0},{2,3},{3,2},{4,5},{5,4},{6,7},{7,6},{8,9},{9,8},{10,11... | collective-permute-start | bytes 208904 | tf_op jit(solution)/shard_map/ppermute | solution.py:585
  33.1 1.4 %collective-permute-start.5 = (bf16[17,16,128]{2,1,0:T(8,128)(2,1)S(1)}, bf16[17,16,128]{2,1,0:T(8,128)(2,1)S(1)}, u32[]{:S(2)}, u32[]{:S(2)}) collective-permute-start(bf16[17,16,128]{2,1,0:T(8,128)(2,1)S(1)} %get-tuple-element.82), channel_id=1, source_target_pairs={{0,1},{1,0},{2,3},{3,2},{4,5},{5,4},{6,7},{7,6},{8,9},{9,8},{10,11... | collective-permute-start | bytes 208904 | tf_op jit(solution)/shard_map/ppermute | solution.py:536
  34.6 6.4 %collective-permute-start.6 = (bf16[34,16,128]{2,1,0:T(8,128)(2,1)S(1)}, bf16[34,16,128]{2,1,0:T(8,128)(2,1)S(1)}, u32[]{:S(2)}, u32[]{:S(2)}) collective-permute-start(bf16[34,16,128]{2,1,0:T(8,128)(2,1)S(1)} %get-tuple-element.85), channel_id=1, source_target_pairs={{1,2},{2,1},{3,4},{4,3},{5,6},{6,5},{7,8},{8,7},{9,10},{10,9},{11,... | collective-permute-start | bytes 417800 | tf_op jit(solution)/shard_map/ppermute | solution.py:556
  41.3 3.7 %collective-permute-start.7 = (bf16[2,16,128]{2,1,0:T(8,128)(2,1)S(1)}, bf16[2,16,128]{2,1,0:T(8,128)(2,1)S(1)}, u32[]{:S(2)}, u32[]{:S(2)}) collective-permute-start(bf16[2,16,128]{2,1,0:T(8,128)(2,1)S(1)} %get-tuple-element.88), channel_id=1, source_target_pairs={{0,32},{32,0},{64,96},{96,64},{128,160},{160,128},{192,224},{224,1... | collective-permute-start | bytes 24584 | tf_op jit(solution)/shard_map/ppermute | solution.py:568
  43.1 5.3 %collective-permute-start.8 = (bf16[2,16,128]{2,1,0:T(8,128)(2,1)S(1)}, bf16[2,16,128]{2,1,0:T(8,128)(2,1)S(1)}, u32[]{:S(2)}, u32[]{:S(2)}) collective-permute-start(bf16[2,16,128]{2,1,0:T(8,128)(2,1)S(1)} %get-tuple-element.89), channel_id=1, source_target_pairs={{32,64},{64,32},{96,128},{128,96},{160,192},{192,160},{33,65},{65,... | collective-permute-start | bytes 24584 | tf_op jit(solution)/shard_map/ppermute | solution.py:569
  48.7 8.4 %collective-permute-start.9 = (bf16[17,16,128]{2,1,0:T(8,128)(2,1)S(1)}, bf16[17,16,128]{2,1,0:T(8,128)(2,1)S(1)}, u32[]{:S(2)}, u32[]{:S(2)}) collective-permute-start(bf16[17,16,128]{2,1,0:T(8,128)(2,1)S(1)} %get-tuple-element.98), channel_id=1, source_target_pairs={{0,1},{1,0},{2,3},{3,2},{4,5},{5,4},{6,7},{7,6},{8,9},{9,8},{10,11... | collective-permute-start | bytes 208904 | tf_op jit(solution)/shard_map/ppermute | solution.py:585

commit v2 on v1

--- a/solution.py
+++ b/solution.py
@@ -62,60 +62,72 @@
     return xs
 
 
-def build_columns(taps, high, low):
-    n = lax.broadcasted_iota(jnp.int32, (L, 2 * L), 1)
-    j = lax.broadcasted_iota(jnp.int32, (L, 2 * L), 0)
-    place = jnp.where(n < L, n, jnp.where(n < L + W, n - L - W, n - W))
-    tap = jnp.where(n < L + 2 * W, place - j + W, -1)
-    for b in range(NB):
-        value = jnp.zeros((L, 2 * L), F32)
-        for e in range(TAPS):
-            value = jnp.where(tap == e, taps[e, 1, b], value)
-        rounded = value.astype(BF16)
-        high[b * L : (b + 1) * L, :] = rounded
-        low[b * L : (b + 1) * L, :] = (value - rounded.astype(F32)).astype(BF16)
-
-
-def back_project(vb, blocks, row_ids, col_ids, contrib, sums):
+def build_columns(col_taps, high, low):
+    strip = 8
+    for start in range(0, L, strip):
+        j = start + lax.broadcasted_iota(jnp.int32, (strip, L), 0)
+        n = lax.broadcasted_iota(jnp.int32, (strip, L), 1)
+        outside = jnp.where(n < W, n - W, jnp.where(n < 2 * W, n - W + L, 2 * L))
+        edge = start == 0 or start == L - strip
+        for tile, place in ((0, n), (1, outside)):
+            tap = place - j + W
+            for b in range(NB):
+                value = jnp.zeros((strip, L), F32)
+                if tile == 0 or edge:
+                    for e in range(TAPS):
+                        value = jnp.where(tap == e, col_taps[e, b], value)
+                rounded = value.astype(BF16)
+                rows, cols = slice(b * L + start, b * L + start + strip), slice(tile * L, (tile + 1) * L)
+                high[rows, cols] = rounded
+                low[rows, cols] = (value - rounded.astype(F32)).astype(BF16)
+
+
+def times(tap, row):
+    return (tap[None] * row.reshape(2, C // 2, L)).reshape(C, L)
+
+
+def filter_row(row_taps, b, terms):
+    total = None
+    for a, row in terms:
+        term = times(row_taps[a, b], row)
+        total = term if total is None else total + term
+    return total
+
+
+def back_project(vb, blocks, across, row_ids, col_ids, contrib, sums):
+    sums[...] = jnp.zeros(sums.shape, F32)
     for k in range(KDEV):
         contrib[k] = lax.dot_general(
-            vb[row_ids[k]], blocks[k], (((1,), (1,)), ((), ())), preferred_element_type=F32
-        )
-    sums[...] = jnp.zeros(sums.shape, F32)
+            vb[row_ids[k]], blocks[k], (((1,), (int(across),)), ((), ())), preferred_element_type=F32
+        )
     for k in range(KDEV):
         q = col_ids[k]
         sums[q] = sums[q] + contrib[k]
 
 
-def synth_rows(taps, b, rows, wide_h, wide_l):
+def turn_kernel(blocks, after, turned):
+    for k in range(KDEV):
+        turned[k] = blocks[k].T
+
+
+def synth_rows(row_taps, b, rows, wide):
     for i in range(RE):
-        total = None
-        for a in range(TAPS):
-            r = i - a
-            if 0 <= r < R:
-                term = taps[a, 0, b] * rows[r]
-                total = term if total is None else total + term
-        high = total.astype(BF16)
-        wide_h[i * C : (i + 1) * C, b * L : (b + 1) * L] = high
-        wide_l[i * C : (i + 1) * C, b * L : (b + 1) * L] = (total - high.astype(F32)).astype(BF16)
-
-
-def filter_columns(rows_h, rows_l, col_h, col_l):
-    return (
-        jnp.dot(rows_h, col_h[...], preferred_element_type=F32)
-        + jnp.dot(rows_l, col_h[...], preferred_element_type=F32)
-        + jnp.dot(rows_h, col_l[...], preferred_element_type=F32)
+        terms = [(a, rows[i - a]) for a in range(TAPS) if 0 <= i - a < R]
+        total = filter_row(row_taps, b, terms)
+        wide[i * C : (i + 1) * C, b * L : (b + 1) * L] = total.astype(BF16)
+
+
+def filter_columns(rows, col_h, col_l):
+    return jnp.dot(rows, col_h[...], preferred_element_type=F32) + jnp.dot(
+        rows, col_l[...], preferred_element_type=F32
     )
 
 
-def make_message(sums, wide_h, wide_l, col_h, col_l, smooth, msg):
+def make_message(sums, wide, col_h, col_l, smooth, msg):
     odd = is_odd("facet")
     tile_row = jnp.where(odd, 0, 2)
     top = pl.multiple_of(jnp.where(odd, 0, (R + W) * C), C)
-    smooth[...] = filter_columns(
-        wide_h[pl.ds(top, W * C), :], wide_l[pl.ds(top, W * C), :], col_h, col_l
-    )
-    spot = jnp.where(odd, R - W, 0)
+    smooth[...] = filter_columns(wide[pl.ds(top, W * C), :], col_h, col_l)
     for h in range(2):
         xs = swap_blocks([sums[tile_row * 8 + t, :, h * L : (h + 1) * L] for t in range(8)])
         for i in range(8):
@@ -130,8 +142,8 @@
     msg[R] = pack([smooth[i * C : (i + 1) * C, L:] for i in range(W)]).astype(BF16)
 
 
-def sums_kernel(sums, wide_h, wide_l, col_h, col_l, main, ext, smooth):
-    smooth[...] = filter_columns(wide_h[...], wide_l[...], col_h, col_l)
+def sums_kernel(sums, wide, col_h, col_l, main, ext, smooth):
+    smooth[...] = filter_columns(wide[...], col_h, col_l)
     for tr in range(3):
         for h in range(2):
             xs = swap_blocks([sums[tr * 8 + t, :, h * L : (h + 1) * L] for t in range(8)])
@@ -155,30 +167,39 @@
 
 def first_kernel(
     taps_hbm, rows_hbm, cols_hbm, u_hbm, v_hbm, blocks_hbm,
-    sums, wide_h, wide_l, msg, u_rows, col_h, col_l, blocks,
-    taps, row_ids, col_ids, u, v, vb, contrib, turned, smooth, sems,
+    sums, wide, msg, u_rows, col_h, col_l, blocks, row_taps,
+    row_ids, col_ids, taps, col_taps, u, v, vb, contrib, turned, smooth, sems,
 ):
-    get_taps, get_u, get_v, get_blocks, get_rows, get_cols = fetch(
-        (taps_hbm, u_hbm, v_hbm, blocks_hbm, rows_hbm, cols_hbm),
-        (taps, u, v, blocks, row_ids, col_ids),
+    get_u, get_taps, get_v, get_blocks, get_rows, get_cols = fetch(
+        (u_hbm, taps_hbm, v_hbm, blocks_hbm, rows_hbm, cols_hbm),
+        (u, taps, v, blocks, row_ids, col_ids),
         sems,
     )
     get_taps.wait()
-    build_columns(taps, col_h, col_l)
+    for a in range(TAPS):
+        for b in range(NB):
+            row_taps[a, b] = jnp.broadcast_to(taps[a, 0:1, b : b + 1], (C // 2, L))
+            col_taps[a, b] = jnp.broadcast_to(taps[a, 1:2, b : b + 1], (C // 2, L))
     get_u.wait()
     for b in range(NB):
         turned[b] = u[b].astype(F32)
+    build_columns(col_taps, col_h, col_l)
+
+    def wavelets(b):
         rows = [turned[b, pl.ds(r, C, stride=R), :] for r in range(R)]
         for r in range(R):
             u_rows[b, r * C : (r + 1) * C, :] = rows[r].astype(BF16)
-        synth_rows(taps, b, rows, wide_h, wide_l)
+        synth_rows(row_taps, b, rows, wide)
+
+    for b in range(NB):
+        wavelets(b)
     get_v.wait()
     get_rows.wait()
     get_cols.wait()
     get_blocks.wait()
     vb[...] = v[...].astype(BF16)
-    back_project(vb, blocks, row_ids, col_ids, contrib, sums)
-    make_message(sums, wide_h, wide_l, col_h, col_l, smooth, msg)
+    back_project(vb, blocks, True, row_ids, col_ids, contrib, sums)
+    make_message(sums, wide, col_h, col_l, smooth, msg)
 
 
 def pair_kernel(with_image, *refs):
@@ -210,7 +231,7 @@
 
 def rim_kernel(with_image, *refs):
     if with_image:
-        total, total_ext, main, ext, got, image, part, part_ext, msg_a, msg_b, x = refs
+        total, total_ext, main, ext, got, image, _, part, part_ext, msg_a, msg_b, x = refs
     else:
         total, total_ext, main, ext, got, part, part_ext, msg_a, msg_b = refs
     odd = is_odd("facet")
@@ -325,7 +346,7 @@
             image_out[c * R : (c + 1) * R, :] = turned[pl.ds(c, R, stride=C), :]
 
 
-def near_kernel(e, e_ext, col_h, col_l, flat, wide, edge):
+def near_kernel(e, e_ext, col_h, col_l, row_taps, flat, wide, edge, middle):
     odd = is_odd("facet")
     base_b = jnp.where(odd, 2, 0)
     for tile_row, base in ((1, 0), (base_b, R)):
@@ -339,6 +360,11 @@
     for i in range(W):
         edge[i * C : (i + 1) * C, :L] = e[start + i]
         edge[i * C : (i + 1) * C, L:] = e_ext[start + i]
+    for b in range(NB):
+        cols = slice(b * L, (b + 1) * L)
+        for r in range(W, R - W):
+            terms = [(a, wide[(r - W + a) * C : (r - W + a + 1) * C, cols]) for a in range(TAPS)]
+            middle[b, (r - W) * C : (r - W + 1) * C, :] = filter_row(row_taps, b, terms)
 
 
 def spread_columns(rows, col_h, col_l):
@@ -349,21 +375,38 @@
 
 
 def dual_kernel(last, *refs):
-    taps_hbm, rows_hbm, cols_hbm, radii_hbm = refs[:4]
-    flat_in, inner, edge, got, v, vis, blocks, u_rows, thr, col_h, col_l = refs[4:15]
-    refs = refs[15:]
+    flat_in, inner, edge, middle, got, v, vis, blocks, u_rows, thr, col_h, col_l = refs[:12]
+    row_taps, radii, rows_vmem, cols_vmem = refs[12:16]
+    refs = refs[16:]
     if last:
-        v_hbm, u_hbm, *refs = refs
+        image, image_hbm, v_hbm, u_hbm, *refs = refs
         v_out, u_out, turned, out_sems, *refs = refs
     else:
-        sums, wide_h, wide_l, msg, v_out, u_out, *refs = refs
+        blocks_turned, sums, wide_next, msg, v_out, u_out, *refs = refs
         vb, tiles, smooth, *refs = refs
-    taps, row_ids, col_ids, radii, sems, flat, wide, edges, contrib, totals = refs
-    get_rows, get_cols, get_radii, get_taps = fetch(
-        (rows_hbm, cols_hbm, radii_hbm, taps_hbm), (row_ids, col_ids, radii, taps), sems
-    )
+    row_ids, col_ids, sems, flat, wide, edges, contrib, totals = refs
+    get_rows, get_cols = fetch((rows_vmem, cols_vmem), (row_ids, col_ids), sems)
+    puts = []
+    if last:
+        put = pltpu.make_async_copy(image, image_hbm, out_sems.at[NB + 1])
+        put.start()
+        puts.append(put)
     odd = is_odd("facet")
     lane = lanes()
+    packed = got[R].astype(F32)
+    near_a = jnp.where(odd, R - W, 0)
+    above, below = edges.at[0], edges.at[1]
+    for i in range(W):
+        rows = slice(i * C, (i + 1) * C)
+        mine = edge[rows, :]
+        rim = jnp.where(odd, roll(packed, -8 * (R - W + i)), roll(packed, -8 * i))
+        theirs = jnp.concatenate(
+            [got[near_a + i], jnp.where(lane < 2 * W, rim, 0.0).astype(BF16)], axis=1
+        )
+        above[rows, :] = jnp.where(odd, theirs, mine)
+        below[rows, :] = jnp.where(odd, mine, theirs)
+    wide[: W * C, :] = spread_columns(above[...], col_h, col_l)
+    wide[W * C :, :] = spread_columns(below[...], col_h, col_l)
     tile_a = jnp.where(odd, 0, 2)
     tile_b = jnp.where(odd, 2, 0)
     for h in range(2):
@@ -373,45 +416,33 @@
     for t in range(8):
         flat[8 + t] = flat_in[8 + t]
         flat[tile_b * 8 + t] = flat_in[tile_b * 8 + t]
-    get_rows.wait()
-    get_cols.wait()
-    for k in range(KDEV):
-        contrib[k] = jnp.dot(flat[col_ids[k]], blocks[k], preferred_element_type=F32)
-    totals[...] = jnp.zeros(totals.shape, F32)
-    for k in range(KDEV):
-        r = row_ids[k]
-        totals[r] = totals[r] + contrib[k]
-    get_radii.wait()
-    for r in range(RB):
-        seen = vis[r]
-        moved = v[r] + 0.5 * totals[r]
-        offset = 2.0 * moved - seen
-        length = jnp.sqrt(jnp.sum(jnp.sum(offset * offset, axis=1, keepdims=True), axis=0, keepdims=True))
-        scale = radii[r] / jnp.maximum(length, radii[r])
-        new = moved - 0.5 * (seen + offset * scale)
-        v_out[r] = new
-        if not last:
-            vb[r] = new.astype(BF16)
-    if last:
-        put_v = pltpu.make_async_copy(v_out, v_hbm, out_sems.at[NB])
-        put_v.start()
-    packed = got[R].astype(F32)
-    near_a = jnp.where(odd, R - W, 0)
-    above, below = edges.at[0], edges.at[1]
-    for i in range(W):
-        rows = slice(i * C, (i + 1) * C)
-        mine = edge[rows, :]
-        theirs = jnp.concatenate(
-            [got[near_a + i].astype(F32), jnp.where(lane < 2 * W, jnp.where(odd, roll(packed, -8 * (R - W + i)), roll(packed, -8 * i)), 0.0)],
-            axis=1,
-        ).astype(BF16)
-        above[rows, :] = jnp.where(odd, theirs, mine)
-        below[rows, :] = jnp.where(odd, mine, theirs)
-    wide[: W * C, :] = spread_columns(above[...], col_h, col_l)
-    wide[W * C :, :] = spread_columns(below[...], col_h, col_l)
-    if not last:
-        back_project(vb, blocks, row_ids, col_ids, tiles, sums)
-    get_taps.wait()
+
+    def operators():
+        totals[...] = jnp.zeros(totals.shape, F32)
+        for k in range(KDEV):
+            contrib[k] = jnp.dot(flat[col_ids[k]], blocks[k], preferred_element_type=F32)
+        for k in range(KDEV):
+            r = row_ids[k]
+            totals[r] = totals[r] + contrib[k]
+        for r in range(RB):
+            seen = vis[r]
+            moved = v[r] + 0.5 * totals[r]
+            offset = 2.0 * moved - seen
+            length = jnp.sqrt(
+                jnp.sum(jnp.sum(offset * offset, axis=1, keepdims=True), axis=0, keepdims=True)
+            )
+            radius = radii[0:1, r : r + 1]
+            scale = radius / jnp.maximum(length, radius)
+            new = moved - 0.5 * (seen + offset * scale)
+            v_out[r] = new
+            if not last:
+                vb[r] = new.astype(BF16)
+        if last:
+            put = pltpu.make_async_copy(v_out, v_hbm, out_sems.at[NB])
+            put.start()
+            puts.append(put)
+        else:
+            back_project(vb, blocks_turned, False, row_ids, col_ids, tiles, sums)
 
     def filtered(t, b):
         cols = slice(b * L, (b + 1) * L)
@@ -421,38 +452,41 @@
             return inner[(t - W) * C : (t - W + 1) * C, cols]
         return wide[(t - R) * C : (t - R + 1) * C, cols]
 
-    puts = []
-    for b in range(NB):
-        rows = []
-        for r in range(R):
-            total = None
-            for a in range(TAPS):
-                term = taps[a, 0, b] * filtered(r + a, b)
-                total = term if total is None else total + term
-            full = u_rows[b, r * C : (r + 1) * C, :].astype(F32) + 0.5 * total
-            size = jnp.sqrt(jnp.sum(full * full, axis=0, keepdims=True))
-            limit = thr[b, r : r + 1, :]
-            new = full * (limit / jnp.maximum(size, limit))
+    def wavelets(bases):
+        for b in bases:
+            rows = []
+            for r in range(R):
+                if W <= r < R - W:
+                    total = middle[b, (r - W) * C : (r - W + 1) * C, :]
+                else:
+                    total = filter_row(row_taps, b, [(a, filtered(r + a, b)) for a in range(TAPS)])
+                full = u_rows[b, r * C : (r + 1) * C, :].astype(F32) + 0.5 * total
+                size = jnp.sqrt(jnp.sum(full * full, axis=0, keepdims=True))
+                limit = thr[b, r : r + 1, :]
+                new = full * (limit / jnp.maximum(size, limit))
+                if last:
+                    turned[b, r * C : (r + 1) * C, :] = new
+                else:
+                    new = new.astype(BF16)
+                    u_out[b, r * C : (r + 1) * C, :] = new
+                    rows.append(new.astype(F32))
             if last:
-                turned[b, r * C : (r + 1) * C, :] = new
+                for c in range(C):
+                    u_out[b, c * R : (c + 1) * R, :] = turned[b, pl.ds(c, R, stride=C), :].astype(BF16)
+                put = pltpu.make_async_copy(u_out.at[b], u_hbm.at[b], out_sems.at[b])
+                put.start()
+                puts.append(put)
             else:
-                new = new.astype(BF16)
-                u_out[b, r * C : (r + 1) * C, :] = new
-                rows.append(new.astype(F32))
-        if last:
-            for c in range(C):
-                u_out[b, c * R : (c + 1) * R, :] = turned[b, pl.ds(c, R, stride=C), :].astype(BF16)
-            put = pltpu.make_async_copy(u_out.at[b], u_hbm.at[b], out_sems.at[b])
-            put.start()
-            puts.append(put)
-        else:
-            synth_rows(taps, b, rows, wide_h, wide_l)
-    if last:
-        put_v.wait()
-        for put in puts:
-            put.wait()
-    else:
-        make_message(sums, wide_h, wide_l, col_h, col_l, smooth, msg)
+                synth_rows(row_taps, b, rows, wide_next)
+
+    wavelets(range(NB))
+    get_rows.wait()
+    get_cols.wait()
+    operators()
+    for put in puts:
+        put.wait()
+    if not last:
+        make_message(sums, wide_next, col_h, col_l, smooth, msg)
 
 
 def shape(dims, dtype=F32):
@@ -467,7 +501,7 @@
     return pltpu.SMEM(dims, dtype)
 
 
-HALF = [shape((NT3, C, VB)), shape((RE * C, NB * L), BF16), shape((RE * C, NB * L), BF16), shape((R + 1, C, L), BF16)]
+HALF = [shape((NT3, C, VB)), shape((RE * C, NB * L), BF16), shape((R + 1, C, L), BF16)]
 
 
 def call(kernel, far, arrays, outs, temps=(), name=None, mib=8, final=0):
@@ -501,12 +535,12 @@
     image_rows = image.reshape(C * R, L)
     u = wavelet_dual.reshape(NB, C * R, L)
     seen, v = visibilities[0, 0], data_dual[0, 0]
-    radii, row_ids, col_ids = ball_radii[0, 0], row_index[0, 0], col_index[0, 0]
+    radii, row_ids, col_ids = ball_radii[0], row_index[0, 0], col_index[0, 0]
     taps = filter_taps.transpose(2, 1, 0)
     facet_in, facet_out = pairs_of("facet")
     grp_in, grp_out = pairs_of("grp")
-    scalars = [small((TAPS, 2, NB), F32), small((KDEV,), jnp.int32), small((KDEV,), jnp.int32)]
-    sums, wide_h, wide_l, msg, u, col_h, col_l, operators = call(
+    scalars = [small((KDEV,), jnp.int32), small((KDEV,), jnp.int32)]
+    sums, wide_rows, msg, u, col_h, col_l, operators, row_taps = call(
         first_kernel,
         (taps, row_ids, col_ids, u, v, blocks[0, 0]),
         (),
@@ -516,9 +550,12 @@
             shape((NB * L, 2 * L), BF16),
             shape((NB * L, 2 * L), BF16),
             shape((KDEV, VB, VB), BF16),
+            shape((TAPS, NB, C // 2, L)),
         ],
         scalars
         + [
+            scratch(TAPS, 2, NB),
+            scratch(TAPS, NB, C // 2, L),
             scratch(NB, C * R, L, dtype=BF16),
             scratch(RB, C, VB),
             scratch(RB, C, VB, dtype=BF16),
@@ -537,7 +574,7 @@
         main, ext = call(
             sums_kernel,
             (),
-            (sums, wide_h, wide_l, col_h, col_l),
+            (sums, wide_rows, col_h, col_l),
             [shape((BAND, C, L)), shape((RE, C, L))],
             [scratch(RE * C, 2 * L)],
             name="sums",
@@ -554,11 +591,15 @@
             name="pair",
         )
         got = lax.ppermute(msg, "facet", facet_out)
+        if first:
+            (turned,) = call(
+                turn_kernel, (), (operators, total), [shape((KDEV, VB, VB), BF16)], name="turn", mib=4
+            )
         rim = shape((4 if first else 2, C, L), BF16)
         part, part_ext, msg_a, msg_b, *rest = call(
             lambda *refs: rim_kernel(first, *refs),
             (),
-            (total, total_ext, main, ext, got) + ((image_rows,) if first else ()),
+            (total, total_ext, main, ext, got) + ((image_rows, turned) if first else ()),
             [shape((2 * R, C, L)), shape((2 * R, C, L)), rim, rim]
             + ([shape((2 * R, C, L))] if first else []),
             name="rim",
@@ -583,33 +624,40 @@
         else:
             x, x_ext = results[:2]
         got = lax.ppermute(msg, "facet", facet_in)
-        flat, inner, edge = call(
+        flat, inner, edge, middle = call(
             near_kernel,
             (),
-            (e, e_ext, col_h, col_l),
-            [shape((NT3, C, VB), BF16), shape((R * C, NB * L)), shape((W * C, 2 * L), BF16)],
+            (e, e_ext, col_h, col_l, row_taps),
+            [
+                shape((NT3, C, VB), BF16),
+                shape((R * C, NB * L)),
+                shape((W * C, 2 * L), BF16),
+                shape((NB, (R - 2 * W) * C, L)),
+            ],
             name="near",
         )
         outs = [shape((RB, C, VB)), shape((NB, R * C, L), BF16)]
         if last:
+            outs = [shape((C * R, L))] + outs
             temps = [
                 scratch(RB, C, VB),
                 scratch(NB, C * R, L, dtype=BF16),
                 scratch(NB, R * C, L),
-                pltpu.SemaphoreType.DMA((NB + 1,)),
+                pltpu.SemaphoreType.DMA((NB + 2,)),
             ]
         else:
             temps = [scratch(RB, C, VB, dtype=BF16), scratch(KDEV, C, VB), scratch(W * C, 2 * L)]
         *half, v, u = call(
             lambda *refs: dual_kernel(last, *refs),
-            (taps, row_ids, col_ids, radii),
-            (flat, inner, edge, got, v, seen, operators, u, thresholds, col_h, col_l),
+            (),
+            (flat, inner, edge, middle, got, v, seen, operators, u, thresholds, col_h, col_l)
+            + (row_taps, radii, row_ids, col_ids)
+            + ((image_out,) if last else (turned,)),
             ([] if last else HALF) + outs,
             temps
             + scalars
             + [
-                small((RB,), F32),
-                pltpu.SemaphoreType.DMA((4,)),
+                pltpu.SemaphoreType.DMA((2,)),
                 scratch(NT3, C, VB, dtype=BF16),
                 scratch(2 * W * C, NB * L),
                 scratch(2, W * C, 2 * L, dtype=BF16),
@@ -618,10 +666,12 @@
             ],
             name="dual",
             mib=16,
-            final=2 if last else 0,
-        )
-        if not last:
-            sums, wide_h, wide_l, msg = half
+            final=3 if last else 0,
+        )
+        if last:
+            (image_out,) = half
+        else:
+            sums, wide_rows, msg = half
     return (image_out.reshape(C, R, L), v[None, None], u.reshape(NB, C, R, L))
 
 

time: 61.4 us -> 58.8 us (0.958)
  Pallas kernels: 16.3 us -> 15.2 us
  local copies, waits for them, and re-layouts: 0.68 us -> 0.03 us
    pallas_call x13 -> x14, Pallas kernels: 16.3 us -> 15.2 us  [call(): pl.pallas_call(kernel, out_shape=tuple(((pltpu.HBM if i < final else pltp...]
    unnamed x9 -> x14, local copies, waits for them, and re-layouts: 0.68 us -> 0.03 us
  transfers between devices with their start and end apart: 10 -> 10, of which waited for: 7 -> 8; matrix products, arithmetic and copies ran while one was open for 1% -> 0% of each run, Pallas kernels for 4% -> 6%
where the time goes in v2:
time: 58.8 us; the launch traced here: 58.6 us
  starting transfers between devices  28.1 us (48%)
  Pallas kernels  15.2 us (26%)
  waiting for transfers between devices  14.4 us (24%)
  between operations  0.82 us (1%)
    ppermute x4, starting transfers between devices, per_device(): got = lax.ppermute(msg, 'facet', facet_in)  15.6 us
    pallas_call x14, Pallas kernels, call(): pl.pallas_call(kernel, out_shape=tuple(((pltpu.HBM if i < final else pltp...  15.2 us
    ppermute x2, waiting for transfers between devices, per_device(): got = lax.ppermute(msg, 'facet', facet_out)  7.48 us
    ppermute x2, waiting for transfers between devices, per_device(): got_b = lax.ppermute(msg_b, 'grp', grp_out)  6.11 us
    ppermute x2, starting transfers between devices, per_device(): got = lax.ppermute(msg, 'facet', facet_out)  5.36 us
    ppermute x2, starting transfers between devices, per_device(): got_b = lax.ppermute(msg_b, 'grp', grp_out)  4.5 us
    ppermute x2, starting transfers between devices, per_device(): got_a = lax.ppermute(msg_a, 'grp', grp_in)  2.63 us
  transfers between devices with their start and end apart: 10, of which 8 were waited for; matrix products, arithmetic and copies ran while one was open for 0% of the time, Pallas kernels for 6%

profile of v2, /device:TPU:131, one launch (start us, length us, event | category | flops | bytes accessed | tf_op | source)
XLA Modules:
  0.0 58.6 jit_solution(15492655388202293193)
XLA Ops:
  0.6 0.0 copy-start.2
  0.6 3.4 %first.1 = (f32[24,16,256]{2,1,0:T(8,128)S(1)}, bf16[352,1024]{1,0:T(8,128)(2,1)S(1)}, bf16[17,16,128]{2,1,0:T(8,128)(2,1)S(1)}, bf16[8,256,128]{2,1,0:T(8,128)(...) custom-call(f32[7,2,8]{2,1,0:T(2,128)} %bitcast.28, ...), custom_call_target="tpu_custom_call" | custom-call | tf_op jit(solution)/shard_map/first/pallas_call | solution.py:511
  4.1 0.8 %collective-permute-start = (bf16[17,16,128]{2,1,0:T(8,128)(2,1)S(1)}, bf16[17,16,128]{2,1,0:T(8,128)(2,1)S(1)}, u32[]{:S(2)}, u32[]{:S(2)}) collective-permute-start(bf16[17,16,128]{2,1,0:T(8,128)(2,1)S(1)} %get-tuple-element.61), channel_id=1, source_target_pairs={{0,1},{1,0},{2,3},{3,2},{4,5},{5,4},{6,7},{7,6},{8,9},{9,8},{10,11... | collective-permute-start | bytes 208904 | tf_op jit(solution)/shard_map/ppermute | solution.py:573
  4.8 0.7 %sums.2 = (f32[48,16,128]{2,1,0:T(8,128)S(1)}, f32[22,16,128]{2,1,0:T(8,128)S(1)}) custom-call(f32[24,16,256]{2,1,0:T(8,128)S(1)} %get-tuple-element.55.sums, bf16[352,1024]{1,0:T(8,128)(2,1)S(1)} %get-tuple-element.56.wide, bf16[1024,256]{1,0:T(8,128)(2,1)S(1)} %get-tuple-element.57.col_h.refs_10_, bf16[1024,256]{1,0:T(8,128)(2,1)S(1)} %get-tuple-element.58.col_l.refs_11_), custom_call_target="tpu_custom_call" | custom-call | tf_op jit(solution)/shard_map/sums/pallas_call | solution.py:511
  5.5 0.2 collective-permute-done.refs_2_
  5.7 0.0 copy-done.2
  5.7 0.2 pair.2
  5.9 3.4 %collective-permute-start.1 = (bf16[50,16,128]{2,1,0:T(8,128)(2,1)S(1)}, bf16[50,16,128]{2,1,0:T(8,128)(2,1)S(1)}, u32[]{:S(2)}, u32[]{:S(2)}) collective-permute-start(bf16[50,16,128]{2,1,0:T(8,128)(2,1)S(1)} %get-tuple-element.64), channel_id=1, source_target_pairs={{1,2},{2,1},{3,4},{4,3},{5,6},{6,5},{7,8},{8,7},{9,10},{10,9},{11,... | collective-permute-start | bytes 614408 | tf_op jit(solution)/shard_map/ppermute | solution.py:593
  9.4 0.6 %turn.1.refs_6_.refs_16_ = bf16[16,256,256]{2,1,0:T(8,128)(2,1)S(1)} custom-call(bf16[16,256,256]{2,1,0:T(8,128)(2,1)S(1)} %get-tuple-element.65.blocks.refs_7_, f32[16,16,128]{2,1,0:T(8,128)S(1)} %get-tuple-element.62.after.refs_0_), custom_call_target="tpu_custom_call" | custom-call | tf_op jit(solution)/shard_map/turn/pallas_call | solution.py:511
  10.0 3.0 %collective-permute-done.1.refs_4_ = bf16[50,16,128]{2,1,0:T(8,128)(2,1)S(1)} collective-permute-done((bf16[50,16,128]{2,1,0:T(8,128)(2,1)S(1)}, bf16[50,16,128]{2,1,0:T(8,128)(2,1)S(1)}, u32[]{:S(2)}, u32[]{:S(2)}) %collective-permute-start.1) | collective-permute-done | bytes 204832 | tf_op jit(solution)/shard_map/ppermute | solution.py:593
  13.0 0.0 copy-start
  13.0 0.0 copy-start.1
  13.0 0.0 copy-start.3
  13.0 0.0 copy-start.4
  13.0 0.0 copy-start.5
  13.0 0.0 copy-start.6
  13.0 0.4 rim.2
  13.4 0.8 %collective-permute-start.2 = (bf16[4,16,128]{2,1,0:T(8,128)(2,1)S(1)}, bf16[4,16,128]{2,1,0:T(8,128)(2,1)S(1)}, u32[]{:S(2)}, u32[]{:S(2)}) collective-permute-start(bf16[4,16,128]{2,1,0:T(8,128)(2,1)S(1)} %get-tuple-element.68), channel_id=1, source_target_pairs={{0,32},{32,0},{64,96},{96,64},{128,160},{160,128},{192,224},{224,1... | collective-permute-start | bytes 49160 | tf_op jit(solution)/shard_map/ppermute | solution.py:609
  14.2 2.6 %collective-permute-start.3 = (bf16[4,16,128]{2,1,0:T(8,128)(2,1)S(1)}, bf16[4,16,128]{2,1,0:T(8,128)(2,1)S(1)}, u32[]{:S(2)}, u32[]{:S(2)}) collective-permute-start(bf16[4,16,128]{2,1,0:T(8,128)(2,1)S(1)} %get-tuple-element.69), channel_id=1, source_target_pairs={{32,64},{64,32},{96,128},{128,96},{160,192},{192,160},{33,65},{65,... | collective-permute-start | bytes 49160 | tf_op jit(solution)/shard_map/ppermute | solution.py:610
  16.8 0.0 collective-permute-done.2.refs_2_
  16.8 2.8 %collective-permute-done.3.refs_3_ = bf16[4,16,128]{2,1,0:T(8,128)(2,1)S(1)} collective-permute-done((bf16[4,16,128]{2,1,0:T(8,128)(2,1)S(1)}, bf16[4,16,128]{2,1,0:T(8,128)(2,1)S(1)}, u32[]{:S(2)}, u32[]{:S(2)}) %collective-permute-start.3) | collective-permute-done | bytes 16416 | tf_op jit(solution)/shard_map/ppermute | solution.py:610
  19.6 0.3 primal.2
  19.9 7.4 %collective-permute-start.4 = (bf16[17,16,128]{2,1,0:T(8,128)(2,1)S(1)}, bf16[17,16,128]{2,1,0:T(8,128)(2,1)S(1)}, u32[]{:S(2)}, u32[]{:S(2)}) collective-permute-start(bf16[17,16,128]{2,1,0:T(8,128)(2,1)S(1)} %get-tuple-element.78), channel_id=1, source_target_pairs={{0,1},{1,0},{2,3},{3,2},{4,5},{5,4},{6,7},{7,6},{8,9},{9,8},{10,11... | collective-permute-start | bytes 208904 | tf_op jit(solution)/shard_map/ppermute | solution.py:626
  27.3 0.7 %near.2 = (bf16[24,16,256]{2,1,0:T(8,128)(2,1)S(1)}, f32[256,1024]{1,0:T(8,128)S(1)}, bf16[48,256]{1,0:T(8,128)(2,1)S(1)}, f32[8,160,128]{2,1,0:T(8,128)S(1)}) custom-call(bf16[32,16,128]{2,1,0:T(8,128)(2,1)S(1)} %get-tuple-element.71.e, bf16[32,16,128]{2,1,0:T(8,128)(2,1)S(1)} %get-tuple-element.72.e_ext, ...), custom_call_target="tpu_custom_call" | custom-call | tf_op jit(solution)/shard_map/near/pallas_call | solution.py:511
  28.0 0.2 collective-permute-done.4.refs_4_
  28.2 0.0 copy-done
  28.2 0.0 copy-done.1
  28.2 0.0 copy-done.3
  28.2 0.0 copy-done.4
  28.2 0.0 copy-done.5
  28.2 0.0 copy-done.6
  28.2 3.4 %dual.2 = (f32[24,16,256]{2,1,0:T(8,128)S(1)}, bf16[352,1024]{1,0:T(8,128)(2,1)S(1)}, bf16[17,16,128]{2,1,0:T(8,128)(2,1)S(1)}, f32[8,16,256]{2,1,0:T(8,128)S(1)}, bf16[8,256,128]{2,1,0:T(8,128)(2,1)S(1)}) custom-call(bf16[24,16,256]{2,1,0:T(8,128)(2,1)S(1)} %get-tuple-element.74.refs_0_, f32[256,1024]{1,0:T(8,128)S(1)} %get-tuple-element.75.refs_1_, ...), custom_call_target="tpu_custom_call" | custom-call | tf_op jit(solution)/shard_map/dual/pallas_call | solution.py:511
  31.7 0.4 collective-permute-start.5
  32.1 0.7 %sums.3 = (f32[48,16,128]{2,1,0:T(8,128)S(1)}, f32[22,16,128]{2,1,0:T(8,128)S(1)}) custom-call(f32[24,16,256]{2,1,0:T(8,128)S(1)} %get-tuple-element.80.sums, bf16[352,1024]{1,0:T(8,128)(2,1)S(1)} %get-tuple-element.81.wide, bf16[1024,256]{1,0:T(8,128)(2,1)S(1)} %get-tuple-element.57.col_h.refs_10_, bf16[1024,256]{1,0:T(8,128)(2,1)S(1)} %get-tuple-element.58.col_l.refs_11_), custom_call_target="tpu_custom_call" | custom-call | tf_op jit(solution)/shard_map/sums/pallas_call | solution.py:511
  32.8 0.2 collective-permute-done.5.refs_2_
  33.0 0.2 pair.3
  33.2 1.9 %collective-permute-start.6 = (bf16[34,16,128]{2,1,0:T(8,128)(2,1)S(1)}, bf16[34,16,128]{2,1,0:T(8,128)(2,1)S(1)}, u32[]{:S(2)}, u32[]{:S(2)}) collective-permute-start(bf16[34,16,128]{2,1,0:T(8,128)(2,1)S(1)} %get-tuple-element.87), channel_id=1, source_target_pairs={{1,2},{2,1},{3,4},{4,3},{5,6},{6,5},{7,8},{8,7},{9,10},{10,9},{11,... | collective-permute-start | bytes 417800 | tf_op jit(solution)/shard_map/ppermute | solution.py:593
  35.1 4.4 %collective-permute-done.6.refs_4_ = bf16[34,16,128]{2,1,0:T(8,128)(2,1)S(1)} collective-permute-done((bf16[34,16,128]{2,1,0:T(8,128)(2,1)S(1)}, bf16[34,16,128]{2,1,0:T(8,128)(2,1)S(1)}, u32[]{:S(2)}, u32[]{:S(2)}) %collective-permute-start.6) | collective-permute-done | bytes 139296 | tf_op jit(solution)/shard_map/ppermute | solution.py:593
  39.6 0.3 rim.3
  39.9 1.8 %collective-permute-start.7 = (bf16[2,16,128]{2,1,0:T(8,128)(2,1)S(1)}, bf16[2,16,128]{2,1,0:T(8,128)(2,1)S(1)}, u32[]{:S(2)}, u32[]{:S(2)}) collective-permute-start(bf16[2,16,128]{2,1,0:T(8,128)(2,1)S(1)} %get-tuple-element.90), channel_id=1, source_target_pairs={{0,32},{32,0},{64,96},{96,64},{128,160},{160,128},{192,224},{224,1... | collective-permute-start | bytes 24584 | tf_op jit(solution)/shard_map/ppermute | solution.py:609
  41.7 1.9 %collective-permute-start.8 = (bf16[2,16,128]{2,1,0:T(8,128)(2,1)S(1)}, bf16[2,16,128]{2,1,0:T(8,128)(2,1)S(1)}, u32[]{:S(2)}, u32[]{:S(2)}) collective-permute-start(bf16[2,16,128]{2,1,0:T(8,128)(2,1)S(1)} %get-tuple-element.91), channel_id=1, source_target_pairs={{32,64},{64,32},{96,128},{128,96},{160,192},{192,160},{33,65},{65,... | collective-permute-start | bytes 24584 | tf_op jit(solution)/shard_map/ppermute | solution.py:610
  43.6 0.0 collective-permute-done.7.refs_2_
  43.6 3.4 %collective-permute-done.8.refs_3_ = bf16[2,16,128]{2,1,0:T(8,128)(2,1)S(1)} collective-permute-done((bf16[2,16,128]{2,1,0:T(8,128)(2,1)S(1)}, bf16[2,16,128]{2,1,0:T(8,128)(2,1)S(1)}, u32[]{:S(2)}, u32[]{:S(2)}) %collective-permute-start.8) | collective-permute-done | bytes 8224 | tf_op jit(solution)/shard_map/ppermute | solution.py:610
  46.9 0.3 primal.3
  47.3 7.0 %collective-permute-start.9 = (bf16[17,16,128]{2,1,0:T(8,128)(2,1)S(1)}, bf16[17,16,128]{2,1,0:T(8,128)(2,1)S(1)}, u32[]{:S(2)}, u32[]{:S(2)}) collective-permute-start(bf16[17,16,128]{2,1,0:T(8,128)(2,1)S(1)} %get-tuple-element.100), channel_id=1, source_target_pairs={{0,1},{1,0},{2,3},{3,2},{4,5},{5,4},{6,7},{7,6},{8,9},{9,8},{10,11... | collective-permute-start | bytes 208904 | tf_op jit(solution)/shard_map/ppermute | solution.py:626
  54.3 0.7 %near.3 = (bf16[24,16,256]{2,1,0:T(8,128)(2,1)S(1)}, f32[256,1024]{1,0:T(8,128)S(1)}, bf16[48,256]{1,0:T(8,128)(2,1)S(1)}, f32[8,160,128]{2,1,0:T(8,128)S(1)}) custom-call(bf16[32,16,128]{2,1,0:T(8,128)(2,1)S(1)} %get-tuple-element.94.e, bf16[32,16,128]{2,1,0:T(8,128)(2,1)S(1)} %get-tuple-element.95.e_ext, ...), custom_call_target="tpu_custom_call" | custom-call | tf_op jit(solution)/shard_map/near/pallas_call | solution.py:511
  55.0 0.2 collective-permute-done.9.refs_4_
  55.2 3.3 %dual.3 = (f32[256,128]{1,0:T(8,128)}, f32[8,16,256]{2,1,0:T(8,128)}, bf16[8,256,128]{2,1,0:T(8,128)(2,1)}) custom-call(bf16[24,16,256]{2,1,0:T(8,128)(2,1)S(1)} %get-tuple-element.96.refs_0_, f32[256,1024]{1,0:T(8,128)S(1)} %get-tuple-element.97.refs_1_, bf16[48,256]{1,0:T(8,128)(2,1)S(1)} %get-tuple-element.98.refs_2_, ...), custom_call_target="tpu_custom_call" | custom-call | tf_op jit(solution)/shard_map/dual/pallas_call | solution.py:511
Async XLA Ops:
  0.6 5.1 %copy-start.2 = (f32[16,16,128]{2,1,0:T(8,128)S(1)}, f32[16,16,128]{2,1,0:T(8,128)}, u32[]{:S(2)}) copy-start(f32[16,16,128]{2,1,0:T(8,128)} %param.10) | copy-start | bytes 393220
  4.1 1.7 %collective-permute-start = (bf16[17,16,128]{2,1,0:T(8,128)(2,1)S(1)}, bf16[17,16,128]{2,1,0:T(8,128)(2,1)S(1)}, u32[]{:S(2)}, u32[]{:S(2)}) collective-permute-start(bf16[17,16,128]{2,1,0:T(8,128)(2,1)S(1)} %get-tuple-element.61), channel_id=1, source_target_pairs={{0,1},{1,0},{2,3},{3,2},{4,5},{5,4},{6,7},{7,6},{8,9},{9,8},{10,11... | collective-permute-start | bytes 208904 | tf_op jit(solution)/shard_map/ppermute | solution.py:573
  5.9 7.1 %collective-permute-start.1 = (bf16[50,16,128]{2,1,0:T(8,128)(2,1)S(1)}, bf16[50,16,128]{2,1,0:T(8,128)(2,1)S(1)}, u32[]{:S(2)}, u32[]{:S(2)}) collective-permute-start(bf16[50,16,128]{2,1,0:T(8,128)(2,1)S(1)} %get-tuple-element.64), channel_id=1, source_target_pairs={{1,2},{2,1},{3,4},{4,3},{5,6},{6,5},{7,8},{8,7},{9,10},{10,9},{11,... | collective-permute-start | bytes 614408 | tf_op jit(solution)/shard_map/ppermute | solution.py:593
  13.0 15.2 %copy-start = (f32[1,1,8,16,256]{4,3,2,1,0:T(8,128)S(1)}, f32[1,1,8,16,256]{4,3,2,1,0:T(8,128)}, u32[]{:S(2)}) copy-start(f32[1,1,8,16,256]{4,3,2,1,0:T(8,128)} %param.14) | copy-start | bytes 393220
  13.0 15.2 %copy-start.1 = (f32[1,1,8,16,256]{4,3,2,1,0:T(8,128)S(1)}, f32[1,1,8,16,256]{4,3,2,1,0:T(8,128)}, u32[]{:S(2)}) copy-start(f32[1,1,8,16,256]{4,3,2,1,0:T(8,128)} %param.15) | copy-start | bytes 393220
  13.0 15.2 %copy-start.3 = (f32[8,16,128]{2,1,0:T(8,128)S(1)}, f32[8,16,128]{2,1,0:T(8,128)}, u32[]{:S(2)}) copy-start(f32[8,16,128]{2,1,0:T(8,128)} %refs_9_.3) | copy-start | bytes 196612
  13.0 15.2 %copy-start.4 = (s32[1,1,16]{2,1,0:T(1,128)S(1)}, s32[1,1,16]{2,1,0:T(1,128)}, u32[]{:S(2)}) copy-start(s32[1,1,16]{2,1,0:T(1,128)} %param.18) | copy-start | bytes 196
  13.0 15.2 %copy-start.5 = (s32[1,1,16]{2,1,0:T(1,128)S(1)}, s32[1,1,16]{2,1,0:T(1,128)}, u32[]{:S(2)}) copy-start(s32[1,1,16]{2,1,0:T(1,128)} %param.19) | copy-start | bytes 196
  13.0 15.2 %copy-start.6 = (f32[1,1,8]{2,1,0:T(1,128)S(1)}, f32[1,1,8]{2,1,0:T(1,128)}, u32[]{:S(2)}) copy-start(f32[1,1,8]{2,1,0:T(1,128)} %param.16) | copy-start | bytes 100
  13.4 3.4 %collective-permute-start.2 = (bf16[4,16,128]{2,1,0:T(8,128)(2,1)S(1)}, bf16[4,16,128]{2,1,0:T(8,128)(2,1)S(1)}, u32[]{:S(2)}, u32[]{:S(2)}) collective-permute-start(bf16[4,16,128]{2,1,0:T(8,128)(2,1)S(1)} %get-tuple-element.68), channel_id=1, source_target_pairs={{0,32},{32,0},{64,96},{96,64},{128,160},{160,128},{192,224},{224,1... | collective-permute-start | bytes 49160 | tf_op jit(solution)/shard_map/ppermute | solution.py:609
  14.2 5.4 %collective-permute-start.3 = (bf16[4,16,128]{2,1,0:T(8,128)(2,1)S(1)}, bf16[4,16,128]{2,1,0:T(8,128)(2,1)S(1)}, u32[]{:S(2)}, u32[]{:S(2)}) collective-permute-start(bf16[4,16,128]{2,1,0:T(8,128)(2,1)S(1)} %get-tuple-element.69), channel_id=1, source_target_pairs={{32,64},{64,32},{96,128},{128,96},{160,192},{192,160},{33,65},{65,... | collective-permute-start | bytes 49160 | tf_op jit(solution)/shard_map/ppermute | solution.py:610
  19.9 8.3 %collective-permute-start.4 = (bf16[17,16,128]{2,1,0:T(8,128)(2,1)S(1)}, bf16[17,16,128]{2,1,0:T(8,128)(2,1)S(1)}, u32[]{:S(2)}, u32[]{:S(2)}) collective-permute-start(bf16[17,16,128]{2,1,0:T(8,128)(2,1)S(1)} %get-tuple-element.78), channel_id=1, source_target_pairs={{0,1},{1,0},{2,3},{3,2},{4,5},{5,4},{6,7},{7,6},{8,9},{9,8},{10,11... | collective-permute-start | bytes 208904 | tf_op jit(solution)/shard_map/ppermute | solution.py:626
  31.7 1.4 %collective-permute-start.5 = (bf16[17,16,128]{2,1,0:T(8,128)(2,1)S(1)}, bf16[17,16,128]{2,1,0:T(8,128)(2,1)S(1)}, u32[]{:S(2)}, u32[]{:S(2)}) collective-permute-start(bf16[17,16,128]{2,1,0:T(8,128)(2,1)S(1)} %get-tuple-element.84), channel_id=1, source_target_pairs={{0,1},{1,0},{2,3},{3,2},{4,5},{5,4},{6,7},{7,6},{8,9},{9,8},{10,11... | collective-permute-start | bytes 208904 | tf_op jit(solution)/shard_map/ppermute | solution.py:573
  33.2 6.4 %collective-permute-start.6 = (bf16[34,16,128]{2,1,0:T(8,128)(2,1)S(1)}, bf16[34,16,128]{2,1,0:T(8,128)(2,1)S(1)}, u32[]{:S(2)}, u32[]{:S(2)}) collective-permute-start(bf16[34,16,128]{2,1,0:T(8,128)(2,1)S(1)} %get-tuple-element.87), channel_id=1, source_target_pairs={{1,2},{2,1},{3,4},{4,3},{5,6},{6,5},{7,8},{8,7},{9,10},{10,9},{11,... | collective-permute-start | bytes 417800 | tf_op jit(solution)/shard_map/ppermute | solution.py:593
  39.9 3.7 %collective-permute-start.7 = (bf16[2,16,128]{2,1,0:T(8,128)(2,1)S(1)}, bf16[2,16,128]{2,1,0:T(8,128)(2,1)S(1)}, u32[]{:S(2)}, u32[]{:S(2)}) collective-permute-start(bf16[2,16,128]{2,1,0:T(8,128)(2,1)S(1)} %get-tuple-element.90), channel_id=1, source_target_pairs={{0,32},{32,0},{64,96},{96,64},{128,160},{160,128},{192,224},{224,1... | collective-permute-start | bytes 24584 | tf_op jit(solution)/shard_map/ppermute | solution.py:609
  41.7 5.3 %collective-permute-start.8 = (bf16[2,16,128]{2,1,0:T(8,128)(2,1)S(1)}, bf16[2,16,128]{2,1,0:T(8,128)(2,1)S(1)}, u32[]{:S(2)}, u32[]{:S(2)}) collective-permute-start(bf16[2,16,128]{2,1,0:T(8,128)(2,1)S(1)} %get-tuple-element.91), channel_id=1, source_target_pairs={{32,64},{64,32},{96,128},{128,96},{160,192},{192,160},{33,65},{65,... | collective-permute-start | bytes 24584 | tf_op jit(solution)/shard_map/ppermute | solution.py:610
  47.3 8.0 %collective-permute-start.9 = (bf16[17,16,128]{2,1,0:T(8,128)(2,1)S(1)}, bf16[17,16,128]{2,1,0:T(8,128)(2,1)S(1)}, u32[]{:S(2)}, u32[]{:S(2)}) collective-permute-start(bf16[17,16,128]{2,1,0:T(8,128)(2,1)S(1)} %get-tuple-element.100), channel_id=1, source_target_pairs={{0,1},{1,0},{2,3},{3,2},{4,5},{5,4},{6,7},{7,6},{8,9},{9,8},{10,11... | collective-permute-start | bytes 208904 | tf_op jit(solution)/shard_map/ppermute | solution.py:626

commit v3 on v2

--- a/solution.py
+++ b/solution.py
@@ -110,24 +110,33 @@
         turned[k] = blocks[k].T
 
 
-def synth_rows(row_taps, b, rows, wide):
-    for i in range(RE):
+def synth_rows(row_taps, b, rows, places, wide_h, wide_l):
+    for spot, i in enumerate(places):
         terms = [(a, rows[i - a]) for a in range(TAPS) if 0 <= i - a < R]
         total = filter_row(row_taps, b, terms)
-        wide[i * C : (i + 1) * C, b * L : (b + 1) * L] = total.astype(BF16)
-
-
-def filter_columns(rows, col_h, col_l):
-    return jnp.dot(rows, col_h[...], preferred_element_type=F32) + jnp.dot(
-        rows, col_l[...], preferred_element_type=F32
+        high = total.astype(BF16)
+        wide_h[spot * C : (spot + 1) * C, b * L : (b + 1) * L] = high
+        wide_l[spot * C : (spot + 1) * C, b * L : (b + 1) * L] = (total - high.astype(F32)).astype(BF16)
+
+
+OUTER = tuple(range(W)) + tuple(range(R + W, RE))
+
+
+def filter_columns(rows_h, rows_l, col_h, col_l):
+    return (
+        jnp.dot(rows_h, col_h[...], preferred_element_type=F32)
+        + jnp.dot(rows_l, col_h[...], preferred_element_type=F32)
+        + jnp.dot(rows_h, col_l[...], preferred_element_type=F32)
     )
 
 
-def make_message(sums, wide, col_h, col_l, smooth, msg):
+def make_message(sums, wide_h, wide_l, col_h, col_l, smooth, msg):
     odd = is_odd("facet")
     tile_row = jnp.where(odd, 0, 2)
-    top = pl.multiple_of(jnp.where(odd, 0, (R + W) * C), C)
-    smooth[...] = filter_columns(wide[pl.ds(top, W * C), :], col_h, col_l)
+    top = pl.multiple_of(jnp.where(odd, 0, W * C), C)
+    smooth[...] = filter_columns(
+        wide_h[pl.ds(top, W * C), :], wide_l[pl.ds(top, W * C), :], col_h, col_l
+    )
     for h in range(2):
         xs = swap_blocks([sums[tile_row * 8 + t, :, h * L : (h + 1) * L] for t in range(8)])
         for i in range(8):
@@ -142,8 +151,11 @@
     msg[R] = pack([smooth[i * C : (i + 1) * C, L:] for i in range(W)]).astype(BF16)
 
 
-def sums_kernel(sums, wide, col_h, col_l, main, ext, smooth):
-    smooth[...] = filter_columns(wide[...], col_h, col_l)
+def sums_kernel(sums, u_rows, row_taps, col_h, col_l, main, ext, smooth, wide_h, wide_l):
+    for b in range(NB):
+        rows = [u_rows[b, r * C : (r + 1) * C, :].astype(F32) for r in range(R)]
+        synth_rows(row_taps, b, rows, range(RE), wide_h, wide_l)
+    smooth[...] = filter_columns(wide_h[...], wide_l[...], col_h, col_l)
     for tr in range(3):
         for h in range(2):
             xs = swap_blocks([sums[tr * 8 + t, :, h * L : (h + 1) * L] for t in range(8)])
@@ -167,8 +179,8 @@
 
 def first_kernel(
     taps_hbm, rows_hbm, cols_hbm, u_hbm, v_hbm, blocks_hbm,
-    sums, wide, msg, u_rows, col_h, col_l, blocks, row_taps,
-    row_ids, col_ids, taps, col_taps, u, v, vb, contrib, turned, smooth, sems,
+    sums, msg, u_rows, col_h, col_l, blocks, row_taps,
+    row_ids, col_ids, taps, col_taps, u, v, vb, contrib, turned, smooth, wide_h, wide_l, sems,
 ):
     get_u, get_taps, get_v, get_blocks, get_rows, get_cols = fetch(
         (u_hbm, taps_hbm, v_hbm, blocks_hbm, rows_hbm, cols_hbm),
@@ -189,7 +201,7 @@
         rows = [turned[b, pl.ds(r, C, stride=R), :] for r in range(R)]
         for r in range(R):
             u_rows[b, r * C : (r + 1) * C, :] = rows[r].astype(BF16)
-        synth_rows(row_taps, b, rows, wide)
+        synth_rows(row_taps, b, rows, OUTER, wide_h, wide_l)
 
     for b in range(NB):
         wavelets(b)
@@ -199,7 +211,7 @@
     get_blocks.wait()
     vb[...] = v[...].astype(BF16)
     back_project(vb, blocks, True, row_ids, col_ids, contrib, sums)
-    make_message(sums, wide, col_h, col_l, smooth, msg)
+    make_message(sums, wide_h, wide_l, col_h, col_l, smooth, msg)
 
 
 def pair_kernel(with_image, *refs):
@@ -346,7 +358,13 @@
             image_out[c * R : (c + 1) * R, :] = turned[pl.ds(c, R, stride=C), :]
 
 
-def near_kernel(e, e_ext, col_h, col_l, row_taps, flat, wide, edge, middle):
+def shrunk(u_row, coefficient, limit):
+    full = u_row.astype(F32) + 0.5 * coefficient
+    size = jnp.sqrt(jnp.sum(full * full, axis=0, keepdims=True))
+    return full * (limit / jnp.maximum(size, limit))
+
+
+def near_kernel(e, e_ext, col_h, col_l, row_taps, u_rows, thr, flat, wide, edge, middle):
     odd = is_odd("facet")
     base_b = jnp.where(odd, 2, 0)
     for tile_row, base in ((1, 0), (base_b, R)):
@@ -364,7 +382,10 @@
         cols = slice(b * L, (b + 1) * L)
         for r in range(W, R - W):
             terms = [(a, wide[(r - W + a) * C : (r - W + a + 1) * C, cols]) for a in range(TAPS)]
-            middle[b, (r - W) * C : (r - W + 1) * C, :] = filter_row(row_taps, b, terms)
+            new = shrunk(
+                u_rows[b, r * C : (r + 1) * C, :], filter_row(row_taps, b, terms), thr[b, r : r + 1, :]
+            )
+            middle[b, (r - W) * C : (r - W + 1) * C, :] = new.astype(BF16)
 
 
 def spread_columns(rows, col_h, col_l):
@@ -382,8 +403,8 @@
         image, image_hbm, v_hbm, u_hbm, *refs = refs
         v_out, u_out, turned, out_sems, *refs = refs
     else:
-        blocks_turned, sums, wide_next, msg, v_out, u_out, *refs = refs
-        vb, tiles, smooth, *refs = refs
+        blocks_turned, sums, msg, v_out, u_out, *refs = refs
+        vb, tiles, smooth, wide_h, wide_l, *refs = refs
     row_ids, col_ids, sems, flat, wide, edges, contrib, totals = refs
     get_rows, get_cols = fetch((rows_vmem, cols_vmem), (row_ids, col_ids), sems)
     puts = []
@@ -457,17 +478,16 @@
             rows = []
             for r in range(R):
                 if W <= r < R - W:
-                    total = middle[b, (r - W) * C : (r - W + 1) * C, :]
+                    new = middle[b, (r - W) * C : (r - W + 1) * C, :]
                 else:
-                    total = filter_row(row_taps, b, [(a, filtered(r + a, b)) for a in range(TAPS)])
-                full = u_rows[b, r * C : (r + 1) * C, :].astype(F32) + 0.5 * total
-                size = jnp.sqrt(jnp.sum(full * full, axis=0, keepdims=True))
-                limit = thr[b, r : r + 1, :]
-                new = full * (limit / jnp.maximum(size, limit))
+                    new = shrunk(
+                        u_rows[b, r * C : (r + 1) * C, :],
+                        filter_row(row_taps, b, [(a, filtered(r + a, b)) for a in range(TAPS)]),
+                        thr[b, r : r + 1, :],
+                    ).astype(BF16)
                 if last:
-                    turned[b, r * C : (r + 1) * C, :] = new
+                    turned[b, r * C : (r + 1) * C, :] = new.astype(F32)
                 else:
-                    new = new.astype(BF16)
                     u_out[b, r * C : (r + 1) * C, :] = new
                     rows.append(new.astype(F32))
             if last:
@@ -477,7 +497,7 @@
                 put.start()
                 puts.append(put)
             else:
-                synth_rows(row_taps, b, rows, wide_next)
+                synth_rows(row_taps, b, rows, OUTER, wide_h, wide_l)
 
     wavelets(range(NB))
     get_rows.wait()
@@ -486,7 +506,7 @@
     for put in puts:
         put.wait()
     if not last:
-        make_message(sums, wide_next, col_h, col_l, smooth, msg)
+        make_message(sums, wide_h, wide_l, col_h, col_l, smooth, msg)
 
 
 def shape(dims, dtype=F32):
@@ -501,7 +521,11 @@
     return pltpu.SMEM(dims, dtype)
 
 
-HALF = [shape((NT3, C, VB)), shape((RE * C, NB * L), BF16), shape((R + 1, C, L), BF16)]
+HALF = [shape((NT3, C, VB)), shape((R + 1, C, L), BF16)]
+OUTER_TEMPS = [
+    scratch(2 * W * C, NB * L, dtype=BF16),
+    scratch(2 * W * C, NB * L, dtype=BF16),
+]
 
 
 def call(kernel, far, arrays, outs, temps=(), name=None, mib=8, final=0):
@@ -540,7 +564,7 @@
     facet_in, facet_out = pairs_of("facet")
     grp_in, grp_out = pairs_of("grp")
     scalars = [small((KDEV,), jnp.int32), small((KDEV,), jnp.int32)]
-    sums, wide_rows, msg, u, col_h, col_l, operators, row_taps = call(
+    sums, msg, u, col_h, col_l, operators, row_taps = call(
         first_kernel,
         (taps, row_ids, col_ids, u, v, blocks[0, 0]),
         (),
@@ -562,6 +586,7 @@
             scratch(KDEV, C, VB),
             scratch(NB, C * R, L),
             scratch(W * C, 2 * L),
+            *OUTER_TEMPS,
             pltpu.SemaphoreType.DMA((6,)),
         ],
         name="first",
@@ -574,9 +599,13 @@
         main, ext = call(
             sums_kernel,
             (),
-            (sums, wide_rows, col_h, col_l),
+            (sums, u, row_taps, col_h, col_l),
             [shape((BAND, C, L)), shape((RE, C, L))],
-            [scratch(RE * C, 2 * L)],
+            [
+                scratch(RE * C, 2 * L),
+                scratch(RE * C, NB * L, dtype=BF16),
+                scratch(RE * C, NB * L, dtype=BF16),
+            ],
             name="sums",
         )
         total, total_ext, msg = call(
@@ -627,12 +656,12 @@
         flat, inner, edge, middle = call(
             near_kernel,
             (),
-            (e, e_ext, col_h, col_l, row_taps),
+            (e, e_ext, col_h, col_l, row_taps, u, thresholds),
             [
                 shape((NT3, C, VB), BF16),
                 shape((R * C, NB * L)),
                 shape((W * C, 2 * L), BF16),
-                shape((NB, (R - 2 * W) * C, L)),
+                shape((NB, (R - 2 * W) * C, L), BF16),
             ],
             name="near",
         )
@@ -646,7 +675,12 @@
                 pltpu.SemaphoreType.DMA((NB + 2,)),
             ]
         else:
-            temps = [scratch(RB, C, VB, dtype=BF16), scratch(KDEV, C, VB), scratch(W * C, 2 * L)]
+            temps = [
+                scratch(RB, C, VB, dtype=BF16),
+                scratch(KDEV, C, VB),
+                scratch(W * C, 2 * L),
+                *OUTER_TEMPS,
+            ]
         *half, v, u = call(
             lambda *refs: dual_kernel(last, *refs),
             (),
@@ -671,7 +705,7 @@
         if last:
             (image_out,) = half
         else:
-            sums, wide_rows, msg = half
+            sums, msg = half
     return (image_out.reshape(C, R, L), v[None, None], u.reshape(NB, C, R, L))
 
 

time: 58.8 us -> 58.9 us (level)
  Pallas kernels: 15.2 us -> 16.1 us
    pallas_call x14, Pallas kernels: 15.2 us -> 16.1 us  [call(): pl.pallas_call(kernel, out_shape=tuple(((pltpu.HBM if i < final else pltp...]
    ppermute x4, waiting for transfers between devices: 0.8 us -> 0.01 us  [per_device(): got = lax.ppermute(msg, 'facet', facet_in)]
  transfers between devices with their start and end apart: 10 -> 10, of which waited for: 8 -> 4; matrix products, arithmetic and copies ran while one was open for 0% -> 0% of each run, Pallas kernels for 6% -> 9%
where the time goes in v3:
time: 58.9 us; the launch traced here: 58.7 us
  starting transfers between devices  27.6 us (47%)
  Pallas kernels  16.1 us (27%)
  waiting for transfers between devices  13.9 us (24%)
  between operations  1.06 us (2%)
    pallas_call x14, Pallas kernels, call(): pl.pallas_call(kernel, out_shape=tuple(((pltpu.HBM if i < final else pltp...  16.1 us
    ppermute x4, starting transfers between devices, per_device(): got = lax.ppermute(msg, 'facet', facet_in)  15.6 us
    ppermute x2, waiting for transfers between devices, per_device(): got = lax.ppermute(msg, 'facet', facet_out)  7.8 us
    ppermute x2, waiting for transfers between devices, per_device(): got_b = lax.ppermute(msg_b, 'grp', grp_out)  6.11 us
    ppermute x2, starting transfers between devices, per_device(): got = lax.ppermute(msg, 'facet', facet_out)  5.03 us
    ppermute x2, starting transfers between devices, per_device(): got_b = lax.ppermute(msg_b, 'grp', grp_out)  4.5 us
    ppermute x2, starting transfers between devices, per_device(): got_a = lax.ppermute(msg_a, 'grp', grp_in)  2.5 us
  transfers between devices with their start and end apart: 10, of which 4 were waited for; matrix products, arithmetic and copies ran while one was open for 0% of the time, Pallas kernels for 9%

profile of v3, /device:TPU:131, one launch (start us, length us, event | category | flops | bytes accessed | tf_op | source)
XLA Modules:
  0.0 58.7 jit_solution(4494482601119648470)
XLA Ops:
  0.6 0.0 copy-start.3
  0.6 3.1 %first.1 = (f32[24,16,256]{2,1,0:T(8,128)S(1)}, bf16[17,16,128]{2,1,0:T(8,128)(2,1)S(1)}, bf16[8,256,128]{2,1,0:T(8,128)(2,1)S(1)}, bf16[1024,256]{1,0:T(8,128)(...) custom-call(f32[7,2,8]{2,1,0:T(2,128)} %bitcast.28, ...), custom_call_target="tpu_custom_call" | custom-call | tf_op jit(solution)/shard_map/first/pallas_call | solution.py:535
  3.8 0.8 %collective-permute-start = (bf16[17,16,128]{2,1,0:T(8,128)(2,1)S(1)}, bf16[17,16,128]{2,1,0:T(8,128)(2,1)S(1)}, u32[]{:S(2)}, u32[]{:S(2)}) collective-permute-start(bf16[17,16,128]{2,1,0:T(8,128)(2,1)S(1)} %get-tuple-element.60), channel_id=1, source_target_pairs={{0,1},{1,0},{2,3},{3,2},{4,5},{5,4},{6,7},{7,6},{8,9},{9,8},{10,11... | collective-permute-start | bytes 208904 | tf_op jit(solution)/shard_map/ppermute | solution.py:598
  4.5 1.4 %sums.2 = (f32[48,16,128]{2,1,0:T(8,128)S(1)}, f32[22,16,128]{2,1,0:T(8,128)S(1)}) custom-call(f32[24,16,256]{2,1,0:T(8,128)S(1)} %get-tuple-element.53.sums, bf16[8,256,128]{2,1,0:T(8,128)(2,1)S(1)} %get-tuple-element.54.u_rows.refs_8_, f32[7,8,8,128]{3,2,1,0:T(8,128)S(1)} %get-tuple-element.55.row_taps.refs_12_, ...), custom_call_target="tpu_custom_call" | custom-call | tf_op jit(solution)/shard_map/sums/pallas_call | solution.py:535
  6.0 0.0 collective-permute-done.refs_2_
  6.0 0.0 copy-done.3
  6.0 0.2 pair.2
  6.2 3.1 %collective-permute-start.1 = (bf16[50,16,128]{2,1,0:T(8,128)(2,1)S(1)}, bf16[50,16,128]{2,1,0:T(8,128)(2,1)S(1)}, u32[]{:S(2)}, u32[]{:S(2)}) collective-permute-start(bf16[50,16,128]{2,1,0:T(8,128)(2,1)S(1)} %get-tuple-element.63), channel_id=1, source_target_pairs={{1,2},{2,1},{3,4},{4,3},{5,6},{6,5},{7,8},{8,7},{9,10},{10,9},{11,... | collective-permute-start | bytes 614408 | tf_op jit(solution)/shard_map/ppermute | solution.py:622
  9.3 0.6 %turn.1.refs_6_.refs_16_ = bf16[16,256,256]{2,1,0:T(8,128)(2,1)S(1)} custom-call(bf16[16,256,256]{2,1,0:T(8,128)(2,1)S(1)} %get-tuple-element.64.blocks.refs_7_, f32[16,16,128]{2,1,0:T(8,128)S(1)} %get-tuple-element.61.after.refs_0_), custom_call_target="tpu_custom_call" | custom-call | tf_op jit(solution)/shard_map/turn/pallas_call | solution.py:535
  9.9 0.0 copy-start
  9.9 3.4 %collective-permute-done.1.refs_4_ = bf16[50,16,128]{2,1,0:T(8,128)(2,1)S(1)} collective-permute-done((bf16[50,16,128]{2,1,0:T(8,128)(2,1)S(1)}, bf16[50,16,128]{2,1,0:T(8,128)(2,1)S(1)}, u32[]{:S(2)}, u32[]{:S(2)}) %collective-permute-start.1) | collective-permute-done | bytes 204832 | tf_op jit(solution)/shard_map/ppermute | solution.py:622
  13.2 0.4 rim.2
  13.6 0.0 copy-start.1
  13.6 0.0 copy-start.2
  13.6 0.0 copy-start.4
  13.6 0.0 copy-start.5
  13.7 0.0 copy-start.6
  13.7 0.8 %collective-permute-start.2 = (bf16[4,16,128]{2,1,0:T(8,128)(2,1)S(1)}, bf16[4,16,128]{2,1,0:T(8,128)(2,1)S(1)}, u32[]{:S(2)}, u32[]{:S(2)}) collective-permute-start(bf16[4,16,128]{2,1,0:T(8,128)(2,1)S(1)} %get-tuple-element.67), channel_id=1, source_target_pairs={{0,32},{32,0},{64,96},{96,64},{128,160},{160,128},{192,224},{224,1... | collective-permute-start | bytes 49160 | tf_op jit(solution)/shard_map/ppermute | solution.py:638
  14.5 2.6 %collective-permute-start.3 = (bf16[4,16,128]{2,1,0:T(8,128)(2,1)S(1)}, bf16[4,16,128]{2,1,0:T(8,128)(2,1)S(1)}, u32[]{:S(2)}, u32[]{:S(2)}) collective-permute-start(bf16[4,16,128]{2,1,0:T(8,128)(2,1)S(1)} %get-tuple-element.68), channel_id=1, source_target_pairs={{32,64},{64,32},{96,128},{128,96},{160,192},{192,160},{33,65},{65,... | collective-permute-start | bytes 49160 | tf_op jit(solution)/shard_map/ppermute | solution.py:639
  17.1 0.0 collective-permute-done.2.refs_2_
  17.1 2.8 %collective-permute-done.3.refs_3_ = bf16[4,16,128]{2,1,0:T(8,128)(2,1)S(1)} collective-permute-done((bf16[4,16,128]{2,1,0:T(8,128)(2,1)S(1)}, bf16[4,16,128]{2,1,0:T(8,128)(2,1)S(1)}, u32[]{:S(2)}, u32[]{:S(2)}) %collective-permute-start.3) | collective-permute-done | bytes 16416 | tf_op jit(solution)/shard_map/ppermute | solution.py:639
  19.9 0.3 primal.2
  20.2 7.2 %collective-permute-start.4 = (bf16[17,16,128]{2,1,0:T(8,128)(2,1)S(1)}, bf16[17,16,128]{2,1,0:T(8,128)(2,1)S(1)}, u32[]{:S(2)}, u32[]{:S(2)}) collective-permute-start(bf16[17,16,128]{2,1,0:T(8,128)(2,1)S(1)} %get-tuple-element.76), channel_id=1, source_target_pairs={{0,1},{1,0},{2,3},{3,2},{4,5},{5,4},{6,7},{7,6},{8,9},{9,8},{10,11... | collective-permute-start | bytes 208904 | tf_op jit(solution)/shard_map/ppermute | solution.py:655
  27.4 0.0 copy-done
  27.4 1.0 %near.2 = (bf16[24,16,256]{2,1,0:T(8,128)(2,1)S(1)}, f32[256,1024]{1,0:T(8,128)S(1)}, bf16[48,256]{1,0:T(8,128)(2,1)S(1)}, bf16[8,160,128]{2,1,0:T(8,128)(2,1)S(1)}) custom-call(bf16[32,16,128]{2,1,0:T(8,128)(2,1)S(1)} %get-tuple-element.70.e, bf16[32,16,128]{2,1,0:T(8,128)(2,1)S(1)} %get-tuple-element.71.e_ext, ...), custom_call_target="tpu_custom_call" | custom-call | tf_op jit(solution)/shard_map/near/pallas_call | solution.py:535
  28.4 0.0 collective-permute-done.4.refs_4_
  28.4 0.0 copy-done.1
  28.4 0.0 copy-done.2
  28.4 0.0 copy-done.4
  28.4 0.0 copy-done.5
  28.4 0.0 copy-done.6
  28.4 3.0 %dual.2 = (f32[24,16,256]{2,1,0:T(8,128)S(1)}, bf16[17,16,128]{2,1,0:T(8,128)(2,1)S(1)}, f32[8,16,256]{2,1,0:T(8,128)S(1)}, bf16[8,256,128]{2,1,0:T(8,128)(2,1)S(1)}) custom-call(bf16[24,16,256]{2,1,0:T(8,128)(2,1)S(1)} %get-tuple-element.72.refs_0_, f32[256,1024]{1,0:T(8,128)S(1)} %get-tuple-element.73.refs_1_, ...), custom_call_target="tpu_custom_call" | custom-call | tf_op jit(solution)/shard_map/dual/pallas_call | solution.py:535
  31.4 0.3 collective-permute-start.5
  31.7 1.4 %sums.3 = (f32[48,16,128]{2,1,0:T(8,128)S(1)}, f32[22,16,128]{2,1,0:T(8,128)S(1)}) custom-call(f32[24,16,256]{2,1,0:T(8,128)S(1)} %get-tuple-element.77.sums, bf16[8,256,128]{2,1,0:T(8,128)(2,1)S(1)} %get-tuple-element.78.u_rows.refs_8_, f32[7,8,8,128]{3,2,1,0:T(8,128)S(1)} %get-tuple-element.55.row_taps.refs_12_, ...), custom_call_target="tpu_custom_call" | custom-call | tf_op jit(solution)/shard_map/sums/pallas_call | solution.py:535
  33.1 0.0 collective-permute-done.5.refs_2_
  33.1 0.2 pair.3
  33.3 1.9 %collective-permute-start.6 = (bf16[34,16,128]{2,1,0:T(8,128)(2,1)S(1)}, bf16[34,16,128]{2,1,0:T(8,128)(2,1)S(1)}, u32[]{:S(2)}, u32[]{:S(2)}) collective-permute-start(bf16[34,16,128]{2,1,0:T(8,128)(2,1)S(1)} %get-tuple-element.84), channel_id=1, source_target_pairs={{1,2},{2,1},{3,4},{4,3},{5,6},{6,5},{7,8},{8,7},{9,10},{10,9},{11,... | collective-permute-start | bytes 417800 | tf_op jit(solution)/shard_map/ppermute | solution.py:622
  35.3 4.4 %collective-permute-done.6.refs_4_ = bf16[34,16,128]{2,1,0:T(8,128)(2,1)S(1)} collective-permute-done((bf16[34,16,128]{2,1,0:T(8,128)(2,1)S(1)}, bf16[34,16,128]{2,1,0:T(8,128)(2,1)S(1)}, u32[]{:S(2)}, u32[]{:S(2)}) %collective-permute-start.6) | collective-permute-done | bytes 139296 | tf_op jit(solution)/shard_map/ppermute | solution.py:622
  39.7 0.3 rim.3
  40.0 1.7 %collective-permute-start.7 = (bf16[2,16,128]{2,1,0:T(8,128)(2,1)S(1)}, bf16[2,16,128]{2,1,0:T(8,128)(2,1)S(1)}, u32[]{:S(2)}, u32[]{:S(2)}) collective-permute-start(bf16[2,16,128]{2,1,0:T(8,128)(2,1)S(1)} %get-tuple-element.87), channel_id=1, source_target_pairs={{0,32},{32,0},{64,96},{96,64},{128,160},{160,128},{192,224},{224,1... | collective-permute-start | bytes 24584 | tf_op jit(solution)/shard_map/ppermute | solution.py:638
  41.7 1.9 %collective-permute-start.8 = (bf16[2,16,128]{2,1,0:T(8,128)(2,1)S(1)}, bf16[2,16,128]{2,1,0:T(8,128)(2,1)S(1)}, u32[]{:S(2)}, u32[]{:S(2)}) collective-permute-start(bf16[2,16,128]{2,1,0:T(8,128)(2,1)S(1)} %get-tuple-element.88), channel_id=1, source_target_pairs={{32,64},{64,32},{96,128},{128,96},{160,192},{192,160},{33,65},{65,... | collective-permute-start | bytes 24584 | tf_op jit(solution)/shard_map/ppermute | solution.py:639
  43.6 0.0 collective-permute-done.7.refs_2_
  43.6 3.4 %collective-permute-done.8.refs_3_ = bf16[2,16,128]{2,1,0:T(8,128)(2,1)S(1)} collective-permute-done((bf16[2,16,128]{2,1,0:T(8,128)(2,1)S(1)}, bf16[2,16,128]{2,1,0:T(8,128)(2,1)S(1)}, u32[]{:S(2)}, u32[]{:S(2)}) %collective-permute-start.8) | collective-permute-done | bytes 8224 | tf_op jit(solution)/shard_map/ppermute | solution.py:639
  47.0 0.3 primal.3
  47.3 7.3 %collective-permute-start.9 = (bf16[17,16,128]{2,1,0:T(8,128)(2,1)S(1)}, bf16[17,16,128]{2,1,0:T(8,128)(2,1)S(1)}, u32[]{:S(2)}, u32[]{:S(2)}) collective-permute-start(bf16[17,16,128]{2,1,0:T(8,128)(2,1)S(1)} %get-tuple-element.97), channel_id=1, source_target_pairs={{0,1},{1,0},{2,3},{3,2},{4,5},{5,4},{6,7},{7,6},{8,9},{9,8},{10,11... | collective-permute-start | bytes 208904 | tf_op jit(solution)/shard_map/ppermute | solution.py:655
  54.6 1.0 %near.3 = (bf16[24,16,256]{2,1,0:T(8,128)(2,1)S(1)}, f32[256,1024]{1,0:T(8,128)S(1)}, bf16[48,256]{1,0:T(8,128)(2,1)S(1)}, bf16[8,160,128]{2,1,0:T(8,128)(2,1)S(1)}) custom-call(bf16[32,16,128]{2,1,0:T(8,128)(2,1)S(1)} %get-tuple-element.91.e, bf16[32,16,128]{2,1,0:T(8,128)(2,1)S(1)} %get-tuple-element.92.e_ext, ...), custom_call_target="tpu_custom_call" | custom-call | tf_op jit(solution)/shard_map/near/pallas_call | solution.py:535
  55.7 0.0 collective-permute-done.9.refs_4_
  55.7 2.9 %dual.3 = (f32[256,128]{1,0:T(8,128)}, f32[8,16,256]{2,1,0:T(8,128)}, bf16[8,256,128]{2,1,0:T(8,128)(2,1)}) custom-call(bf16[24,16,256]{2,1,0:T(8,128)(2,1)S(1)} %get-tuple-element.93.refs_0_, f32[256,1024]{1,0:T(8,128)S(1)} %get-tuple-element.94.refs_1_, bf16[48,256]{1,0:T(8,128)(2,1)S(1)} %get-tuple-element.95.refs_2_, ...), custom_call_target="tpu_custom_call" | custom-call | tf_op jit(solution)/shard_map/dual/pallas_call | solution.py:535
Async XLA Ops:
  0.6 5.3 %copy-start.3 = (f32[16,16,128]{2,1,0:T(8,128)S(1)}, f32[16,16,128]{2,1,0:T(8,128)}, u32[]{:S(2)}) copy-start(f32[16,16,128]{2,1,0:T(8,128)} %param.10) | copy-start | bytes 393220
  3.8 2.2 %collective-permute-start = (bf16[17,16,128]{2,1,0:T(8,128)(2,1)S(1)}, bf16[17,16,128]{2,1,0:T(8,128)(2,1)S(1)}, u32[]{:S(2)}, u32[]{:S(2)}) collective-permute-start(bf16[17,16,128]{2,1,0:T(8,128)(2,1)S(1)} %get-tuple-element.60), channel_id=1, source_target_pairs={{0,1},{1,0},{2,3},{3,2},{4,5},{5,4},{6,7},{7,6},{8,9},{9,8},{10,11... | collective-permute-start | bytes 208904 | tf_op jit(solution)/shard_map/ppermute | solution.py:598
  6.2 7.1 %collective-permute-start.1 = (bf16[50,16,128]{2,1,0:T(8,128)(2,1)S(1)}, bf16[50,16,128]{2,1,0:T(8,128)(2,1)S(1)}, u32[]{:S(2)}, u32[]{:S(2)}) collective-permute-start(bf16[50,16,128]{2,1,0:T(8,128)(2,1)S(1)} %get-tuple-element.63), channel_id=1, source_target_pairs={{1,2},{2,1},{3,4},{4,3},{5,6},{6,5},{7,8},{8,7},{9,10},{10,9},{11,... | collective-permute-start | bytes 614408 | tf_op jit(solution)/shard_map/ppermute | solution.py:622
  9.9 17.5 %copy-start = (f32[8,16,128]{2,1,0:T(8,128)S(1)}, f32[8,16,128]{2,1,0:T(8,128)}, u32[]{:S(2)}) copy-start(f32[8,16,128]{2,1,0:T(8,128)} %refs_9_.3) | copy-start | bytes 196612
  13.6 14.8 %copy-start.1 = (f32[1,1,8,16,256]{4,3,2,1,0:T(8,128)S(1)}, f32[1,1,8,16,256]{4,3,2,1,0:T(8,128)}, u32[]{:S(2)}) copy-start(f32[1,1,8,16,256]{4,3,2,1,0:T(8,128)} %param.14) | copy-start | bytes 393220
  13.6 14.8 %copy-start.2 = (f32[1,1,8,16,256]{4,3,2,1,0:T(8,128)S(1)}, f32[1,1,8,16,256]{4,3,2,1,0:T(8,128)}, u32[]{:S(2)}) copy-start(f32[1,1,8,16,256]{4,3,2,1,0:T(8,128)} %param.15) | copy-start | bytes 393220
  13.6 14.8 %copy-start.4 = (s32[1,1,16]{2,1,0:T(1,128)S(1)}, s32[1,1,16]{2,1,0:T(1,128)}, u32[]{:S(2)}) copy-start(s32[1,1,16]{2,1,0:T(1,128)} %param.18) | copy-start | bytes 196
  13.6 14.8 %copy-start.5 = (s32[1,1,16]{2,1,0:T(1,128)S(1)}, s32[1,1,16]{2,1,0:T(1,128)}, u32[]{:S(2)}) copy-start(s32[1,1,16]{2,1,0:T(1,128)} %param.19) | copy-start | bytes 196
  13.7 14.8 %copy-start.6 = (f32[1,1,8]{2,1,0:T(1,128)S(1)}, f32[1,1,8]{2,1,0:T(1,128)}, u32[]{:S(2)}) copy-start(f32[1,1,8]{2,1,0:T(1,128)} %param.16) | copy-start | bytes 100
  13.7 3.4 %collective-permute-start.2 = (bf16[4,16,128]{2,1,0:T(8,128)(2,1)S(1)}, bf16[4,16,128]{2,1,0:T(8,128)(2,1)S(1)}, u32[]{:S(2)}, u32[]{:S(2)}) collective-permute-start(bf16[4,16,128]{2,1,0:T(8,128)(2,1)S(1)} %get-tuple-element.67), channel_id=1, source_target_pairs={{0,32},{32,0},{64,96},{96,64},{128,160},{160,128},{192,224},{224,1... | collective-permute-start | bytes 49160 | tf_op jit(solution)/shard_map/ppermute | solution.py:638
  14.5 5.4 %collective-permute-start.3 = (bf16[4,16,128]{2,1,0:T(8,128)(2,1)S(1)}, bf16[4,16,128]{2,1,0:T(8,128)(2,1)S(1)}, u32[]{:S(2)}, u32[]{:S(2)}) collective-permute-start(bf16[4,16,128]{2,1,0:T(8,128)(2,1)S(1)} %get-tuple-element.68), channel_id=1, source_target_pairs={{32,64},{64,32},{96,128},{128,96},{160,192},{192,160},{33,65},{65,... | collective-permute-start | bytes 49160 | tf_op jit(solution)/shard_map/ppermute | solution.py:639
  20.2 8.2 %collective-permute-start.4 = (bf16[17,16,128]{2,1,0:T(8,128)(2,1)S(1)}, bf16[17,16,128]{2,1,0:T(8,128)(2,1)S(1)}, u32[]{:S(2)}, u32[]{:S(2)}) collective-permute-start(bf16[17,16,128]{2,1,0:T(8,128)(2,1)S(1)} %get-tuple-element.76), channel_id=1, source_target_pairs={{0,1},{1,0},{2,3},{3,2},{4,5},{5,4},{6,7},{7,6},{8,9},{9,8},{10,11... | collective-permute-start | bytes 208904 | tf_op jit(solution)/shard_map/ppermute | solution.py:655
  31.4 1.7 %collective-permute-start.5 = (bf16[17,16,128]{2,1,0:T(8,128)(2,1)S(1)}, bf16[17,16,128]{2,1,0:T(8,128)(2,1)S(1)}, u32[]{:S(2)}, u32[]{:S(2)}) collective-permute-start(bf16[17,16,128]{2,1,0:T(8,128)(2,1)S(1)} %get-tuple-element.81), channel_id=1, source_target_pairs={{0,1},{1,0},{2,3},{3,2},{4,5},{5,4},{6,7},{7,6},{8,9},{9,8},{10,11... | collective-permute-start | bytes 208904 | tf_op jit(solution)/shard_map/ppermute | solution.py:598
  33.3 6.4 %collective-permute-start.6 = (bf16[34,16,128]{2,1,0:T(8,128)(2,1)S(1)}, bf16[34,16,128]{2,1,0:T(8,128)(2,1)S(1)}, u32[]{:S(2)}, u32[]{:S(2)}) collective-permute-start(bf16[34,16,128]{2,1,0:T(8,128)(2,1)S(1)} %get-tuple-element.84), channel_id=1, source_target_pairs={{1,2},{2,1},{3,4},{4,3},{5,6},{6,5},{7,8},{8,7},{9,10},{10,9},{11,... | collective-permute-start | bytes 417800 | tf_op jit(solution)/shard_map/ppermute | solution.py:622
  40.0 3.6 %collective-permute-start.7 = (bf16[2,16,128]{2,1,0:T(8,128)(2,1)S(1)}, bf16[2,16,128]{2,1,0:T(8,128)(2,1)S(1)}, u32[]{:S(2)}, u32[]{:S(2)}) collective-permute-start(bf16[2,16,128]{2,1,0:T(8,128)(2,1)S(1)} %get-tuple-element.87), channel_id=1, source_target_pairs={{0,32},{32,0},{64,96},{96,64},{128,160},{160,128},{192,224},{224,1... | collective-permute-start | bytes 24584 | tf_op jit(solution)/shard_map/ppermute | solution.py:638
  41.7 5.3 %collective-permute-start.8 = (bf16[2,16,128]{2,1,0:T(8,128)(2,1)S(1)}, bf16[2,16,128]{2,1,0:T(8,128)(2,1)S(1)}, u32[]{:S(2)}, u32[]{:S(2)}) collective-permute-start(bf16[2,16,128]{2,1,0:T(8,128)(2,1)S(1)} %get-tuple-element.88), channel_id=1, source_target_pairs={{32,64},{64,32},{96,128},{128,96},{160,192},{192,160},{33,65},{65,... | collective-permute-start | bytes 24584 | tf_op jit(solution)/shard_map/ppermute | solution.py:639
  47.3 8.4 %collective-permute-start.9 = (bf16[17,16,128]{2,1,0:T(8,128)(2,1)S(1)}, bf16[17,16,128]{2,1,0:T(8,128)(2,1)S(1)}, u32[]{:S(2)}, u32[]{:S(2)}) collective-permute-start(bf16[17,16,128]{2,1,0:T(8,128)(2,1)S(1)} %get-tuple-element.97), channel_id=1, source_target_pairs={{0,1},{1,0},{2,3},{3,2},{4,5},{5,4},{6,7},{7,6},{8,9},{9,8},{10,11... | collective-permute-start | bytes 208904 | tf_op jit(solution)/shard_map/ppermute | solution.py:655

commit v4 on v3

--- a/solution.py
+++ b/solution.py
@@ -116,7 +116,9 @@
         total = filter_row(row_taps, b, terms)
         high = total.astype(BF16)
         wide_h[spot * C : (spot + 1) * C, b * L : (b + 1) * L] = high
-        wide_l[spot * C : (spot + 1) * C, b * L : (b + 1) * L] = (total - high.astype(F32)).astype(BF16)
+        if wide_l is not None:
+            low = (total - high.astype(F32)).astype(BF16)
+            wide_l[spot * C : (spot + 1) * C, b * L : (b + 1) * L] = low
 
 
 OUTER = tuple(range(W)) + tuple(range(R + W, RE))
@@ -151,11 +153,13 @@
     msg[R] = pack([smooth[i * C : (i + 1) * C, L:] for i in range(W)]).astype(BF16)
 
 
-def sums_kernel(sums, u_rows, row_taps, col_h, col_l, main, ext, smooth, wide_h, wide_l):
+def sums_kernel(sums, u_rows, row_taps, col_h, col_l, main, ext, smooth, wide):
     for b in range(NB):
         rows = [u_rows[b, r * C : (r + 1) * C, :].astype(F32) for r in range(R)]
-        synth_rows(row_taps, b, rows, range(RE), wide_h, wide_l)
-    smooth[...] = filter_columns(wide_h[...], wide_l[...], col_h, col_l)
+        synth_rows(row_taps, b, rows, range(RE), wide, None)
+    smooth[...] = jnp.dot(wide[...], col_h[...], preferred_element_type=F32) + jnp.dot(
+        wide[...], col_l[...], preferred_element_type=F32
+    )
     for tr in range(3):
         for h in range(2):
             xs = swap_blocks([sums[tr * 8 + t, :, h * L : (h + 1) * L] for t in range(8)])
@@ -603,7 +607,6 @@
             [shape((BAND, C, L)), shape((RE, C, L))],
             [
                 scratch(RE * C, 2 * L),
-                scratch(RE * C, NB * L, dtype=BF16),
                 scratch(RE * C, NB * L, dtype=BF16),
             ],
             name="sums",

time: 58.9 us -> 58 us (0.985)
  Pallas kernels: 16.1 us -> 15.4 us
    pallas_call x14, Pallas kernels: 16.1 us -> 15.4 us  [call(): pl.pallas_call(kernel, out_shape=tuple(((pltpu.HBM if i < final else pltp...]
  transfers between devices with their start and end apart: 10 -> 10, of which waited for: 4 -> 4; matrix products, arithmetic and copies ran while one was open for 0% -> 0% of each run, Pallas kernels for 9% -> 8%
where the time goes in v4:
time: 58 us; the launch traced here: 57.8 us
  starting transfers between devices  27.7 us (48%)
  Pallas kernels  15.4 us (27%)
  waiting for transfers between devices  13.8 us (24%)
  between operations  0.9 us (2%)
    ppermute x4, starting transfers between devices, per_device(): got = lax.ppermute(msg, 'facet', facet_in)  15.5 us
    pallas_call x14, Pallas kernels, call(): pl.pallas_call(kernel, out_shape=tuple(((pltpu.HBM if i < final else pltp...  15.4 us
    ppermute x2, waiting for transfers between devices, per_device(): got = lax.ppermute(msg, 'facet', facet_out)  7.64 us
    ppermute x2, waiting for transfers between devices, per_device(): got_b = lax.ppermute(msg_b, 'grp', grp_out)  6.11 us
    ppermute x2, starting transfers between devices, per_device(): got = lax.ppermute(msg, 'facet', facet_out)  5.19 us
    ppermute x2, starting transfers between devices, per_device(): got_b = lax.ppermute(msg_b, 'grp', grp_out)  4.5 us
    ppermute x2, starting transfers between devices, per_device(): got_a = lax.ppermute(msg_a, 'grp', grp_in)  2.5 us
  transfers between devices with their start and end apart: 10, of which 4 were waited for; matrix products, arithmetic and copies ran while one was open for 0% of the time, Pallas kernels for 8%

profile of v4, /device:TPU:131, one launch (start us, length us, event | category | flops | bytes accessed | tf_op | source)
XLA Modules:
  0.0 57.8 jit_solution(9758124513813038741)
XLA Ops:
  0.6 0.0 copy-start.3
  0.6 3.1 %first.1 = (f32[24,16,256]{2,1,0:T(8,128)S(1)}, bf16[17,16,128]{2,1,0:T(8,128)(2,1)S(1)}, bf16[8,256,128]{2,1,0:T(8,128)(2,1)S(1)}, bf16[1024,256]{1,0:T(8,128)(...) custom-call(f32[7,2,8]{2,1,0:T(2,128)} %bitcast.28, ...), custom_call_target="tpu_custom_call" | custom-call | tf_op jit(solution)/shard_map/first/pallas_call | solution.py:539
  3.8 0.8 %collective-permute-start = (bf16[17,16,128]{2,1,0:T(8,128)(2,1)S(1)}, bf16[17,16,128]{2,1,0:T(8,128)(2,1)S(1)}, u32[]{:S(2)}, u32[]{:S(2)}) collective-permute-start(bf16[17,16,128]{2,1,0:T(8,128)(2,1)S(1)} %get-tuple-element.60), channel_id=1, source_target_pairs={{0,1},{1,0},{2,3},{3,2},{4,5},{5,4},{6,7},{7,6},{8,9},{9,8},{10,11... | collective-permute-start | bytes 208904 | tf_op jit(solution)/shard_map/ppermute | solution.py:602
  4.5 1.1 %sums.2 = (f32[48,16,128]{2,1,0:T(8,128)S(1)}, f32[22,16,128]{2,1,0:T(8,128)S(1)}) custom-call(f32[24,16,256]{2,1,0:T(8,128)S(1)} %get-tuple-element.53.sums, bf16[8,256,128]{2,1,0:T(8,128)(2,1)S(1)} %get-tuple-element.54.u_rows.refs_8_, f32[7,8,8,128]{3,2,1,0:T(8,128)S(1)} %get-tuple-element.55.row_taps.refs_12_, ...), custom_call_target="tpu_custom_call" | custom-call | tf_op jit(solution)/shard_map/sums/pallas_call | solution.py:539
  5.6 0.0 collective-permute-done.refs_2_
  5.6 0.0 copy-done.3
  5.6 0.2 pair.2
  5.8 3.3 %collective-permute-start.1 = (bf16[50,16,128]{2,1,0:T(8,128)(2,1)S(1)}, bf16[50,16,128]{2,1,0:T(8,128)(2,1)S(1)}, u32[]{:S(2)}, u32[]{:S(2)}) collective-permute-start(bf16[50,16,128]{2,1,0:T(8,128)(2,1)S(1)} %get-tuple-element.63), channel_id=1, source_target_pairs={{1,2},{2,1},{3,4},{4,3},{5,6},{6,5},{7,8},{8,7},{9,10},{10,9},{11,... | collective-permute-start | bytes 614408 | tf_op jit(solution)/shard_map/ppermute | solution.py:625
  9.1 0.6 %turn.1.refs_6_.refs_16_ = bf16[16,256,256]{2,1,0:T(8,128)(2,1)S(1)} custom-call(bf16[16,256,256]{2,1,0:T(8,128)(2,1)S(1)} %get-tuple-element.64.blocks.refs_7_, f32[16,16,128]{2,1,0:T(8,128)S(1)} %get-tuple-element.61.after.refs_0_), custom_call_target="tpu_custom_call" | custom-call | tf_op jit(solution)/shard_map/turn/pallas_call | solution.py:539
  9.7 0.0 copy-start
  9.7 3.2 %collective-permute-done.1.refs_4_ = bf16[50,16,128]{2,1,0:T(8,128)(2,1)S(1)} collective-permute-done((bf16[50,16,128]{2,1,0:T(8,128)(2,1)S(1)}, bf16[50,16,128]{2,1,0:T(8,128)(2,1)S(1)}, u32[]{:S(2)}, u32[]{:S(2)}) %collective-permute-start.1) | collective-permute-done | bytes 204832 | tf_op jit(solution)/shard_map/ppermute | solution.py:625
  12.9 0.4 rim.2
  13.3 0.0 copy-start.1
  13.3 0.0 copy-start.2
  13.3 0.0 copy-start.4
  13.3 0.0 copy-start.5
  13.3 0.0 copy-start.6
  13.3 0.8 %collective-permute-start.2 = (bf16[4,16,128]{2,1,0:T(8,128)(2,1)S(1)}, bf16[4,16,128]{2,1,0:T(8,128)(2,1)S(1)}, u32[]{:S(2)}, u32[]{:S(2)}) collective-permute-start(bf16[4,16,128]{2,1,0:T(8,128)(2,1)S(1)} %get-tuple-element.67), channel_id=1, source_target_pairs={{0,32},{32,0},{64,96},{96,64},{128,160},{160,128},{192,224},{224,1... | collective-permute-start | bytes 49160 | tf_op jit(solution)/shard_map/ppermute | solution.py:641
  14.1 2.6 %collective-permute-start.3 = (bf16[4,16,128]{2,1,0:T(8,128)(2,1)S(1)}, bf16[4,16,128]{2,1,0:T(8,128)(2,1)S(1)}, u32[]{:S(2)}, u32[]{:S(2)}) collective-permute-start(bf16[4,16,128]{2,1,0:T(8,128)(2,1)S(1)} %get-tuple-element.68), channel_id=1, source_target_pairs={{32,64},{64,32},{96,128},{128,96},{160,192},{192,160},{33,65},{65,... | collective-permute-start | bytes 49160 | tf_op jit(solution)/shard_map/ppermute | solution.py:642
  16.7 0.0 collective-permute-done.2.refs_2_
  16.8 2.8 %collective-permute-done.3.refs_3_ = bf16[4,16,128]{2,1,0:T(8,128)(2,1)S(1)} collective-permute-done((bf16[4,16,128]{2,1,0:T(8,128)(2,1)S(1)}, bf16[4,16,128]{2,1,0:T(8,128)(2,1)S(1)}, u32[]{:S(2)}, u32[]{:S(2)}) %collective-permute-start.3) | collective-permute-done | bytes 16416 | tf_op jit(solution)/shard_map/ppermute | solution.py:642
  19.5 0.3 primal.2
  19.8 7.3 %collective-permute-start.4 = (bf16[17,16,128]{2,1,0:T(8,128)(2,1)S(1)}, bf16[17,16,128]{2,1,0:T(8,128)(2,1)S(1)}, u32[]{:S(2)}, u32[]{:S(2)}) collective-permute-start(bf16[17,16,128]{2,1,0:T(8,128)(2,1)S(1)} %get-tuple-element.76), channel_id=1, source_target_pairs={{0,1},{1,0},{2,3},{3,2},{4,5},{5,4},{6,7},{7,6},{8,9},{9,8},{10,11... | collective-permute-start | bytes 208904 | tf_op jit(solution)/shard_map/ppermute | solution.py:658
  27.2 0.0 copy-done
  27.2 1.0 %near.2 = (bf16[24,16,256]{2,1,0:T(8,128)(2,1)S(1)}, f32[256,1024]{1,0:T(8,128)S(1)}, bf16[48,256]{1,0:T(8,128)(2,1)S(1)}, bf16[8,160,128]{2,1,0:T(8,128)(2,1)S(1)}) custom-call(bf16[32,16,128]{2,1,0:T(8,128)(2,1)S(1)} %get-tuple-element.70.e, bf16[32,16,128]{2,1,0:T(8,128)(2,1)S(1)} %get-tuple-element.71.e_ext, ...), custom_call_target="tpu_custom_call" | custom-call | tf_op jit(solution)/shard_map/near/pallas_call | solution.py:539
  28.2 0.0 collective-permute-done.4.refs_4_
  28.2 0.0 copy-done.1
  28.2 0.0 copy-done.2
  28.2 0.0 copy-done.4
  28.2 0.0 copy-done.5
  28.2 0.0 copy-done.6
  28.2 3.0 %dual.2 = (f32[24,16,256]{2,1,0:T(8,128)S(1)}, bf16[17,16,128]{2,1,0:T(8,128)(2,1)S(1)}, f32[8,16,256]{2,1,0:T(8,128)S(1)}, bf16[8,256,128]{2,1,0:T(8,128)(2,1)S(1)}) custom-call(bf16[24,16,256]{2,1,0:T(8,128)(2,1)S(1)} %get-tuple-element.72.refs_0_, f32[256,1024]{1,0:T(8,128)S(1)} %get-tuple-element.73.refs_1_, ...), custom_call_target="tpu_custom_call" | custom-call | tf_op jit(solution)/shard_map/dual/pallas_call | solution.py:539
  31.2 0.3 collective-permute-start.5
  31.5 1.1 %sums.3 = (f32[48,16,128]{2,1,0:T(8,128)S(1)}, f32[22,16,128]{2,1,0:T(8,128)S(1)}) custom-call(f32[24,16,256]{2,1,0:T(8,128)S(1)} %get-tuple-element.77.sums, bf16[8,256,128]{2,1,0:T(8,128)(2,1)S(1)} %get-tuple-element.78.u_rows.refs_8_, f32[7,8,8,128]{3,2,1,0:T(8,128)S(1)} %get-tuple-element.55.row_taps.refs_12_, ...), custom_call_target="tpu_custom_call" | custom-call | tf_op jit(solution)/shard_map/sums/pallas_call | solution.py:539
  32.6 0.0 collective-permute-done.5.refs_2_
  32.6 0.2 pair.3
  32.8 1.9 %collective-permute-start.6 = (bf16[34,16,128]{2,1,0:T(8,128)(2,1)S(1)}, bf16[34,16,128]{2,1,0:T(8,128)(2,1)S(1)}, u32[]{:S(2)}, u32[]{:S(2)}) collective-permute-start(bf16[34,16,128]{2,1,0:T(8,128)(2,1)S(1)} %get-tuple-element.84), channel_id=1, source_target_pairs={{1,2},{2,1},{3,4},{4,3},{5,6},{6,5},{7,8},{8,7},{9,10},{10,9},{11,... | collective-permute-start | bytes 417800 | tf_op jit(solution)/shard_map/ppermute | solution.py:625
  34.7 4.4 %collective-permute-done.6.refs_4_ = bf16[34,16,128]{2,1,0:T(8,128)(2,1)S(1)} collective-permute-done((bf16[34,16,128]{2,1,0:T(8,128)(2,1)S(1)}, bf16[34,16,128]{2,1,0:T(8,128)(2,1)S(1)}, u32[]{:S(2)}, u32[]{:S(2)}) %collective-permute-start.6) | collective-permute-done | bytes 139296 | tf_op jit(solution)/shard_map/ppermute | solution.py:625
  39.2 0.3 rim.3
  39.5 1.7 %collective-permute-start.7 = (bf16[2,16,128]{2,1,0:T(8,128)(2,1)S(1)}, bf16[2,16,128]{2,1,0:T(8,128)(2,1)S(1)}, u32[]{:S(2)}, u32[]{:S(2)}) collective-permute-start(bf16[2,16,128]{2,1,0:T(8,128)(2,1)S(1)} %get-tuple-element.87), channel_id=1, source_target_pairs={{0,32},{32,0},{64,96},{96,64},{128,160},{160,128},{192,224},{224,1... | collective-permute-start | bytes 24584 | tf_op jit(solution)/shard_map/ppermute | solution.py:641
  41.1 1.9 %collective-permute-start.8 = (bf16[2,16,128]{2,1,0:T(8,128)(2,1)S(1)}, bf16[2,16,128]{2,1,0:T(8,128)(2,1)S(1)}, u32[]{:S(2)}, u32[]{:S(2)}) collective-permute-start(bf16[2,16,128]{2,1,0:T(8,128)(2,1)S(1)} %get-tuple-element.88), channel_id=1, source_target_pairs={{32,64},{64,32},{96,128},{128,96},{160,192},{192,160},{33,65},{65,... | collective-permute-start | bytes 24584 | tf_op jit(solution)/shard_map/ppermute | solution.py:642
  43.0 0.0 collective-permute-done.7.refs_2_
  43.1 3.4 %collective-permute-done.8.refs_3_ = bf16[2,16,128]{2,1,0:T(8,128)(2,1)S(1)} collective-permute-done((bf16[2,16,128]{2,1,0:T(8,128)(2,1)S(1)}, bf16[2,16,128]{2,1,0:T(8,128)(2,1)S(1)}, u32[]{:S(2)}, u32[]{:S(2)}) %collective-permute-start.8) | collective-permute-done | bytes 8224 | tf_op jit(solution)/shard_map/ppermute | solution.py:642
  46.4 0.3 primal.3
  46.7 7.1 %collective-permute-start.9 = (bf16[17,16,128]{2,1,0:T(8,128)(2,1)S(1)}, bf16[17,16,128]{2,1,0:T(8,128)(2,1)S(1)}, u32[]{:S(2)}, u32[]{:S(2)}) collective-permute-start(bf16[17,16,128]{2,1,0:T(8,128)(2,1)S(1)} %get-tuple-element.97), channel_id=1, source_target_pairs={{0,1},{1,0},{2,3},{3,2},{4,5},{5,4},{6,7},{7,6},{8,9},{9,8},{10,11... | collective-permute-start | bytes 208904 | tf_op jit(solution)/shard_map/ppermute | solution.py:658
  53.9 1.0 %near.3 = (bf16[24,16,256]{2,1,0:T(8,128)(2,1)S(1)}, f32[256,1024]{1,0:T(8,128)S(1)}, bf16[48,256]{1,0:T(8,128)(2,1)S(1)}, bf16[8,160,128]{2,1,0:T(8,128)(2,1)S(1)}) custom-call(bf16[32,16,128]{2,1,0:T(8,128)(2,1)S(1)} %get-tuple-element.91.e, bf16[32,16,128]{2,1,0:T(8,128)(2,1)S(1)} %get-tuple-element.92.e_ext, ...), custom_call_target="tpu_custom_call" | custom-call | tf_op jit(solution)/shard_map/near/pallas_call | solution.py:539
  54.9 0.0 collective-permute-done.9.refs_4_
  54.9 2.9 %dual.3 = (f32[256,128]{1,0:T(8,128)}, f32[8,16,256]{2,1,0:T(8,128)}, bf16[8,256,128]{2,1,0:T(8,128)(2,1)}) custom-call(bf16[24,16,256]{2,1,0:T(8,128)(2,1)S(1)} %get-tuple-element.93.refs_0_, f32[256,1024]{1,0:T(8,128)S(1)} %get-tuple-element.94.refs_1_, bf16[48,256]{1,0:T(8,128)(2,1)S(1)} %get-tuple-element.95.refs_2_, ...), custom_call_target="tpu_custom_call" | custom-call | tf_op jit(solution)/shard_map/dual/pallas_call | solution.py:539
Async XLA Ops:
  0.6 5.0 %copy-start.3 = (f32[16,16,128]{2,1,0:T(8,128)S(1)}, f32[16,16,128]{2,1,0:T(8,128)}, u32[]{:S(2)}) copy-start(f32[16,16,128]{2,1,0:T(8,128)} %param.10) | copy-start | bytes 393220
  3.8 1.8 %collective-permute-start = (bf16[17,16,128]{2,1,0:T(8,128)(2,1)S(1)}, bf16[17,16,128]{2,1,0:T(8,128)(2,1)S(1)}, u32[]{:S(2)}, u32[]{:S(2)}) collective-permute-start(bf16[17,16,128]{2,1,0:T(8,128)(2,1)S(1)} %get-tuple-element.60), channel_id=1, source_target_pairs={{0,1},{1,0},{2,3},{3,2},{4,5},{5,4},{6,7},{7,6},{8,9},{9,8},{10,11... | collective-permute-start | bytes 208904 | tf_op jit(solution)/shard_map/ppermute | solution.py:602
  5.8 7.1 %collective-permute-start.1 = (bf16[50,16,128]{2,1,0:T(8,128)(2,1)S(1)}, bf16[50,16,128]{2,1,0:T(8,128)(2,1)S(1)}, u32[]{:S(2)}, u32[]{:S(2)}) collective-permute-start(bf16[50,16,128]{2,1,0:T(8,128)(2,1)S(1)} %get-tuple-element.63), channel_id=1, source_target_pairs={{1,2},{2,1},{3,4},{4,3},{5,6},{6,5},{7,8},{8,7},{9,10},{10,9},{11,... | collective-permute-start | bytes 614408 | tf_op jit(solution)/shard_map/ppermute | solution.py:625
  9.7 17.5 %copy-start = (f32[8,16,128]{2,1,0:T(8,128)S(1)}, f32[8,16,128]{2,1,0:T(8,128)}, u32[]{:S(2)}) copy-start(f32[8,16,128]{2,1,0:T(8,128)} %refs_9_.3) | copy-start | bytes 196612
  13.3 14.9 %copy-start.1 = (f32[1,1,8,16,256]{4,3,2,1,0:T(8,128)S(1)}, f32[1,1,8,16,256]{4,3,2,1,0:T(8,128)}, u32[]{:S(2)}) copy-start(f32[1,1,8,16,256]{4,3,2,1,0:T(8,128)} %param.14) | copy-start | bytes 393220
  13.3 14.9 %copy-start.2 = (f32[1,1,8,16,256]{4,3,2,1,0:T(8,128)S(1)}, f32[1,1,8,16,256]{4,3,2,1,0:T(8,128)}, u32[]{:S(2)}) copy-start(f32[1,1,8,16,256]{4,3,2,1,0:T(8,128)} %param.15) | copy-start | bytes 393220
  13.3 14.9 %copy-start.4 = (s32[1,1,16]{2,1,0:T(1,128)S(1)}, s32[1,1,16]{2,1,0:T(1,128)}, u32[]{:S(2)}) copy-start(s32[1,1,16]{2,1,0:T(1,128)} %param.18) | copy-start | bytes 196
  13.3 14.9 %copy-start.5 = (s32[1,1,16]{2,1,0:T(1,128)S(1)}, s32[1,1,16]{2,1,0:T(1,128)}, u32[]{:S(2)}) copy-start(s32[1,1,16]{2,1,0:T(1,128)} %param.19) | copy-start | bytes 196
  13.3 14.9 %copy-start.6 = (f32[1,1,8]{2,1,0:T(1,128)S(1)}, f32[1,1,8]{2,1,0:T(1,128)}, u32[]{:S(2)}) copy-start(f32[1,1,8]{2,1,0:T(1,128)} %param.16) | copy-start | bytes 100
  13.3 3.4 %collective-permute-start.2 = (bf16[4,16,128]{2,1,0:T(8,128)(2,1)S(1)}, bf16[4,16,128]{2,1,0:T(8,128)(2,1)S(1)}, u32[]{:S(2)}, u32[]{:S(2)}) collective-permute-start(bf16[4,16,128]{2,1,0:T(8,128)(2,1)S(1)} %get-tuple-element.67), channel_id=1, source_target_pairs={{0,32},{32,0},{64,96},{96,64},{128,160},{160,128},{192,224},{224,1... | collective-permute-start | bytes 49160 | tf_op jit(solution)/shard_map/ppermute | solution.py:641
  14.1 5.4 %collective-permute-start.3 = (bf16[4,16,128]{2,1,0:T(8,128)(2,1)S(1)}, bf16[4,16,128]{2,1,0:T(8,128)(2,1)S(1)}, u32[]{:S(2)}, u32[]{:S(2)}) collective-permute-start(bf16[4,16,128]{2,1,0:T(8,128)(2,1)S(1)} %get-tuple-element.68), channel_id=1, source_target_pairs={{32,64},{64,32},{96,128},{128,96},{160,192},{192,160},{33,65},{65,... | collective-permute-start | bytes 49160 | tf_op jit(solution)/shard_map/ppermute | solution.py:642
  19.8 8.3 %collective-permute-start.4 = (bf16[17,16,128]{2,1,0:T(8,128)(2,1)S(1)}, bf16[17,16,128]{2,1,0:T(8,128)(2,1)S(1)}, u32[]{:S(2)}, u32[]{:S(2)}) collective-permute-start(bf16[17,16,128]{2,1,0:T(8,128)(2,1)S(1)} %get-tuple-element.76), channel_id=1, source_target_pairs={{0,1},{1,0},{2,3},{3,2},{4,5},{5,4},{6,7},{7,6},{8,9},{9,8},{10,11... | collective-permute-start | bytes 208904 | tf_op jit(solution)/shard_map/ppermute | solution.py:658
  31.2 1.4 %collective-permute-start.5 = (bf16[17,16,128]{2,1,0:T(8,128)(2,1)S(1)}, bf16[17,16,128]{2,1,0:T(8,128)(2,1)S(1)}, u32[]{:S(2)}, u32[]{:S(2)}) collective-permute-start(bf16[17,16,128]{2,1,0:T(8,128)(2,1)S(1)} %get-tuple-element.81), channel_id=1, source_target_pairs={{0,1},{1,0},{2,3},{3,2},{4,5},{5,4},{6,7},{7,6},{8,9},{9,8},{10,11... | collective-permute-start | bytes 208904 | tf_op jit(solution)/shard_map/ppermute | solution.py:602
  32.8 6.4 %collective-permute-start.6 = (bf16[34,16,128]{2,1,0:T(8,128)(2,1)S(1)}, bf16[34,16,128]{2,1,0:T(8,128)(2,1)S(1)}, u32[]{:S(2)}, u32[]{:S(2)}) collective-permute-start(bf16[34,16,128]{2,1,0:T(8,128)(2,1)S(1)} %get-tuple-element.84), channel_id=1, source_target_pairs={{1,2},{2,1},{3,4},{4,3},{5,6},{6,5},{7,8},{8,7},{9,10},{10,9},{11,... | collective-permute-start | bytes 417800 | tf_op jit(solution)/shard_map/ppermute | solution.py:625
  39.5 3.6 %collective-permute-start.7 = (bf16[2,16,128]{2,1,0:T(8,128)(2,1)S(1)}, bf16[2,16,128]{2,1,0:T(8,128)(2,1)S(1)}, u32[]{:S(2)}, u32[]{:S(2)}) collective-permute-start(bf16[2,16,128]{2,1,0:T(8,128)(2,1)S(1)} %get-tuple-element.87), channel_id=1, source_target_pairs={{0,32},{32,0},{64,96},{96,64},{128,160},{160,128},{192,224},{224,1... | collective-permute-start | bytes 24584 | tf_op jit(solution)/shard_map/ppermute | solution.py:641
  41.1 5.3 %collective-permute-start.8 = (bf16[2,16,128]{2,1,0:T(8,128)(2,1)S(1)}, bf16[2,16,128]{2,1,0:T(8,128)(2,1)S(1)}, u32[]{:S(2)}, u32[]{:S(2)}) collective-permute-start(bf16[2,16,128]{2,1,0:T(8,128)(2,1)S(1)} %get-tuple-element.88), channel_id=1, source_target_pairs={{32,64},{64,32},{96,128},{128,96},{160,192},{192,160},{33,65},{65,... | collective-permute-start | bytes 24584 | tf_op jit(solution)/shard_map/ppermute | solution.py:642
  46.7 8.2 %collective-permute-start.9 = (bf16[17,16,128]{2,1,0:T(8,128)(2,1)S(1)}, bf16[17,16,128]{2,1,0:T(8,128)(2,1)S(1)}, u32[]{:S(2)}, u32[]{:S(2)}) collective-permute-start(bf16[17,16,128]{2,1,0:T(8,128)(2,1)S(1)} %get-tuple-element.97), channel_id=1, source_target_pairs={{0,1},{1,0},{2,3},{3,2},{4,5},{5,4},{6,7},{7,6},{8,9},{9,8},{10,11... | collective-permute-start | bytes 208904 | tf_op jit(solution)/shard_map/ppermute | solution.py:658
